TPU v7x, 32 devices: a whole 2x2x4 slice. The times are simulated.
32 devices in a mesh: inner: 4 (over x, core), outer: 8 (over z, y).
Axes of the slice: x: 2, y: 2, z: 4, core: 2. Of those that a mesh axis runs over, the one named last changes fastest.
Arguments:
- queries: bfloat16 [8192, 512], P(('inner', 'outer')), may hold values from -12 to 12
- keys: bfloat16 [8192, 128], P(('inner', 'outer')), may hold values from -12 to 12
- values: bfloat16 [8192, 128], P(('inner', 'outer')), may hold values from -6 to 6
- out_grad: bfloat16 [8192, 512], P(('inner', 'outer')), may hold values from -6 to 6
- block_place: int32 [64], replicated, may hold values from 0 to 63, each once
Outputs:
- query_grad: bfloat16 [8192, 512], P(('inner', 'outer'))
- key_grad: bfloat16 [8192, 128], P(('inner', 'outer'))
- value_grad: bfloat16 [8192, 128], P(('inner', 'outer'))
Inputs may be any that keep to these rules, and one draw needn't show every extreme that they name: `block_place`: every block place appears exactly once.
All inputs are finite; a program needn't handle non-finite values.
Results may differ from a plain program's by a relative error of at most 0.017.
Values may be sent and summed in bfloat16 or wider, within the bound.
No kernel may reach another device: no remote copies, remote signals or barrier semaphores. Data moves between devices by JAX's collectives and lax.ppermute only.
A program may use at most 128 MiB of HBM per device.

v0:
```python
import math

import jax
import jax.numpy as jnp
from jax import lax
from jax.sharding import PartitionSpec as P

STEPS = 4


def as_sent(array):

    def short(part):
        return part.astype(jnp.bfloat16) if part.dtype == jnp.float32 else part

    return jax.tree.map(short, array)


def from_behind(block, axis, distance):
    devices = range(lax.axis_size(axis))
    route = [((i - distance) % len(devices), i) for i in devices]
    return lax.ppermute(block, axis, route)


def per_device(queries, keys, values, out_grad, block_place):
    row_count = keys.shape[0]
    head_size = keys.shape[1]
    head_count = queries.shape[1] // head_size
    inner_size = lax.axis_size("inner")
    outer_size = lax.axis_size("outer")
    block_len = row_count // 2
    group_rows = inner_size * row_count
    score_scale = 1.0 / math.sqrt(head_size)
    inner_index = lax.axis_index("inner")
    outer_index = lax.axis_index("outer")
    places = block_place.reshape(inner_size, outer_size, 2)
    offsets = jnp.arange(block_len, dtype=jnp.int32)
    own_blocks = lax.dynamic_index_in_dim(
        lax.dynamic_index_in_dim(places, inner_index, 0, False), outer_index, 0, False
    )
    query_place = (own_blocks[:, None] * block_len + offsets[None, :]).reshape(row_count)
    query_rows = queries.reshape(row_count, head_count, head_size)
    grad_rows = out_grad.reshape(row_count, head_count, head_size)
    group_keys, group_values = (
        lax.all_gather(keys, "inner", axis=0, tiled=True),
        lax.all_gather(values, "inner", axis=0, tiled=True),
    )
    bundles = [(group_keys, group_values)]
    for step in range(1, STEPS):
        bundles.append(from_behind(as_sent(bundles[-1]), "outer", 1))
    masks = []
    score_list = []
    run_max = jnp.full((row_count, head_count), -1e30, jnp.float32)
    for step in range(STEPS):
        key_rows = bundles[step][0]
        scores = (
            jnp.einsum("thd,kd->thk", query_rows, key_rows, preferred_element_type=jnp.float32)
            * score_scale
        )
        source = (outer_index - step) % outer_size
        bundle_blocks = lax.dynamic_index_in_dim(places, source, 1, False)
        allowed = (bundle_blocks[:, :, None] * block_len + offsets).reshape(group_rows)[
            None, None, :
        ] <= query_place[:, None, None]
        scores = jnp.where(allowed, scores, -1e30)
        run_max = jnp.maximum(run_max, jnp.max(scores, axis=-1))
        masks.append(allowed)
        score_list.append(scores)
    run_sum = jnp.zeros((row_count, head_count), jnp.float32)
    for step in range(STEPS):
        run_sum = run_sum + jnp.sum(
            jnp.where(masks[step], jnp.exp(score_list[step] - run_max[..., None]), 0.0), axis=-1
        )
    log_total = run_max + jnp.log(run_sum)
    prob_list = []
    grad_prob_list = []
    row_dot = jnp.zeros((row_count, head_count), jnp.float32)
    for step in range(STEPS):
        value_rows = bundles[step][1]
        probs = jnp.where(masks[step], jnp.exp(score_list[step] - log_total[..., None]), 0.0)
        probs_low = probs.astype(jnp.bfloat16)
        grad_probs = jnp.einsum(
            "thd,kd->thk", grad_rows, value_rows, preferred_element_type=jnp.float32
        )
        row_dot = row_dot + jnp.sum(probs_low.astype(jnp.float32) * grad_probs, axis=-1)
        prob_list.append(probs)
        grad_prob_list.append(grad_probs)
    query_acc = jnp.zeros((row_count, head_count, head_size), jnp.float32)
    key_sum = jnp.zeros((group_rows, head_size), jnp.float32)
    value_sum = jnp.zeros((group_rows, head_size), jnp.float32)
    for step in reversed(range(STEPS)):
        bundle_key_rows = bundles[step][0]
        bundle_probs = prob_list[step]
        bundle_probs_low = bundle_probs.astype(jnp.bfloat16)
        grad_scores = (bundle_probs * (grad_prob_list[step] - row_dot[..., None])).astype(
            jnp.bfloat16
        )
        query_part = jnp.einsum(
            "thk,kd->thd", grad_scores, bundle_key_rows, preferred_element_type=jnp.float32
        )
        key_part = (
            jnp.einsum("thk,thd->kd", grad_scores, query_rows, preferred_element_type=jnp.float32)
            * score_scale
        )
        value_part = jnp.einsum(
            "thk,thd->kd", bundle_probs_low, grad_rows, preferred_element_type=jnp.float32
        )
        query_part, key_part, value_part = (query_part, key_part, value_part)
        query_acc = query_acc + query_part
        key_sum = key_sum + key_part
        value_sum = value_sum + value_part
        if step > 0:
            key_sum, value_sum = from_behind((key_sum, value_sum), "outer", -1)
    key_total, value_total = (
        lax.psum_scatter(key_sum, "inner", scatter_dimension=0, tiled=True),
        lax.psum_scatter(value_sum, "inner", scatter_dimension=0, tiled=True),
    )
    query_grad = (
        (query_acc * score_scale).reshape(row_count, head_count * head_size).astype(jnp.bfloat16)
    )
    return (query_grad, key_total.astype(jnp.bfloat16), value_total.astype(jnp.bfloat16))


def solution(mesh):
    placed = (
        P(("inner", "outer"), None),
        P(("inner", "outer"), None),
        P(("inner", "outer"), None),
        P(("inner", "outer"), None),
        P(),
    )
    return jax.shard_map(
        per_device,
        mesh=mesh,
        in_specs=placed,
        out_specs=(
            P(("inner", "outer"), None),
            P(("inner", "outer"), None),
            P(("inner", "outer"), None),
        ),
        check_vma=False,
    )
```

profile of v0, /device:TPU:0, one launch (start us, length us, event | category | flops | bytes accessed | tf_op | source)
XLA Modules:
  0.0 202.8 jit_solution(17395007558814114574)
XLA Ops:
  7.2 7.6 %all_gather.7 = bf16[1024,128]{1,0:T(8,128)(2,1)S(1)} all-gather(bf16[256,128]{1,0:T(8,128)(2,1)} %param.7), channel_id=1, replica_groups=mesh['inner'=4,'outer'=8] {'inner'}, dimensions={0}, use_global_device_ids=true | all-gather | bytes 327680 | tf_op jit(solution)/shard_map/all_gather | solution.py:46
  14.8 1.6 collective-permute-start.3
  16.4 6.0 %all_gather.6 = bf16[1024,128]{1,0:T(8,128)(2,1)S(1)} all-gather(bf16[256,128]{1,0:T(8,128)(2,1)} %param.6), channel_id=1, replica_groups=mesh['inner'=4,'outer'=8] {'inner'}, dimensions={0}, use_global_device_ids=true | all-gather | bytes 327680 | tf_op jit(solution)/shard_map/all_gather | solution.py:45
  22.3 1.5 collective-permute-start
  23.8 0.7 reshape.297
  26.5 1.0 fusion.5
  27.5 3.0 %fusion.26 = f32[256,4,1024]{2,0,1:T(8,128)} fusion(bf16[1024,128]{1,0:T(8,128)(2,1)S(1)} %all_gather.7, bf16[256,512]{1,0:T(8,128)(2,1)S(1)} %copy-done.12), kind=kOutput, calls=%fused_computation.59 | convolution fusion | flops 268435456 | bytes 4718592 | tf_op jit(solution)/shard_map/thd,kd->thk/dot_general | solution.py:82
  30.5 1.5 collective-permute-start.4
  32.1 1.5 collective-permute-done
  33.6 1.0 fusion.6
  34.6 7.8 %collective-permute-done.4 = bf16[1024,128]{1,0:T(8,128)(2,1)S(1)} collective-permute-done((bf16[1024,128]{1,0:T(8,128)(2,1)S(1)}, bf16[1024,128]{1,0:T(8,128)(2,1)S(1)}, u32[]{:S(2)}, u32[]{:S(2)}) %collective-permute-start.4) | collective-permute-done | bytes 262176 | tf_op jit(solution)/shard_map/ppermute | solution.py:22
  42.4 5.6 %collective-permute-done.1 = bf16[1024,128]{1,0:T(8,128)(2,1)S(1)} collective-permute-done((bf16[1024,128]{1,0:T(8,128)(2,1)S(1)}, bf16[1024,128]{1,0:T(8,128)(2,1)S(1)}, u32[]{:S(2)}, u32[]{:S(2)}) %collective-permute-start.1) | collective-permute-done | bytes 262176 | tf_op jit(solution)/shard_map/ppermute | solution.py:22
  48.0 1.0 fusion.7
  49.1 3.1 %fusion.22 = f32[256,4,1024]{2,0,1:T(8,128)} fusion(bf16[1024,128]{1,0:T(8,128)(2,1)S(1)} %collective-permute-done.4, bf16[256,512]{1,0:T(8,128)(2,1)S(1)} %copy-done.12), kind=kOutput, calls=%fused_computation.55 | convolution fusion | flops 268435456 | bytes 4718592 | tf_op jit(solution)/shard_map/thd,kd->thk/dot_general | solution.py:82
  52.2 6.2 %collective-permute-done.2 = bf16[1024,128]{1,0:T(8,128)(2,1)S(1)} collective-permute-done((bf16[1024,128]{1,0:T(8,128)(2,1)S(1)}, bf16[1024,128]{1,0:T(8,128)(2,1)S(1)}, u32[]{:S(2)}, u32[]{:S(2)}) %collective-permute-start.2) | collective-permute-done | bytes 262176 | tf_op jit(solution)/shard_map/ppermute | solution.py:22
  58.4 1.0 fusion.4
  59.4 5.0 %select_reduce_fusion.2 = (f32[256,4]{0,1:T(4,128)S(1)}, f32[256,4]{0,1:T(4,128)S(1)}, f32[256,4]{0,1:T(4,128)S(1)}, f32[256,4]{0,1:T(4,128)S(1)}) fusion(f32[256,4,1024]{2,0,1:T(8,128)S(1)} %get-tuple-element.37, f32[256,4]{0,1:T(4,128)S(1)} %maximum_maximum_fusion, pred[256,1024]{1,0:T(8,128)(4,1)S(1)} %get-tuple-element.29, ...), kind=kLoop, calls=%fused_computation.14 | loop fusion | flops 20967424 | bytes 17846272 | tf_op jit(solution)/shard_map/reduce_sum | solution.py:71
  64.4 2.7 %fusion.28 = f32[256,4,1024]{2,0,1:T(8,128)} fusion(bf16[1024,128]{1,0:T(8,128)(2,1)S(1)} %collective-permute-done.5, bf16[256,512]{1,0:T(8,128)(2,1)S(1)} %copy-done.12), kind=kOutput, calls=%fused_computation.61 | convolution fusion | flops 268435456 | bytes 4718592 | tf_op jit(solution)/shard_map/thd,kd->thk/dot_general | solution.py:82
  67.1 10.8 %multiply_reduce_fusion.2 = (f32[256,4]{0,1:T(4,128)S(1)}, f32[256,4]{0,1:T(4,128)S(1)}, f32[256,4]{0,1:T(4,128)S(1)}, f32[256,4]{0,1:T(4,128)S(1)}, f32[256,4,1024]{2,0,1:T(8,128)}) fusion(f32[256,4]{0,1:T(4,128)S(1)} %log_add_fusion, f32[256,4,1024]{2,0,1:T(8,128)S(1)} %get-tuple-element.37, pred[256,1024]{1,0:T(8,128)(4,1)S(1)} %get-tuple-element.29, ...), kind=kOutput, calls=%fused_computation.7 | convolution fusion | flops 301985792 | bytes 35147776 | tf_op jit(solution)/shard_map/thd,kd->thk/dot_general | solution.py:82
  77.9 14.9 %multiply_convert_fusion.3 = (bf16[256,4,1024]{2,0,1:T(8,128)(2,1)S(1)}, bf16[256,4,1024]{2,0,1:T(8,128)(2,1)}, bf16[256,4,1024]{2,0,1:T(8,128)(2,1)}, bf16[256,4,1024]{2,0,1:T(8,128)(2,1)}) fusion(f32[256,4,1024]{2,0,1:T(8,128)} %fusion.28, f32[256,4,1024]{2,0,1:T(8,128)} %copy-done.6, f32[256,4]{0,1:T(4,128)S(1)} %add_add_fusion, ...), kind=kLoop, calls=%fused_computation.3 | loop fusion | flops 29360128 | bytes 42999808 | tf_op jit(solution)/shard_map/convert_element_type | solution.py:95
  94.0 11.9 %collective-permute-done.6 = f32[1024,128]{1,0:T(8,128)S(1)} collective-permute-done((f32[1024,128]{1,0:T(8,128)S(1)}, f32[1024,128]{1,0:T(8,128)S(1)}, u32[]{:S(2)}, u32[]{:S(2)}) %collective-permute-start.6) | collective-permute-done | bytes 524320 | tf_op jit(solution)/shard_map/ppermute | solution.py:22
  105.9 0.7 fusion.11
  106.7 4.1 %collective-permute-start.7 = (f32[1024,128]{1,0:T(8,128)S(1)}, f32[1024,128]{1,0:T(8,128)S(1)}, u32[]{:S(2)}, u32[]{:S(2)}) collective-permute-start(f32[1024,128]{1,0:T(8,128)S(1)} %fusion.11), channel_id=1, source_target_pairs={{1,0},{2,1},{3,2},{4,3},{5,4},{6,5},{7,6},{0,7},{9,8},{10,9},{11,1... | collective-permute-start | bytes 1572872 | tf_op jit(solution)/shard_map/ppermute | solution.py:22
  110.8 1.4 convolution_bitcast_fusion.3
  112.3 0.7 fusion.9
  113.1 10.0 %collective-permute-done.7 = f32[1024,128]{1,0:T(8,128)S(1)} collective-permute-done((f32[1024,128]{1,0:T(8,128)S(1)}, f32[1024,128]{1,0:T(8,128)S(1)}, u32[]{:S(2)}, u32[]{:S(2)}) %collective-permute-start.7) | collective-permute-done | bytes 524320 | tf_op jit(solution)/shard_map/ppermute | solution.py:22
  123.2 5.2 %collective-permute-start.8 = (f32[1024,128]{1,0:T(8,128)S(1)}, f32[1024,128]{1,0:T(8,128)S(1)}, u32[]{:S(2)}, u32[]{:S(2)}) collective-permute-start(f32[1024,128]{1,0:T(8,128)S(1)} %add.261), channel_id=1, source_target_pairs={{1,0},{2,1},{3,2},{4,3},{5,4},{6,5},{7,6},{0,7},{9,8},{10,9},{11,1... | collective-permute-start | bytes 1572872 | tf_op jit(solution)/shard_map/ppermute | solution.py:22
  128.4 5.9 %collective-permute-done.9 = f32[1024,128]{1,0:T(8,128)S(1)} collective-permute-done((f32[1024,128]{1,0:T(8,128)S(1)}, f32[1024,128]{1,0:T(8,128)S(1)}, u32[]{:S(2)}, u32[]{:S(2)}) %collective-permute-start.9) | collective-permute-done | bytes 524320 | tf_op jit(solution)/shard_map/ppermute | solution.py:22
  134.4 2.4 %fusion.16 = f32[1024,128]{1,0:T(8,128)} fusion(f32[1024,128]{1,0:T(8,128)S(1)} %collective-permute-done.9, f32[256,4,1024]{2,0,1:T(8,128)S(1)} %copy-done.5, f32[256,4]{0,1:T(4,128)S(1)} %log_add_fusion, pred[256,1024]{1,0:T(8,128)(4,1)S(1)} %get-tuple-element.30, bf16[256,512]{1,0:T(8,128)(2,1)S(1)} %copy-done.12), kind=kOutput, calls=%fused_computation.45 | convolution fusion | flops 273809408 | bytes 5771264 | tf_op jit(solution)/shard_map/thk,thd->kd/dot_general | solution.py:105
  136.7 5.2 %collective-permute-start.10 = (f32[1024,128]{1,0:T(8,128)}, f32[1024,128]{1,0:T(8,128)}, u32[]{:S(2)}, u32[]{:S(2)}) collective-permute-start(f32[1024,128]{1,0:T(8,128)} %fusion.16), channel_id=1, source_target_pairs={{1,0},{2,1},{3,2},{4,3},{5,4},{6,5},{7,6},{0,7},{9,8},{10,9},{11,1... | collective-permute-start | bytes 1572872 | tf_op jit(solution)/shard_map/ppermute | solution.py:22
  141.9 0.7 fusion.8
  142.7 2.9 %collective-permute-done.8 = f32[1024,128]{1,0:T(8,128)S(1)} collective-permute-done((f32[1024,128]{1,0:T(8,128)S(1)}, f32[1024,128]{1,0:T(8,128)S(1)}, u32[]{:S(2)}, u32[]{:S(2)}) %collective-permute-start.8) | collective-permute-done | bytes 524320 | tf_op jit(solution)/shard_map/ppermute | solution.py:22
  145.6 0.9 add.262
  146.6 3.7 %convolution_bitcast_fusion.1 = f32[1024,128]{1,0:T(8,128)S(1)} fusion(f32[256,4,1024]{2,0,1:T(8,128)} %copy-done.3, f32[256,4]{0,1:T(4,128)S(1)} %log_add_fusion, pred[256,1024]{1,0:T(8,128)(4,1)S(1)} %get-tuple-element.29, bf16[256,512]{1,0:T(8,128)(2,1)S(1)} %copy-done.12), kind=kOutput, calls=%fused_computation.29 | convolution fusion | flops 273678336 | bytes 5246976 | tf_op jit(solution)/shard_map/thk,thd->kd/dot_general | solution.py:105
  150.3 4.0 %collective-permute-done.10 = f32[1024,128]{1,0:T(8,128)} collective-permute-done((f32[1024,128]{1,0:T(8,128)}, f32[1024,128]{1,0:T(8,128)}, u32[]{:S(2)}, u32[]{:S(2)}) %collective-permute-start.10) | collective-permute-done | bytes 524320 | tf_op jit(solution)/shard_map/ppermute | solution.py:22
  154.3 1.1 add.264
  155.4 5.3 %collective-permute-start.11 = (f32[1024,128]{1,0:T(8,128)S(1)}, f32[1024,128]{1,0:T(8,128)S(1)}, u32[]{:S(2)}, u32[]{:S(2)}) collective-permute-start(f32[1024,128]{1,0:T(8,128)S(1)} %add.264), channel_id=1, source_target_pairs={{1,0},{2,1},{3,2},{4,3},{5,4},{6,5},{7,6},{0,7},{9,8},{10,9},{11,1... | collective-permute-start | bytes 1572872 | tf_op jit(solution)/shard_map/ppermute | solution.py:22
  160.7 1.4 convolution_bitcast_fusion
  162.1 7.4 %collective-permute-done.11 = f32[1024,128]{1,0:T(8,128)S(1)} collective-permute-done((f32[1024,128]{1,0:T(8,128)S(1)}, f32[1024,128]{1,0:T(8,128)S(1)}, u32[]{:S(2)}, u32[]{:S(2)}) %collective-permute-start.11) | collective-permute-done | bytes 524320 | tf_op jit(solution)/shard_map/ppermute | solution.py:22
  169.5 0.8 add.265
  170.4 2.6 %fusion.52 = f32[256,4,128]{0,2,1:T(8,128)S(1)} fusion(bf16[256,4,1024]{2,0,1:T(8,128)(2,1)} %get-tuple-element.27, bf16[1024,128]{1,0:T(8,128)(2,1)S(1)} %all_gather.6), kind=kOutput, calls=%fused_computation.85 | convolution fusion | flops 268435456 | bytes 2883584 | tf_op jit(solution)/shard_map/thk,kd->thd/dot_general | solution.py:98
  172.9 2.4 %fusion.49 = f32[256,4,128]{0,2,1:T(8,128)S(1)} fusion(bf16[256,4,1024]{2,0,1:T(8,128)(2,1)} %get-tuple-element.26, bf16[1024,128]{1,0:T(8,128)(2,1)} %copy-done.15), kind=kOutput, calls=%fused_computation.82 | convolution fusion | flops 268435456 | bytes 2883584 | tf_op jit(solution)/shard_map/thk,kd->thd/dot_general | solution.py:98
  175.4 1.8 fusion.46
  177.2 0.8 fusion.17
  178.0 0.8 copy.118
  178.9 1.5 convert_element_type.66
  180.4 14.0 %reduce-scatter.5.cloned.1.call-done = f32[256,128]{1,0:T(8,128)} async-done(((f32[1024,128]{1,0:T(8,128)}), f32[256,128]{1,0:T(8,128)}) %reduce-scatter.5.cloned.1.call-update) | async-done | bytes 131088 | tf_op jit(solution)/shard_map/reduce_scatter | solution.py:116
  194.4 1.5 convert_element_type.67
  (71 shorter events, 3.5 us)
Async XLA Ops:
  7.2 19.3 %copy-start = (bf16[256,512]{1,0:T(8,128)(2,1)S(1)}, bf16[256,512]{1,0:T(8,128)(2,1)}, u32[]{:S(2)}) copy-start(bf16[256,512]{1,0:T(8,128)(2,1)} %param.5) | copy-start | bytes 786436
  7.2 20.3 %copy-start.12 = (bf16[256,512]{1,0:T(8,128)(2,1)S(1)}, bf16[256,512]{1,0:T(8,128)(2,1)}, u32[]{:S(2)}) copy-start(bf16[256,512]{1,0:T(8,128)(2,1)} %param.8) | copy-start | bytes 786436
  7.2 171.7 %reduce-scatter.3.cloned.1.call-start = ((), (), s32[]{:S(2)}) async-start(), calls=%async_computation.2 | async-start | bytes 655360 | tf_op jit(solution)/shard_map/reduce_scatter | solution.py:115
  14.8 15.7 %collective-permute-start.3 = (bf16[1024,128]{1,0:T(8,128)(2,1)S(1)}, bf16[1024,128]{1,0:T(8,128)(2,1)S(1)}, u32[]{:S(2)}, u32[]{:S(2)}) collective-permute-start(bf16[1024,128]{1,0:T(8,128)(2,1)S(1)} %all_gather.7), channel_id=1, source_target_pairs={{7,0},{0,1},{1,2},{2,3},{3,4},{4,5},{5,6},{6,7},{15,8},{8,9},{9,10... | collective-permute-start | bytes 786440 | tf_op jit(solution)/shard_map/ppermute | solution.py:22
  22.3 11.3 %collective-permute-start = (bf16[1024,128]{1,0:T(8,128)(2,1)S(1)}, bf16[1024,128]{1,0:T(8,128)(2,1)S(1)}, u32[]{:S(2)}, u32[]{:S(2)}) collective-permute-start(bf16[1024,128]{1,0:T(8,128)(2,1)S(1)} %all_gather.6), channel_id=1, source_target_pairs={{7,0},{0,1},{1,2},{2,3},{3,4},{4,5},{5,6},{6,7},{15,8},{8,9},{9,10... | collective-permute-start | bytes 786440 | tf_op jit(solution)/shard_map/ppermute | solution.py:22
  27.5 50.4 %copy-start.1 = (f32[256,4,1024]{2,0,1:T(8,128)}, f32[256,4,1024]{2,0,1:T(8,128)S(1)}, u32[]{:S(2)}) copy-start(f32[256,4,1024]{2,0,1:T(8,128)S(1)} %get-tuple-element.39) | copy-start | bytes 12582916
  30.5 11.9 %collective-permute-start.4 = (bf16[1024,128]{1,0:T(8,128)(2,1)S(1)}, bf16[1024,128]{1,0:T(8,128)(2,1)S(1)}, u32[]{:S(2)}, u32[]{:S(2)}) collective-permute-start(bf16[1024,128]{1,0:T(8,128)(2,1)S(1)} %collective-permute-done.3), channel_id=1, source_target_pairs={{7,0},{0,1},{1,2},{2,3},{3,4},{4,5},{5,6},{6,7},{15,8},{8,9},{9,10... | collective-permute-start | bytes 786440 | tf_op jit(solution)/shard_map/ppermute | solution.py:22
  33.6 15.5 %copy-start.15 = (bf16[1024,128]{1,0:T(8,128)(2,1)}, bf16[1024,128]{1,0:T(8,128)(2,1)S(1)}, u32[]{:S(2)}) copy-start(bf16[1024,128]{1,0:T(8,128)(2,1)S(1)} %collective-permute-done) | copy-start | bytes 786436
  33.6 14.5 %collective-permute-start.1 = (bf16[1024,128]{1,0:T(8,128)(2,1)S(1)}, bf16[1024,128]{1,0:T(8,128)(2,1)S(1)}, u32[]{:S(2)}, u32[]{:S(2)}) collective-permute-start(bf16[1024,128]{1,0:T(8,128)(2,1)S(1)} %collective-permute-done), channel_id=1, source_target_pairs={{7,0},{0,1},{1,2},{2,3},{3,4},{4,5},{5,6},{6,7},{15,8},{8,9},{9,10... | collective-permute-start | bytes 786440 | tf_op jit(solution)/shard_map/ppermute | solution.py:22
  34.6 32.5 %copy-start.3 = (f32[256,4,1024]{2,0,1:T(8,128)}, f32[256,4,1024]{2,0,1:T(8,128)S(1)}, u32[]{:S(2)}) copy-start(f32[256,4,1024]{2,0,1:T(8,128)S(1)} %get-tuple-element.37) | copy-start | bytes 12582916
  42.4 22.0 %collective-permute-start.5 = (bf16[1024,128]{1,0:T(8,128)(2,1)S(1)}, bf16[1024,128]{1,0:T(8,128)(2,1)S(1)}, u32[]{:S(2)}, u32[]{:S(2)}) collective-permute-start(bf16[1024,128]{1,0:T(8,128)(2,1)S(1)} %collective-permute-done.4), channel_id=1, source_target_pairs={{7,0},{0,1},{1,2},{2,3},{3,4},{4,5},{5,6},{6,7},{15,8},{8,9},{9,10... | collective-permute-start | bytes 786440 | tf_op jit(solution)/shard_map/ppermute | solution.py:22
  48.0 4.2 %copy-start.16 = (bf16[1024,128]{1,0:T(8,128)(2,1)}, bf16[1024,128]{1,0:T(8,128)(2,1)S(1)}, u32[]{:S(2)}) copy-start(bf16[1024,128]{1,0:T(8,128)(2,1)S(1)} %collective-permute-done.1) | copy-start | bytes 786436
  48.0 10.3 %collective-permute-start.2 = (bf16[1024,128]{1,0:T(8,128)(2,1)S(1)}, bf16[1024,128]{1,0:T(8,128)(2,1)S(1)}, u32[]{:S(2)}, u32[]{:S(2)}) collective-permute-start(bf16[1024,128]{1,0:T(8,128)(2,1)S(1)} %collective-permute-done.1), channel_id=1, source_target_pairs={{7,0},{0,1},{1,2},{2,3},{3,4},{4,5},{5,6},{6,7},{15,8},{8,9},{9,10... | collective-permute-start | bytes 786440 | tf_op jit(solution)/shard_map/ppermute | solution.py:22
  49.1 18.0 %copy-start.4 = (f32[256,4,1024]{2,0,1:T(8,128)}, f32[256,4,1024]{2,0,1:T(8,128)S(1)}, u32[]{:S(2)}) copy-start(f32[256,4,1024]{2,0,1:T(8,128)S(1)} %get-tuple-element.35) | copy-start | bytes 12582916
  58.4 6.0 %copy-start.13 = (bf16[1024,128]{1,0:T(8,128)(2,1)}, bf16[1024,128]{1,0:T(8,128)(2,1)S(1)}, u32[]{:S(2)}) copy-start(bf16[1024,128]{1,0:T(8,128)(2,1)S(1)} %collective-permute-done.2) | copy-start | bytes 786436
  59.4 5.0 %copy-start.6 = (f32[256,4,1024]{2,0,1:T(8,128)}, f32[256,4,1024]{2,0,1:T(8,128)S(1)}, u32[]{:S(2)}) copy-start(f32[256,4,1024]{2,0,1:T(8,128)S(1)} %get-tuple-element.33) | copy-start | bytes 12582916
  92.7 13.2 %copy-start.10 = (bf16[256,4,1024]{2,0,1:T(8,128)(2,1)S(1)}, bf16[256,4,1024]{2,0,1:T(8,128)(2,1)}, u32[]{:S(2)}) copy-start(bf16[256,4,1024]{2,0,1:T(8,128)(2,1)} %get-tuple-element.25) | copy-start | bytes 6291460
  92.7 18.1 %copy-start.7 = (f32[256,4,1024]{2,0,1:T(8,128)S(1)}, f32[256,4,1024]{2,0,1:T(8,128)}, u32[]{:S(2)}) copy-start(f32[256,4,1024]{2,0,1:T(8,128)} %copy-done.6) | copy-start | bytes 12582916
  93.5 12.4 %collective-permute-start.6 = (f32[1024,128]{1,0:T(8,128)S(1)}, f32[1024,128]{1,0:T(8,128)S(1)}, u32[]{:S(2)}, u32[]{:S(2)}) collective-permute-start(f32[1024,128]{1,0:T(8,128)S(1)} %fusion.12), channel_id=1, source_target_pairs={{1,0},{2,1},{3,2},{4,3},{5,4},{6,5},{7,6},{0,7},{9,8},{10,9},{11,1... | collective-permute-start | bytes 1572872 | tf_op jit(solution)/shard_map/ppermute | solution.py:22
  106.7 5.7 %copy-start.8 = (bf16[256,4,1024]{2,0,1:T(8,128)(2,1)S(1)}, bf16[256,4,1024]{2,0,1:T(8,128)(2,1)}, u32[]{:S(2)}) copy-start(bf16[256,4,1024]{2,0,1:T(8,128)(2,1)} %get-tuple-element.26) | copy-start | bytes 6291460
  106.7 16.4 %collective-permute-start.7 = (f32[1024,128]{1,0:T(8,128)S(1)}, f32[1024,128]{1,0:T(8,128)S(1)}, u32[]{:S(2)}, u32[]{:S(2)}) collective-permute-start(f32[1024,128]{1,0:T(8,128)S(1)} %fusion.11), channel_id=1, source_target_pairs={{1,0},{2,1},{3,2},{4,3},{5,4},{6,5},{7,6},{0,7},{9,8},{10,9},{11,1... | collective-permute-start | bytes 1572872 | tf_op jit(solution)/shard_map/ppermute | solution.py:22
  112.3 22.1 %copy-start.5 = (f32[256,4,1024]{2,0,1:T(8,128)S(1)}, f32[256,4,1024]{2,0,1:T(8,128)}, u32[]{:S(2)}) copy-start(f32[256,4,1024]{2,0,1:T(8,128)} %copy-done.4) | copy-start | bytes 12582916
  112.3 22.1 %collective-permute-start.9 = (f32[1024,128]{1,0:T(8,128)S(1)}, f32[1024,128]{1,0:T(8,128)S(1)}, u32[]{:S(2)}, u32[]{:S(2)}) collective-permute-start(f32[1024,128]{1,0:T(8,128)S(1)} %convolution_bitcast_fusion.3), channel_id=1, source_target_pairs={{1,0},{2,1},{3,2},{4,3},{5,4},{6,5},{7,6},{0,7},{9,8},{10,9},{11,1... | collective-permute-start | bytes 1572872 | tf_op jit(solution)/shard_map/ppermute | solution.py:22
  123.2 18.7 %copy-start.9 = (bf16[256,4,1024]{2,0,1:T(8,128)(2,1)S(1)}, bf16[256,4,1024]{2,0,1:T(8,128)(2,1)}, u32[]{:S(2)}) copy-start(bf16[256,4,1024]{2,0,1:T(8,128)(2,1)} %get-tuple-element.27) | copy-start | bytes 6291460
  123.2 22.4 %collective-permute-start.8 = (f32[1024,128]{1,0:T(8,128)S(1)}, f32[1024,128]{1,0:T(8,128)S(1)}, u32[]{:S(2)}, u32[]{:S(2)}) collective-permute-start(f32[1024,128]{1,0:T(8,128)S(1)} %add.261), channel_id=1, source_target_pairs={{1,0},{2,1},{3,2},{4,3},{5,4},{6,5},{7,6},{0,7},{9,8},{10,9},{11,1... | collective-permute-start | bytes 1572872 | tf_op jit(solution)/shard_map/ppermute | solution.py:22
  136.7 17.6 %collective-permute-start.10 = (f32[1024,128]{1,0:T(8,128)}, f32[1024,128]{1,0:T(8,128)}, u32[]{:S(2)}, u32[]{:S(2)}) collective-permute-start(f32[1024,128]{1,0:T(8,128)} %fusion.16), channel_id=1, source_target_pairs={{1,0},{2,1},{3,2},{4,3},{5,4},{6,5},{7,6},{0,7},{9,8},{10,9},{11,1... | collective-permute-start | bytes 1572872 | tf_op jit(solution)/shard_map/ppermute | solution.py:22
  146.5 47.9 %reduce-scatter.5.cloned.1.call-start = ((), (), s32[]{:S(2)}) async-start(), calls=%async_computation.3 | async-start | bytes 655360 | tf_op jit(solution)/shard_map/reduce_scatter | solution.py:116
  146.6 14.1 %copy-start.2 = (f32[256,4,1024]{2,0,1:T(8,128)S(1)}, f32[256,4,1024]{2,0,1:T(8,128)}, u32[]{:S(2)}) copy-start(f32[256,4,1024]{2,0,1:T(8,128)} %copy-done.1) | copy-start | bytes 12582916
  155.4 14.1 %collective-permute-start.11 = (f32[1024,128]{1,0:T(8,128)S(1)}, f32[1024,128]{1,0:T(8,128)S(1)}, u32[]{:S(2)}, u32[]{:S(2)}) collective-permute-start(f32[1024,128]{1,0:T(8,128)S(1)} %add.264), channel_id=1, source_target_pairs={{1,0},{2,1},{3,2},{4,3},{5,4},{6,5},{7,6},{0,7},{9,8},{10,9},{11,1... | collective-permute-start | bytes 1572872 | tf_op jit(solution)/shard_map/ppermute | solution.py:22
  170.4 5.0 %copy-start.11 = (bf16[256,4,1024]{2,0,1:T(8,128)(2,1)S(1)}, bf16[256,4,1024]{2,0,1:T(8,128)(2,1)}, u32[]{:S(2)}) copy-start(bf16[256,4,1024]{2,0,1:T(8,128)(2,1)} %get-tuple-element.25) | copy-start | bytes 6291460
  170.4 6.8 %copy-start.14 = (bf16[1024,128]{1,0:T(8,128)(2,1)S(1)}, bf16[1024,128]{1,0:T(8,128)(2,1)}, u32[]{:S(2)}) copy-start(bf16[1024,128]{1,0:T(8,128)(2,1)} %copy-done.13) | copy-start | bytes 786436
Sparse Core Ops, SparseCore 0:
  146.6 23.5 reduce-scatter.2
  172.7 21.6 reduce-scatter.4
where the time goes:
time: 203 us
  waiting for transfers between devices  77.3 us (38%)
  matrix products  43.1 us (21%)
  other arithmetic  26.9 us (13%)
  starting transfers between devices  25.1 us (12%)
  between operations  14.3 us (7%)
  blocking collectives  13.5 us (7%)
  local copies, waits for them, and re-layouts  2.43 us (1%)
    ppermute x12, waiting for transfers between devices, from_behind(): return lax.ppermute(block, axis, route)  63.3 us
    ppermute x12, starting transfers between devices, from_behind(): return lax.ppermute(block, axis, route)  25 us
    dot_general x4, matrix products, per_device(): jnp.einsum('thd,kd->thk', grad_rows, value_rows, preferred_element_type=j...  19.6 us
    convert_element_type x1, other arithmetic, per_device(): (bundle_probs * (grad_prob_list[step] - row_dot[..., None])).astype(jnp.b...  14.9 us
    reduce_scatter x1, waiting for transfers between devices, per_device(): lax.psum_scatter(value_sum, 'inner', scatter_dimension=0, tiled=True)  14 us
    dot_general x4, matrix products, per_device(): jnp.einsum('thk,thd->kd', bundle_probs_low, grad_rows, preferred_element_...  8.96 us
    dot_general x4, matrix products, per_device(): jnp.einsum('thk,kd->thd', grad_scores, bundle_key_rows, preferred_element...  7.62 us
    all_gather x1, blocking collectives, per_device(): lax.all_gather(values, 'inner', axis=0, tiled=True)  7.57 us
  transfers between devices with their start and end apart: 14, of which 11 were waited for; matrix products, arithmetic and copies ran while one was open for 20% of the time, Pallas kernels for 0%

commit v1 on v0

v1 whole, which is shorter than its diff:
```python
import functools
import math

import jax
import jax.numpy as jnp
from jax import lax
from jax.experimental import pallas as pl
from jax.experimental.pallas import tpu as pltpu
from jax.sharding import PartitionSpec as P


STEPS = 4
NEG = -1e30
LOG2E = math.log2(math.e)
NT = (((1,), (1,)), ((), ()))


def dot_nt(a, b):
    return lax.dot_general(a, b, NT, preferred_element_type=jnp.float32)


def from_behind(block, axis, distance):
    devices = range(lax.axis_size(axis))
    route = [((i - distance) % len(devices), i) for i in devices]
    return lax.ppermute(block, axis, route)


def swap(block, axis, bit):
    return lax.ppermute(block, axis, [(i, i ^ bit) for i in range(lax.axis_size(axis))])


def fill_bias(bias_ref):
    size = bias_ref.shape[1]
    key_off = lax.broadcasted_iota(jnp.int32, (size, size), 0)
    query_off = lax.broadcasted_iota(jnp.int32, (size, size), 1)
    bias_ref[0] = jnp.zeros((size, size), jnp.float32)
    bias_ref[1] = jnp.where(key_off <= query_off, 0.0, NEG).astype(jnp.float32)
    bias_ref[2] = jnp.full((size, size), NEG, jnp.float32)


def build_list(sizes, queries, blocks, place_ref, where_ref, list_ref):
    outer_size, key_blocks = sizes
    outer = where_ref[4]
    key_place = {}
    for block in blocks:
        step, core, half = block // 4, (block // 2) % 2, block % 2
        source = lax.rem(outer - step + outer_size, outer_size)
        key_place[block] = place_ref[(where_ref[core] * outer_size + source) * 2 + half]
    position = jnp.int32(0)
    for query in queries:
        query_place = place_ref[(where_ref[query // 2] * outer_size + outer) * 2 + query % 2]
        for block in blocks:
            kind = jnp.where(key_place[block] == query_place, 1, 0)
            list_ref[position] = (query * key_blocks + block) * 4 + kind
            position = position + jnp.where(key_place[block] <= query_place, 1, 0)
        list_ref[position] = (query * key_blocks + blocks[0]) * 4 + 2
        position = position + lax.rem(position, 2)
    for extra in range(4):
        list_ref[position + extra] = (queries[0] * key_blocks + blocks[0]) * 4 + 2
    return (position + 2) // 4


def entry_of(list_ref, index, key_blocks):
    e0, e1 = list_ref[2 * index], list_ref[2 * index + 1]
    at0, at1 = e0 // 4, e1 // 4
    return at0 // key_blocks, at0 % key_blocks, e0 % 4, at1 % key_blocks, e1 % 4


def score_tiles(entry, factor, qg, kv, bias, t_ref, dp_ref):
    query, j0, b0, j1, b1 = entry
    k2 = jnp.concatenate([kv[2 * j0], kv[2 * j1]], axis=0)
    v2 = jnp.concatenate([kv[2 * j0 + 1], kv[2 * j1 + 1]], axis=0)
    low, high = bias[b0], bias[b1]
    b2 = jnp.concatenate(
        [jnp.concatenate([low, low], axis=1), jnp.concatenate([high, high], axis=1)], axis=0
    )
    t_ref[...] = dot_nt(k2, qg[2 * query]) * factor + b2
    dp_ref[...] = dot_nt(v2, qg[2 * query + 1])


def stack_refs(refs, dst):
    for i, src in enumerate(refs):
        count = src.shape[0]
        dst[pl.ds(i * count, count)] = src[...]


def pair_loop(trips, load, use):
    load(0, 0)

    @pl.loop(0, trips)
    def _(i):
        load(2 * i + 1, 1)
        use(2 * i, 0)
        load(2 * i + 2, 0)
        use(2 * i + 1, 1)


def pack_kernel(where_ref, q_ref, g_ref, k_ref, v_ref, mine, theirs, kv):
    size = k_ref.shape[1]
    half_len = k_ref.shape[0] // 2
    pairs = q_ref.shape[1] // size // 2
    near = lax.rem(where_ref[0], 2)

    def put(dst, first):
        for half in range(2):
            for which, src in enumerate((q_ref, g_ref)):
                for head in range(pairs):
                    row = ((half * 2 + which) * pairs + head) * half_len
                    dst[pl.ds(row, half_len), :] = src[
                        pl.ds(half * half_len, half_len), pl.ds((first + head) * size, size)
                    ]

    for core in range(2):

        @pl.when(near == core)
        def _():
            put(mine, core * pairs)
            put(theirs, (1 - core) * pairs)

    for half in range(2):
        for which, src in enumerate((k_ref, v_ref)):
            kv[pl.ds((half * 2 + which) * half_len, half_len), :] = src[
                pl.ds(half * half_len, half_len), :
            ]


def stats_kernel(sizes, factor, which, shards, place_ref, where_ref, *rest):
    outer_size, key_blocks, _, width = sizes
    q_refs, kv_refs = rest[: len(which)], rest[len(which) : len(which) + shards]
    out_ref, qg, kv, bias, t0, d0, t1, d1, state, lists = rest[len(which) + shards :]
    stack_refs(kv_refs, kv)
    stack_refs(q_refs, qg)
    here = [2 * t + half for t in which for half in range(2)]
    first = here[0]
    trips = build_list(
        (outer_size, key_blocks), here, range(key_blocks), place_ref, where_ref, lists
    )
    fill_bias(bias)
    count = len(here)
    state[0] = jnp.full((count, 8, width), NEG, jnp.float32)
    state[1] = jnp.zeros((count, 8, width), jnp.float32)
    state[2] = jnp.zeros((count, 8, width), jnp.float32)
    slots = ((t0, d0), (t1, d1))

    def entry(n):
        query, j0, b0, j1, b1 = entry_of(lists, n, key_blocks)
        return query - first, j0, b0, j1, b1

    def load(n, slot):
        score_tiles(entry(n), factor, qg, kv, bias, *slots[slot])

    def use(n, slot):
        query = entry(n)[0]
        t_ref, d_ref = slots[slot]
        m, l, r = state[0, query], state[1, query], state[2, query]
        top = jnp.max(t_ref[...].reshape(-1, 8, width), axis=0)
        m_new = jnp.maximum(m, jnp.max(top, axis=0, keepdims=True))
        corr = jnp.exp2(m - m_new)
        p = jnp.exp2(t_ref[...].reshape(-1, 8, width) - m_new)
        state[0, query] = m_new
        state[1, query] = l * corr + jnp.sum(p, axis=0)
        state[2, query] = r * corr + jnp.sum(p * d_ref[...].reshape(-1, 8, width), axis=0)

    pair_loop(trips, load, use)
    for i in range(count):
        out_ref[i, 0:1] = state[0, i, 0:1]
        out_ref[i, 1:2] = jnp.sum(state[1, i], axis=0, keepdims=True)
        out_ref[i, 2:3] = jnp.sum(state[2, i], axis=0, keepdims=True)
        out_ref[i, 3:8] = jnp.zeros((5, width), jnp.float32)


def grads_kernel(sizes, scale, steps, last, place_ref, where_ref, *rest):
    outer_size, key_blocks, size, width = sizes
    pairs = width // size
    stat_refs = rest[:4] if not last else ()
    carry_in = rest[:2] if last else ()
    rest = rest[2:] if last else rest[4:]
    q_refs, kv_refs = rest[:4], rest[4 : 4 + 2 * len(steps)]
    rest = rest[4 + 2 * len(steps) :]
    outs, rest = rest[: 2 * len(steps)], rest[2 * len(steps) :]
    tops, rest = rest[: (4 if last else 2)], rest[(4 if last else 2) :]
    qg, kv, kt, dk, dv, dq, base, bias, t0, d0, t1, d1, lists = rest
    low = 4 * min(steps)
    blocks = [4 * step + i for step in sorted(steps) for i in range(4)]
    stack_refs(kv_refs, kv)
    stack_refs(q_refs, qg)
    if last:
        dq[...] = carry_in[0][...]
        base[...] = carry_in[1][...]
    trips = build_list((outer_size, key_blocks), range(8), blocks, place_ref, where_ref, lists)
    fill_bias(bias)
    if not last:
        for query in range(8):
            a = stat_refs[query // 4][query % 4]
            b = stat_refs[2 + (1 - query // 4)][query % 4]
            m = jnp.maximum(a[0:1], b[0:1])
            ea, eb = jnp.exp2(a[0:1] - m), jnp.exp2(b[0:1] - m)
            total = a[1:2] * ea + b[1:2] * eb
            base[query, 0:1] = m + jnp.log2(total)
            base[query, 1:2] = (a[2:3] * ea + b[2:3] * eb) / total
            base[query, 2:8] = jnp.zeros((6, width), jnp.float32)
        dq[...] = jnp.zeros_like(dq)
    dk[...] = jnp.zeros_like(dk)
    dv[...] = jnp.zeros_like(dv)
    for block in range(len(blocks)):
        kt[block] = kv[2 * block].T
    factor = scale * LOG2E
    slots = ((t0, d0), (t1, d1))

    def entry(n):
        query, j0, b0, j1, b1 = entry_of(lists, n, key_blocks)
        return query, j0 - low, b0, j1 - low, b1

    def load(n, slot):
        score_tiles(entry(n), factor, qg, kv, bias, *slots[slot])

    def use(n, slot):
        query, j0, _, j1, _ = entry(n)
        t_ref, d_ref = slots[slot]
        p = jnp.exp2(t_ref[...] - base[query, 0:1])
        ds = (p * (d_ref[...] - base[query, 1:2])).astype(jnp.bfloat16)
        p = p.astype(jnp.bfloat16)
        dv_part = jnp.dot(p, qg[2 * query + 1], preferred_element_type=jnp.float32)
        dk_part = jnp.dot(ds, qg[2 * query], preferred_element_type=jnp.float32)
        kt2 = jnp.concatenate([kt[j0], kt[j1]], axis=1)
        dq[query] += jnp.dot(kt2, ds, preferred_element_type=jnp.float32)
        dk[j0] += dk_part[:size]
        dv[j0] += dv_part[:size]
        dk[j1] += dk_part[size:]
        dv[j1] += dv_part[size:]

    pair_loop(trips, load, use)
    for i in range(len(steps)):
        for half in range(2):
            for core in range(2):
                dst = outs[2 * i + core]
                block = i * 4 + core * 2 + half
                dst[pl.ds(2 * half * size, size), :] = (dk[block] * scale).astype(dst.dtype)
                dst[pl.ds((2 * half + 1) * size, size), :] = dv[block].astype(dst.dtype)
    if last:
        for query in range(8):
            dst = tops[query // 2]
            for head in range(pairs):
                dst[pl.ds((query % 2) * size, size), pl.ds(head * size, size)] = (
                    dq[query, :, pl.ds(head * size, size)].T * scale
                ).astype(dst.dtype)
    else:
        tops[0][...] = dq[...]
        tops[1][...] = base[...]


def attention_grads(queries, keys, values, out_grad, block_place):
    row_count, size = keys.shape
    block_len = row_count // 2
    pairs = queries.shape[1] // size // 2
    width = pairs * block_len
    outer_size = lax.axis_size("outer")
    key_blocks = STEPS * 4
    scale = 1.0 / math.sqrt(size)
    inner = lax.axis_index("inner")
    outer = lax.axis_index("outer")
    where = jnp.stack([inner, inner ^ 1, inner ^ 2, inner ^ 3, outer]).astype(jnp.int32)
    smem = pl.BlockSpec(memory_space=pltpu.SMEM)
    vmem = pl.BlockSpec(memory_space=pltpu.VMEM)
    params = pltpu.CompilerParams(vmem_limit_bytes=16 << 20)
    low, full = jnp.bfloat16, jnp.float32

    q_shape, kv_shape = (4 * width, size), (4 * block_len, size)
    mine, theirs, kv = pl.pallas_call(
        pack_kernel,
        name="pack",
        out_shape=[
            jax.ShapeDtypeStruct(q_shape, low),
            jax.ShapeDtypeStruct(q_shape, low),
            jax.ShapeDtypeStruct(kv_shape, low),
        ],
        in_specs=[smem] + [vmem] * 4,
        out_specs=[vmem] * 3,
        compiler_params=params,
    )(where, queries, out_grad, keys, values)
    asked = [mine, swap(theirs, "inner", 1), swap(mine, "inner", 2), swap(theirs, "inner", 3)]
    own = [kv] + [from_behind(kv, "outer", step) for step in range(1, STEPS)]
    near = [swap(block, "inner", 1) for block in own]
    q_parts = [part.reshape(4, width, size) for part in asked]
    shards = [block.reshape(4, block_len, size) for two in zip(own, near) for block in two]

    sizes = (outer_size, key_blocks, size, width)
    flops = 2 * 2 * width * 8 * key_blocks * block_len * size
    tile = pltpu.VMEM((2 * block_len, width), full)
    bias_table = pltpu.VMEM((3, block_len, block_len), full)

    def stats_call(which):
        count = 2 * len(which)
        return pl.pallas_call(
            functools.partial(stats_kernel, sizes, scale * LOG2E, which, len(shards)),
            name="stats",
            out_shape=jax.ShapeDtypeStruct((count, 8, width), full),
            in_specs=[smem, smem] + [vmem] * (len(which) + len(shards)),
            out_specs=vmem,
            scratch_shapes=[
                pltpu.VMEM((2 * count, width, size), low),
                pltpu.VMEM((2 * key_blocks, block_len, size), low),
                bias_table,
                tile,
                tile,
                tile,
                tile,
                pltpu.VMEM((3, count, 8, width), full),
                pltpu.SMEM((count * (key_blocks + 1) + 8,), jnp.int32),
            ],
            compiler_params=params,
            cost_estimate=pl.CostEstimate(
                flops=flops // 2, bytes_accessed=1 << 20, transcendentals=0
            ),
        )(block_place, where, *[q_parts[t] for t in which], *shards)

    stats = []
    for which in ((0, 1), (2, 3)):
        stats.append(stats_call(which))
    others = [swap(stat, "inner", 2) for stat in stats]
    shard_f32 = jax.ShapeDtypeStruct(kv_shape, full)
    shard_low = jax.ShapeDtypeStruct(kv_shape, low)

    def grads_call(steps, last, *extra):
        n = len(steps)
        if last:
            tops = [jax.ShapeDtypeStruct((row_count, width), full if t == 0 else low) for t in range(4)]
        else:
            tops = [
                jax.ShapeDtypeStruct((8, size, width), full),
                jax.ShapeDtypeStruct((8, 8, width), full),
            ]
        used = [part for step in steps for part in shards[2 * step : 2 * step + 2]]
        return pl.pallas_call(
            functools.partial(grads_kernel, sizes, scale, steps, last),
            name="grads",
            out_shape=[shard_f32, shard_low] * n + tops,
            in_specs=[smem, smem] + [vmem] * (len(extra) + 4 + 2 * n),
            out_specs=[vmem] * (2 * n + len(tops)),
            scratch_shapes=[
                pltpu.VMEM((16, width, size), low),
                pltpu.VMEM((8 * n, block_len, size), low),
                pltpu.VMEM((4 * n, size, block_len), low),
                pltpu.VMEM((4 * n, block_len, size), full),
                pltpu.VMEM((4 * n, block_len, size), full),
                pltpu.VMEM((8, size, width), full),
                pltpu.VMEM((8, 8, width), full),
                bias_table,
                tile,
                tile,
                tile,
                tile,
                pltpu.SMEM((8 * (4 * n + 1) + 8,), jnp.int32),
            ],
            compiler_params=params,
            cost_estimate=pl.CostEstimate(
                flops=flops * 3 * n // STEPS, bytes_accessed=1 << 21, transcendentals=0
            ),
        )(block_place, where, *extra, *q_parts, *used)

    far_steps = tuple(range(STEPS // 2, STEPS))
    near_steps = tuple(range(STEPS // 2))
    parts = {}
    got = grads_call(far_steps, False, *stats, *others)
    for i, step in enumerate(far_steps):
        parts[step] = got[2 * i : 2 * i + 2]
    got = grads_call(near_steps, True, *got[2 * len(far_steps) :])
    for i, step in enumerate(near_steps):
        parts[step] = got[2 * i : 2 * i + 2]
    tops = got[2 * len(near_steps) :]
    back = []
    for step in reversed(range(STEPS)):
        whole = parts[step][0] + swap(parts[step][1], "inner", 1).astype(full)
        if step > 0:
            whole = from_behind(whole.astype(low), "outer", -step)
        back.append(whole.astype(full))
    heads_mine = tops[0] + swap(tops[2], "inner", 2).astype(full)
    heads_other = swap(tops[1], "inner", 1).astype(full) + swap(tops[3], "inner", 3).astype(full)
    first = inner % 2 == 0
    dq = jnp.concatenate(
        [jnp.where(first, heads_mine, heads_other), jnp.where(first, heads_other, heads_mine)], axis=1
    )
    total = sum(back[1:], back[0]).astype(low).reshape(2, 2, block_len, size)
    return (
        dq.astype(low),
        total[:, 0].reshape(row_count, size),
        total[:, 1].reshape(row_count, size),
    )


def solution(mesh):
    placed = (
        P(("inner", "outer"), None),
        P(("inner", "outer"), None),
        P(("inner", "outer"), None),
        P(("inner", "outer"), None),
        P(),
    )
    return jax.shard_map(
        attention_grads,
        mesh=mesh,
        in_specs=placed,
        out_specs=(
            P(("inner", "outer"), None),
            P(("inner", "outer"), None),
            P(("inner", "outer"), None),
        ),
        check_vma=False,
    )
```

time: 203 us -> 73.8 us (0.36)
  waiting for transfers between devices: 77.3 us -> 22.4 us
  matrix products: 43.1 us -> 0 us
  other arithmetic: 26.9 us -> 1.01 us
  Pallas kernels: 0 us -> 17.6 us
  between operations: 14.3 us -> 0.74 us
  blocking collectives: 13.5 us -> 0 us
  local copies, waits for them, and re-layouts: 2.43 us -> 4.98 us
    ppermute x12 -> x6, waiting for transfers between devices: 63.3 us -> 13.1 us  [from_behind(): return lax.ppermute(block, axis, route)]
    dot_general x20 -> x0, matrix products: 43.1 us -> none  [the longest x4 19.6 us: per_device(): jnp.einsum('thd,kd->thk', grad_rows, value_rows, preferred_element_type=j...]
    convert_element_type x3 -> x4, other arithmetic: 17.9 us -> 0.2 us  [the longest x3 0.11 us: attention_grads(): whole = from_behind(whole.astype(low), 'outer', -step)]
    pallas_call x0 -> x5, Pallas kernels: none -> 17.6 us  [the longest x2 9.89 us: grads_call(): pl.pallas_call(functools.partial(grads_kernel, sizes, scale, steps, last)...]
    reduce_scatter x2 -> x0, waiting for transfers between devices: 14 us -> none  [the longest x1 14 us: per_device(): lax.psum_scatter(value_sum, 'inner', scatter_dimension=0, tiled=True)]
    all_gather x2 -> x0, blocking collectives: 13.5 us -> none  [the longest x1 7.57 us: per_device(): lax.all_gather(values, 'inner', axis=0, tiled=True)]
    ppermute x0 -> x16, starting transfers between devices: none -> 10.1 us  [swap(): lax.ppermute(block, axis, [(i, i ^ bit) for i in range(lax.axis_size(axis...]
    ppermute x0 -> x16, waiting for transfers between devices: none -> 9.23 us  [swap(): lax.ppermute(block, axis, [(i, i ^ bit) for i in range(lax.axis_size(axis...]
  transfers between devices with their start and end apart: 14 -> 22, of which waited for: 11 -> 9; matrix products, arithmetic and copies ran while one was open for 20% -> 1% of each run, Pallas kernels for 0% -> 17%
where the time goes in v1:
time: 73.8 us; the launch traced here: 73.5 us
  starting transfers between devices  26.9 us (36%)
  waiting for transfers between devices  22.4 us (30%)
  Pallas kernels  17.6 us (24%)
  local copies, waits for them, and re-layouts  4.98 us (7%)
  other arithmetic  1.01 us (1%)
  between operations  0.74 us (1%)
    ppermute x6, starting transfers between devices, from_behind(): return lax.ppermute(block, axis, route)  16.8 us
    ppermute x6, waiting for transfers between devices, from_behind(): return lax.ppermute(block, axis, route)  13.1 us
    ppermute x16, starting transfers between devices, swap(): lax.ppermute(block, axis, [(i, i ^ bit) for i in range(lax.axis_size(axis...  10.1 us
    pallas_call x2, Pallas kernels, grads_call(): pl.pallas_call(functools.partial(grads_kernel, sizes, scale, steps, last)...  9.89 us
    ppermute x16, waiting for transfers between devices, swap(): lax.ppermute(block, axis, [(i, i ^ bit) for i in range(lax.axis_size(axis...  9.23 us
    pallas_call x2, Pallas kernels, stats_call(): pl.pallas_call(functools.partial(stats_kernel, sizes, scale * LOG2E, whic...  7.04 us
    unnamed x10, local copies, waits for them, and re-layouts  4.23 us
  transfers between devices with their start and end apart: 22, of which 9 were waited for; matrix products, arithmetic and copies ran while one was open for 1% of the time, Pallas kernels for 17%

profile of v1, /device:TPU:0, one launch (start us, length us, event | category | flops | bytes accessed | tf_op | source)
XLA Modules:
  0.0 73.5 jit_solution(8742079576239426244)
XLA Ops:
  0.6 0.1 stack.23.where_ref
  0.7 0.9 %copy-done = bf16[256,512]{1,0:T(8,128)(2,1)S(1)} copy-done((bf16[256,512]{1,0:T(8,128)(2,1)S(1)}, bf16[256,512]{1,0:T(8,128)(2,1)}, u32[]{:S(2)}) %copy-start) | copy-done | bytes 262168
  1.7 0.9 %copy-done.1 = bf16[256,512]{1,0:T(8,128)(2,1)S(1)} copy-done((bf16[256,512]{1,0:T(8,128)(2,1)S(1)}, bf16[256,512]{1,0:T(8,128)(2,1)}, u32[]{:S(2)}) %copy-start.1) | copy-done | bytes 262168
  2.6 0.8 %copy-done.2 = bf16[256,128]{1,0:T(8,128)(2,1)S(1)} copy-done((bf16[256,128]{1,0:T(8,128)(2,1)S(1)}, bf16[256,128]{1,0:T(8,128)(2,1)}, u32[]{:S(2)}) %copy-start.2) | copy-done | bytes 65560
  3.5 0.8 %copy-done.3 = bf16[256,128]{1,0:T(8,128)(2,1)S(1)} copy-done((bf16[256,128]{1,0:T(8,128)(2,1)S(1)}, bf16[256,128]{1,0:T(8,128)(2,1)}, u32[]{:S(2)}) %copy-start.3) | copy-done | bytes 65560
  4.3 0.6 pack.1
  5.0 3.0 %collective-permute-start.2 = (bf16[512,128]{1,0:T(8,128)(2,1)S(1)}, bf16[512,128]{1,0:T(8,128)(2,1)S(1)}, u32[]{:S(2)}, u32[]{:S(2)}) collective-permute-start(bf16[512,128]{1,0:T(8,128)(2,1)S(1)} %get-tuple-element.22), channel_id=1, source_target_pairs={{7,0},{0,1},{1,2},{2,3},{3,4},{4,5},{5,6},{6,7},{15,8},{8,9},{9,10... | collective-permute-start | bytes 393224 | tf_op jit(solution)/shard_map/ppermute | solution.py:25
  8.0 1.6 %collective-permute-start.4 = (bf16[512,128]{1,0:T(8,128)(2,1)S(1)}, bf16[512,128]{1,0:T(8,128)(2,1)S(1)}, u32[]{:S(2)}, u32[]{:S(2)}) collective-permute-start(bf16[512,128]{1,0:T(8,128)(2,1)S(1)} %get-tuple-element.22), channel_id=1, source_target_pairs={{6,0},{7,1},{0,2},{1,3},{2,4},{3,5},{4,6},{5,7},{14,8},{15,9},{8,1... | collective-permute-start | bytes 393224 | tf_op jit(solution)/shard_map/ppermute | solution.py:25
  9.6 2.5 %collective-permute-start.6 = (bf16[512,128]{1,0:T(8,128)(2,1)S(1)}, bf16[512,128]{1,0:T(8,128)(2,1)S(1)}, u32[]{:S(2)}, u32[]{:S(2)}) collective-permute-start(bf16[512,128]{1,0:T(8,128)(2,1)S(1)} %get-tuple-element.22), channel_id=1, source_target_pairs={{5,0},{6,1},{7,2},{0,3},{1,4},{2,5},{3,6},{4,7},{13,8},{14,9},{15,... | collective-permute-start | bytes 393224 | tf_op jit(solution)/shard_map/ppermute | solution.py:25
  12.1 3.4 %collective-permute-done.2 = bf16[512,128]{1,0:T(8,128)(2,1)S(1)} collective-permute-done((bf16[512,128]{1,0:T(8,128)(2,1)S(1)}, bf16[512,128]{1,0:T(8,128)(2,1)S(1)}, u32[]{:S(2)}, u32[]{:S(2)}) %collective-permute-start.2) | collective-permute-done | bytes 131104 | tf_op jit(solution)/shard_map/ppermute | solution.py:25
  15.5 1.7 %collective-permute-start.8 = (bf16[1024,128]{1,0:T(8,128)(2,1)S(1)}, bf16[1024,128]{1,0:T(8,128)(2,1)S(1)}, u32[]{:S(2)}, u32[]{:S(2)}) collective-permute-start(bf16[1024,128]{1,0:T(8,128)(2,1)S(1)} %get-tuple-element.20), channel_id=1, source_target_pairs={{0,16},{8,24},{16,0},{24,8},{1,17},{9,25},{17,1},{25,9},{2,18},{10... | collective-permute-start | bytes 786440 | tf_op jit(solution)/shard_map/ppermute | solution.py:29
  17.1 0.0 collective-permute-done.4
  17.1 0.2 collective-permute-start.9
  17.4 5.6 %collective-permute-done.6 = bf16[512,128]{1,0:T(8,128)(2,1)S(1)} collective-permute-done((bf16[512,128]{1,0:T(8,128)(2,1)S(1)}, bf16[512,128]{1,0:T(8,128)(2,1)S(1)}, u32[]{:S(2)}, u32[]{:S(2)}) %collective-permute-start.6) | collective-permute-done | bytes 131104 | tf_op jit(solution)/shard_map/ppermute | solution.py:25
  23.0 0.0 collective-permute-start
  23.0 0.0 collective-permute-done.1
  23.0 0.5 collective-permute-start.5
  23.5 0.0 collective-permute-done.3
  23.5 0.1 collective-permute-start.7
  23.6 1.1 %collective-permute-done.5 = bf16[512,128]{1,0:T(8,128)(2,1)S(1)} collective-permute-done((bf16[512,128]{1,0:T(8,128)(2,1)S(1)}, bf16[512,128]{1,0:T(8,128)(2,1)S(1)}, u32[]{:S(2)}, u32[]{:S(2)}) %collective-permute-start.5) | collective-permute-done | bytes 131104 | tf_op jit(solution)/shard_map/ppermute | solution.py:29
  24.7 0.2 collective-permute-done.7
  24.9 4.5 %collective-permute-done.9 = bf16[1024,128]{1,0:T(8,128)(2,1)S(1)} collective-permute-done((bf16[1024,128]{1,0:T(8,128)(2,1)S(1)}, bf16[1024,128]{1,0:T(8,128)(2,1)S(1)}, u32[]{:S(2)}, u32[]{:S(2)}) %collective-permute-start.9) | collective-permute-done | bytes 262176 | tf_op jit(solution)/shard_map/ppermute | solution.py:29
  29.4 0.7 copy-done.4
  30.0 3.7 %stats.3.rest_1_ = f32[4,8,256]{2,1,0:T(8,128)S(1)} custom-call(s32[64]{0:T(128)S(1)} %copy-done.4, s32[5]{0:T(128)S(1)} %stack.23.where_ref, bf16[4,256,128]{2,1,0:T(8,128)(2,1)S(1)} %bitcast.23, bf16[4,256,128]{2,1,0:T(8,128)(2,1)S(1)} %bitcast.26, bf16[4,128,128]{2,1,0:T(8,128)(2,1)S(1)} %bitcast.32, bf16[4,128,128]{2,1,0:T(8,128)(2,1)S(1)} %bitcast.38, ...), custom_call_target="tpu_custom_call" | custom-call | flops 1073741824 | bytes 1048576 | tf_op jit(solution)/shard_map/stats/pallas_call | solution.py:294
  33.7 1.4 %collective-permute-start.11 = (f32[4,8,256]{2,1,0:T(8,128)S(1)}, f32[4,8,256]{2,1,0:T(8,128)S(1)}, u32[]{:S(2)}, u32[]{:S(2)}) collective-permute-start(f32[4,8,256]{2,1,0:T(8,128)S(1)} %stats.3.rest_1_), channel_id=1, source_target_pairs={{0,16},{8,24},{16,0},{24,8},{1,17},{9,25},{17,1},{25,9},{2,18},{10... | collective-permute-start | bytes 98312 | tf_op jit(solution)/shard_map/ppermute | solution.py:29
  35.1 3.4 %stats.2.rest_0_ = f32[4,8,256]{2,1,0:T(8,128)S(1)} custom-call(s32[64]{0:T(128)S(1)} %copy-done.4, s32[5]{0:T(128)S(1)} %stack.23.where_ref, bf16[4,256,128]{2,1,0:T(8,128)(2,1)S(1)} %bitcast.20, bf16[4,256,128]{2,1,0:T(8,128)(2,1)S(1)} %bitcast.29, bf16[4,128,128]{2,1,0:T(8,128)(2,1)S(1)} %bitcast.33, bf16[4,128,128]{2,1,0:T(8,128)(2,1)S(1)} %bitcast.39, ...), custom_call_target="tpu_custom_call" | custom-call | flops 1073741824 | bytes 1048576 | tf_op jit(solution)/shard_map/stats/pallas_call | solution.py:294
  38.5 1.8 %collective-permute-start.10 = (f32[4,8,256]{2,1,0:T(8,128)S(1)}, f32[4,8,256]{2,1,0:T(8,128)S(1)}, u32[]{:S(2)}, u32[]{:S(2)}) collective-permute-start(f32[4,8,256]{2,1,0:T(8,128)S(1)} %stats.2.rest_0_), channel_id=1, source_target_pairs={{0,16},{8,24},{16,0},{24,8},{1,17},{9,25},{17,1},{25,9},{2,18},{10... | collective-permute-start | bytes 98312 | tf_op jit(solution)/shard_map/ppermute | solution.py:29
  40.2 0.0 collective-permute-done.11.rest_3_
  40.2 2.2 %collective-permute-done.10.rest_2_ = f32[4,8,256]{2,1,0:T(8,128)S(1)} collective-permute-done((f32[4,8,256]{2,1,0:T(8,128)S(1)}, f32[4,8,256]{2,1,0:T(8,128)S(1)}, u32[]{:S(2)}, u32[]{:S(2)}) %collective-permute-start.10) | collective-permute-done | bytes 32800 | tf_op jit(solution)/shard_map/ppermute | solution.py:29
  42.4 4.6 %grads.2 = (f32[512,128]{1,0:T(8,128)S(1)}, bf16[512,128]{1,0:T(8,128)(2,1)S(1)}, f32[512,128]{1,0:T(8,128)S(1)}, bf16[512,128]{1,0:T(8,128)(2,1)S(1)}, f32[8,12...) custom-call(s32[64]{0:T(128)S(1)} %copy-done.4, s32[5]{0:T(128)S(1)} %stack.23.where_ref, f32[4,8,256]{2,1,0:T(8,128)S(1)} %stats.2.rest_0_, ...), custom_call_target="tpu_custom_call" | custom-call | flops 3221225472 | bytes 2097152 | tf_op jit(solution)/shard_map/grads/pallas_call | solution.py:334
  47.0 0.1 collective-permute-start.15
  47.1 0.5 collective-permute-start.17
  47.6 5.3 %grads.3 = (f32[512,128]{1,0:T(8,128)S(1)}, bf16[512,128]{1,0:T(8,128)(2,1)S(1)}, f32[512,128]{1,0:T(8,128)S(1)}, bf16[512,128]{1,0:T(8,128)(2,1)S(1)}, f32[256,...) custom-call(s32[64]{0:T(128)S(1)} %copy-done.4, ...), custom_call_target="tpu_custom_call" | custom-call | flops 3221225472 | bytes 2097152 | tf_op jit(solution)/shard_map/grads/pallas_call | solution.py:334
  52.9 0.1 collective-permute-start.19
  53.1 0.4 collective-permute-start.21
  53.5 3.2 %collective-permute-start.12 = (bf16[256,256]{1,0:T(8,128)(2,1)S(1)}, bf16[256,256]{1,0:T(8,128)(2,1)S(1)}, u32[]{:S(2)}, u32[]{:S(2)}) collective-permute-start(bf16[256,256]{1,0:T(8,128)(2,1)S(1)} %get-tuple-element.26), channel_id=1, source_target_pairs={{0,16},{8,24},{16,0},{24,8},{1,17},{9,25},{17,1},{25,9},{2,18},{10... | collective-permute-start | bytes 393224 | tf_op jit(solution)/shard_map/ppermute | solution.py:29
  56.7 0.0 collective-permute-done.15
  56.7 0.0 collective-permute-start.13
  56.7 0.2 collective-permute-start.14
  57.0 2.8 %collective-permute-start.16 = (bf16[512,128]{1,0:T(8,128)(2,1)S(1)}, bf16[512,128]{1,0:T(8,128)(2,1)S(1)}, u32[]{:S(2)}, u32[]{:S(2)}) collective-permute-start(bf16[512,128]{1,0:T(8,128)(2,1)S(1)} %add_convert_fusion.3), channel_id=1, source_target_pairs={{3,0},{4,1},{5,2},{6,3},{7,4},{0,5},{1,6},{2,7},{11,8},{12,9},{13,... | collective-permute-start | bytes 393224 | tf_op jit(solution)/shard_map/ppermute | solution.py:25
  59.8 1.2 %collective-permute-done.12 = bf16[256,256]{1,0:T(8,128)(2,1)S(1)} collective-permute-done((bf16[256,256]{1,0:T(8,128)(2,1)S(1)}, bf16[256,256]{1,0:T(8,128)(2,1)S(1)}, u32[]{:S(2)}, u32[]{:S(2)}) %collective-permute-start.12) | collective-permute-done | bytes 131104 | tf_op jit(solution)/shard_map/ppermute | solution.py:29
  61.0 6.8 %collective-permute-start.18 = (bf16[512,128]{1,0:T(8,128)(2,1)S(1)}, bf16[512,128]{1,0:T(8,128)(2,1)S(1)}, u32[]{:S(2)}, u32[]{:S(2)}) collective-permute-start(bf16[512,128]{1,0:T(8,128)(2,1)S(1)} %add_convert_fusion.2), channel_id=1, source_target_pairs={{2,0},{3,1},{4,2},{5,3},{6,4},{7,5},{0,6},{1,7},{10,8},{11,9},{12,... | collective-permute-start | bytes 393224 | tf_op jit(solution)/shard_map/ppermute | solution.py:25
  67.8 0.1 select_convert_fusion.1
  67.9 0.7 pad_maximum_fusion
  68.6 1.8 %collective-permute-done.18 = bf16[512,128]{1,0:T(8,128)(2,1)S(1)} collective-permute-done((bf16[512,128]{1,0:T(8,128)(2,1)S(1)}, bf16[512,128]{1,0:T(8,128)(2,1)S(1)}, u32[]{:S(2)}, u32[]{:S(2)}) %collective-permute-start.18) | collective-permute-done | bytes 131104 | tf_op jit(solution)/shard_map/ppermute | solution.py:25
  70.4 2.3 %collective-permute-done.20 = bf16[512,128]{1,0:T(8,128)(2,1)S(1)} collective-permute-done((bf16[512,128]{1,0:T(8,128)(2,1)S(1)}, bf16[512,128]{1,0:T(8,128)(2,1)S(1)}, u32[]{:S(2)}, u32[]{:S(2)}) %collective-permute-start.20) | collective-permute-done | bytes 131104 | tf_op jit(solution)/shard_map/ppermute | solution.py:25
  72.8 0.1 add_convert_fusion
  72.9 0.7 fusion
  (19 shorter events, 0.2 us)
Async XLA Ops:
  0.7 1.0 %copy-start = (bf16[256,512]{1,0:T(8,128)(2,1)S(1)}, bf16[256,512]{1,0:T(8,128)(2,1)}, u32[]{:S(2)}) copy-start(bf16[256,512]{1,0:T(8,128)(2,1)} %q_ref.1) | copy-start | bytes 786436
  1.7 0.9 %copy-start.1 = (bf16[256,512]{1,0:T(8,128)(2,1)S(1)}, bf16[256,512]{1,0:T(8,128)(2,1)}, u32[]{:S(2)}) copy-start(bf16[256,512]{1,0:T(8,128)(2,1)} %g_ref.1) | copy-start | bytes 786436
  2.6 0.8 %copy-start.2 = (bf16[256,128]{1,0:T(8,128)(2,1)S(1)}, bf16[256,128]{1,0:T(8,128)(2,1)}, u32[]{:S(2)}) copy-start(bf16[256,128]{1,0:T(8,128)(2,1)} %k_ref.1) | copy-start | bytes 196612
  3.5 0.8 %copy-start.3 = (bf16[256,128]{1,0:T(8,128)(2,1)S(1)}, bf16[256,128]{1,0:T(8,128)(2,1)}, u32[]{:S(2)}) copy-start(bf16[256,128]{1,0:T(8,128)(2,1)} %v_ref.1) | copy-start | bytes 196612
  5.0 10.5 %collective-permute-start.2 = (bf16[512,128]{1,0:T(8,128)(2,1)S(1)}, bf16[512,128]{1,0:T(8,128)(2,1)S(1)}, u32[]{:S(2)}, u32[]{:S(2)}) collective-permute-start(bf16[512,128]{1,0:T(8,128)(2,1)S(1)} %get-tuple-element.22), channel_id=1, source_target_pairs={{7,0},{0,1},{1,2},{2,3},{3,4},{4,5},{5,6},{6,7},{15,8},{8,9},{9,10... | collective-permute-start | bytes 393224 | tf_op jit(solution)/shard_map/ppermute | solution.py:25
  8.0 9.1 %collective-permute-start.4 = (bf16[512,128]{1,0:T(8,128)(2,1)S(1)}, bf16[512,128]{1,0:T(8,128)(2,1)S(1)}, u32[]{:S(2)}, u32[]{:S(2)}) collective-permute-start(bf16[512,128]{1,0:T(8,128)(2,1)S(1)} %get-tuple-element.22), channel_id=1, source_target_pairs={{6,0},{7,1},{0,2},{1,3},{2,4},{3,5},{4,6},{5,7},{14,8},{15,9},{8,1... | collective-permute-start | bytes 393224 | tf_op jit(solution)/shard_map/ppermute | solution.py:25
  9.6 13.4 %collective-permute-start.6 = (bf16[512,128]{1,0:T(8,128)(2,1)S(1)}, bf16[512,128]{1,0:T(8,128)(2,1)S(1)}, u32[]{:S(2)}, u32[]{:S(2)}) collective-permute-start(bf16[512,128]{1,0:T(8,128)(2,1)S(1)} %get-tuple-element.22), channel_id=1, source_target_pairs={{5,0},{6,1},{7,2},{0,3},{1,4},{2,5},{3,6},{4,7},{13,8},{14,9},{15,... | collective-permute-start | bytes 393224 | tf_op jit(solution)/shard_map/ppermute | solution.py:25
  12.1 10.9 %collective-permute-start.1 = (bf16[512,128]{1,0:T(8,128)(2,1)S(1)}, bf16[512,128]{1,0:T(8,128)(2,1)S(1)}, u32[]{:S(2)}, u32[]{:S(2)}) collective-permute-start(bf16[512,128]{1,0:T(8,128)(2,1)S(1)} %get-tuple-element.22), channel_id=1, source_target_pairs={{0,8},{8,0},{16,24},{24,16},{1,9},{9,1},{17,25},{25,17},{2,10},{10... | collective-permute-start | bytes 393224 | tf_op jit(solution)/shard_map/ppermute | solution.py:29
  15.5 8.0 %collective-permute-start.3 = (bf16[512,128]{1,0:T(8,128)(2,1)S(1)}, bf16[512,128]{1,0:T(8,128)(2,1)S(1)}, u32[]{:S(2)}, u32[]{:S(2)}) collective-permute-start(bf16[512,128]{1,0:T(8,128)(2,1)S(1)} %collective-permute-done.2), channel_id=1, source_target_pairs={{0,8},{8,0},{16,24},{24,16},{1,9},{9,1},{17,25},{25,17},{2,10},{10... | collective-permute-start | bytes 393224 | tf_op jit(solution)/shard_map/ppermute | solution.py:29
  15.5 9.4 %collective-permute-start.8 = (bf16[1024,128]{1,0:T(8,128)(2,1)S(1)}, bf16[1024,128]{1,0:T(8,128)(2,1)S(1)}, u32[]{:S(2)}, u32[]{:S(2)}) collective-permute-start(bf16[1024,128]{1,0:T(8,128)(2,1)S(1)} %get-tuple-element.20), channel_id=1, source_target_pairs={{0,16},{8,24},{16,0},{24,8},{1,17},{9,25},{17,1},{25,9},{2,18},{10... | collective-permute-start | bytes 786440 | tf_op jit(solution)/shard_map/ppermute | solution.py:29
  17.1 12.2 %collective-permute-start.9 = (bf16[1024,128]{1,0:T(8,128)(2,1)S(1)}, bf16[1024,128]{1,0:T(8,128)(2,1)S(1)}, u32[]{:S(2)}, u32[]{:S(2)}) collective-permute-start(bf16[1024,128]{1,0:T(8,128)(2,1)S(1)} %get-tuple-element.21), channel_id=1, source_target_pairs={{0,24},{8,16},{16,8},{24,0},{1,25},{9,17},{17,9},{25,1},{2,26},{10... | collective-permute-start | bytes 786440 | tf_op jit(solution)/shard_map/ppermute | solution.py:29
  23.0 12.1 %collective-permute-start = (bf16[1024,128]{1,0:T(8,128)(2,1)S(1)}, bf16[1024,128]{1,0:T(8,128)(2,1)S(1)}, u32[]{:S(2)}, u32[]{:S(2)}) collective-permute-start(bf16[1024,128]{1,0:T(8,128)(2,1)S(1)} %get-tuple-element.21), channel_id=1, source_target_pairs={{0,8},{8,0},{16,24},{24,16},{1,9},{9,1},{17,25},{25,17},{2,10},{10... | collective-permute-start | bytes 786440 | tf_op jit(solution)/shard_map/ppermute | solution.py:29
  23.0 1.7 %collective-permute-start.5 = (bf16[512,128]{1,0:T(8,128)(2,1)S(1)}, bf16[512,128]{1,0:T(8,128)(2,1)S(1)}, u32[]{:S(2)}, u32[]{:S(2)}) collective-permute-start(bf16[512,128]{1,0:T(8,128)(2,1)S(1)} %collective-permute-done.4), channel_id=1, source_target_pairs={{0,8},{8,0},{16,24},{24,16},{1,9},{9,1},{17,25},{25,17},{2,10},{10... | collective-permute-start | bytes 393224 | tf_op jit(solution)/shard_map/ppermute | solution.py:29
  23.5 1.4 %collective-permute-start.7 = (bf16[512,128]{1,0:T(8,128)(2,1)S(1)}, bf16[512,128]{1,0:T(8,128)(2,1)S(1)}, u32[]{:S(2)}, u32[]{:S(2)}) collective-permute-start(bf16[512,128]{1,0:T(8,128)(2,1)S(1)} %collective-permute-done.6), channel_id=1, source_target_pairs={{0,8},{8,0},{16,24},{24,16},{1,9},{9,1},{17,25},{25,17},{2,10},{10... | collective-permute-start | bytes 393224 | tf_op jit(solution)/shard_map/ppermute | solution.py:29
  29.4 0.7 copy-start.4
  33.7 6.5 %collective-permute-start.11 = (f32[4,8,256]{2,1,0:T(8,128)S(1)}, f32[4,8,256]{2,1,0:T(8,128)S(1)}, u32[]{:S(2)}, u32[]{:S(2)}) collective-permute-start(f32[4,8,256]{2,1,0:T(8,128)S(1)} %stats.3.rest_1_), channel_id=1, source_target_pairs={{0,16},{8,24},{16,0},{24,8},{1,17},{9,25},{17,1},{25,9},{2,18},{10... | collective-permute-start | bytes 98312 | tf_op jit(solution)/shard_map/ppermute | solution.py:29
  38.5 4.0 %collective-permute-start.10 = (f32[4,8,256]{2,1,0:T(8,128)S(1)}, f32[4,8,256]{2,1,0:T(8,128)S(1)}, u32[]{:S(2)}, u32[]{:S(2)}) collective-permute-start(f32[4,8,256]{2,1,0:T(8,128)S(1)} %stats.2.rest_0_), channel_id=1, source_target_pairs={{0,16},{8,24},{16,0},{24,8},{1,17},{9,25},{17,1},{25,9},{2,18},{10... | collective-permute-start | bytes 98312 | tf_op jit(solution)/shard_map/ppermute | solution.py:29
  47.0 9.6 %collective-permute-start.15 = (bf16[512,128]{1,0:T(8,128)(2,1)S(1)}, bf16[512,128]{1,0:T(8,128)(2,1)S(1)}, u32[]{:S(2)}, u32[]{:S(2)}) collective-permute-start(bf16[512,128]{1,0:T(8,128)(2,1)S(1)} %get-tuple-element.30), channel_id=1, source_target_pairs={{0,8},{8,0},{16,24},{24,16},{1,9},{9,1},{17,25},{25,17},{2,10},{10... | collective-permute-start | bytes 393224 | tf_op jit(solution)/shard_map/ppermute | solution.py:29
  47.1 9.6 %collective-permute-start.17 = (bf16[512,128]{1,0:T(8,128)(2,1)S(1)}, bf16[512,128]{1,0:T(8,128)(2,1)S(1)}, u32[]{:S(2)}, u32[]{:S(2)}) collective-permute-start(bf16[512,128]{1,0:T(8,128)(2,1)S(1)} %get-tuple-element.32), channel_id=1, source_target_pairs={{0,8},{8,0},{16,24},{24,16},{1,9},{9,1},{17,25},{25,17},{2,10},{10... | collective-permute-start | bytes 393224 | tf_op jit(solution)/shard_map/ppermute | solution.py:29
  52.9 4.0 %collective-permute-start.19 = (bf16[512,128]{1,0:T(8,128)(2,1)S(1)}, bf16[512,128]{1,0:T(8,128)(2,1)S(1)}, u32[]{:S(2)}, u32[]{:S(2)}) collective-permute-start(bf16[512,128]{1,0:T(8,128)(2,1)S(1)} %get-tuple-element.34), channel_id=1, source_target_pairs={{0,8},{8,0},{16,24},{24,16},{1,9},{9,1},{17,25},{25,17},{2,10},{10... | collective-permute-start | bytes 393224 | tf_op jit(solution)/shard_map/ppermute | solution.py:29
  53.1 15.6 %collective-permute-start.21 = (bf16[512,128]{1,0:T(8,128)(2,1)S(1)}, bf16[512,128]{1,0:T(8,128)(2,1)S(1)}, u32[]{:S(2)}, u32[]{:S(2)}) collective-permute-start(bf16[512,128]{1,0:T(8,128)(2,1)S(1)} %get-tuple-element.36), channel_id=1, source_target_pairs={{0,8},{8,0},{16,24},{24,16},{1,9},{9,1},{17,25},{25,17},{2,10},{10... | collective-permute-start | bytes 393224 | tf_op jit(solution)/shard_map/ppermute | solution.py:29
  53.5 7.5 %collective-permute-start.12 = (bf16[256,256]{1,0:T(8,128)(2,1)S(1)}, bf16[256,256]{1,0:T(8,128)(2,1)S(1)}, u32[]{:S(2)}, u32[]{:S(2)}) collective-permute-start(bf16[256,256]{1,0:T(8,128)(2,1)S(1)} %get-tuple-element.26), channel_id=1, source_target_pairs={{0,16},{8,24},{16,0},{24,8},{1,17},{9,25},{17,1},{25,9},{2,18},{10... | collective-permute-start | bytes 393224 | tf_op jit(solution)/shard_map/ppermute | solution.py:29
  56.7 11.1 %collective-permute-start.13 = (bf16[256,256]{1,0:T(8,128)(2,1)S(1)}, bf16[256,256]{1,0:T(8,128)(2,1)S(1)}, u32[]{:S(2)}, u32[]{:S(2)}) collective-permute-start(bf16[256,256]{1,0:T(8,128)(2,1)S(1)} %get-tuple-element.27), channel_id=1, source_target_pairs={{0,8},{8,0},{16,24},{24,16},{1,9},{9,1},{17,25},{25,17},{2,10},{10... | collective-permute-start | bytes 393224 | tf_op jit(solution)/shard_map/ppermute | solution.py:29
  56.7 11.1 %collective-permute-start.14 = (bf16[256,256]{1,0:T(8,128)(2,1)S(1)}, bf16[256,256]{1,0:T(8,128)(2,1)S(1)}, u32[]{:S(2)}, u32[]{:S(2)}) collective-permute-start(bf16[256,256]{1,0:T(8,128)(2,1)S(1)} %get-tuple-element.28), channel_id=1, source_target_pairs={{0,24},{8,16},{16,8},{24,0},{1,25},{9,17},{17,9},{25,1},{2,26},{10... | collective-permute-start | bytes 393224 | tf_op jit(solution)/shard_map/ppermute | solution.py:29
  57.0 11.7 %collective-permute-start.16 = (bf16[512,128]{1,0:T(8,128)(2,1)S(1)}, bf16[512,128]{1,0:T(8,128)(2,1)S(1)}, u32[]{:S(2)}, u32[]{:S(2)}) collective-permute-start(bf16[512,128]{1,0:T(8,128)(2,1)S(1)} %add_convert_fusion.3), channel_id=1, source_target_pairs={{3,0},{4,1},{5,2},{6,3},{7,4},{0,5},{1,6},{2,7},{11,8},{12,9},{13,... | collective-permute-start | bytes 393224 | tf_op jit(solution)/shard_map/ppermute | solution.py:25
  61.0 9.4 %collective-permute-start.18 = (bf16[512,128]{1,0:T(8,128)(2,1)S(1)}, bf16[512,128]{1,0:T(8,128)(2,1)S(1)}, u32[]{:S(2)}, u32[]{:S(2)}) collective-permute-start(bf16[512,128]{1,0:T(8,128)(2,1)S(1)} %add_convert_fusion.2), channel_id=1, source_target_pairs={{2,0},{3,1},{4,2},{5,3},{6,4},{7,5},{0,6},{1,7},{10,8},{11,9},{12,... | collective-permute-start | bytes 393224 | tf_op jit(solution)/shard_map/ppermute | solution.py:25
  67.8 5.0 %collective-permute-start.20 = (bf16[512,128]{1,0:T(8,128)(2,1)S(1)}, bf16[512,128]{1,0:T(8,128)(2,1)S(1)}, u32[]{:S(2)}, u32[]{:S(2)}) collective-permute-start(bf16[512,128]{1,0:T(8,128)(2,1)S(1)} %add_convert_fusion.1), channel_id=1, source_target_pairs={{1,0},{2,1},{3,2},{4,3},{5,4},{6,5},{7,6},{0,7},{9,8},{10,9},{11,1... | collective-permute-start | bytes 393224 | tf_op jit(solution)/shard_map/ppermute | solution.py:25

commit v2 on v1

--- a/solution.py
+++ b/solution.py
@@ -38,26 +38,26 @@
     bias_ref[2] = jnp.full((size, size), NEG, jnp.float32)
 
 
-def build_list(sizes, queries, blocks, place_ref, where_ref, list_ref):
+def build_list(sizes, queries, blocks, where_ref, list_ref):
     outer_size, key_blocks = sizes
     outer = where_ref[4]
     key_place = {}
     for block in blocks:
         step, core, half = block // 4, (block // 2) % 2, block % 2
         source = lax.rem(outer - step + outer_size, outer_size)
-        key_place[block] = place_ref[(where_ref[core] * outer_size + source) * 2 + half]
+        key_place[block] = where_ref[8 + (where_ref[core] * outer_size + source) * 2 + half]
     position = jnp.int32(0)
     for query in queries:
-        query_place = place_ref[(where_ref[query // 2] * outer_size + outer) * 2 + query % 2]
+        query_place = where_ref[8 + (where_ref[query // 2] * outer_size + outer) * 2 + query % 2]
         for block in blocks:
             kind = jnp.where(key_place[block] == query_place, 1, 0)
             list_ref[position] = (query * key_blocks + block) * 4 + kind
             position = position + jnp.where(key_place[block] <= query_place, 1, 0)
         list_ref[position] = (query * key_blocks + blocks[0]) * 4 + 2
         position = position + lax.rem(position, 2)
-    for extra in range(4):
+    for extra in range(10):
         list_ref[position + extra] = (queries[0] * key_blocks + blocks[0]) * 4 + 2
-    return (position + 2) // 4
+    return (position + 6) // 8
 
 
 def entry_of(list_ref, index, key_blocks):
@@ -66,7 +66,7 @@
     return at0 // key_blocks, at0 % key_blocks, e0 % 4, at1 % key_blocks, e1 % 4
 
 
-def score_tiles(entry, factor, qg, kv, bias, t_ref, dp_ref):
+def score_tiles(entry, factor, qg, kv, bias, t_ref, dp_ref, top_ref=None):
     query, j0, b0, j1, b1 = entry
     k2 = jnp.concatenate([kv[2 * j0], kv[2 * j1]], axis=0)
     v2 = jnp.concatenate([kv[2 * j0 + 1], kv[2 * j1 + 1]], axis=0)
@@ -74,7 +74,10 @@
     b2 = jnp.concatenate(
         [jnp.concatenate([low, low], axis=1), jnp.concatenate([high, high], axis=1)], axis=0
     )
-    t_ref[...] = dot_nt(k2, qg[2 * query]) * factor + b2
+    t = dot_nt(k2, qg[2 * query]) * factor + b2
+    t_ref[...] = t
+    if top_ref is not None:
+        top_ref[...] = jnp.max(t.reshape(-1, 8, t.shape[1]), axis=0)
     dp_ref[...] = dot_nt(v2, qg[2 * query + 1])
 
 
@@ -86,61 +89,63 @@
 
 def pair_loop(trips, load, use):
     load(0, 0)
+    load(1, 1)
 
     @pl.loop(0, trips)
     def _(i):
-        load(2 * i + 1, 1)
-        use(2 * i, 0)
-        load(2 * i + 2, 0)
-        use(2 * i + 1, 1)
-
-
-def pack_kernel(where_ref, q_ref, g_ref, k_ref, v_ref, mine, theirs, kv):
-    size = k_ref.shape[1]
-    half_len = k_ref.shape[0] // 2
+        load(4 * i + 2, 2)
+        load(4 * i + 3, 3)
+        use(4 * i, 0)
+        use(4 * i + 1, 1)
+        load(4 * i + 4, 0)
+        load(4 * i + 5, 1)
+        use(4 * i + 2, 2)
+        use(4 * i + 3, 3)
+
+
+def pack_kernel(size, where_ref, q_ref, g_ref, mine, theirs, sems):
+    half_len = q_ref.shape[0] // 2
     pairs = q_ref.shape[1] // size // 2
     near = lax.rem(where_ref[0], 2)
-
-    def put(dst, first):
-        for half in range(2):
+    copies = []
+
+    def put(src, dst):
+        copies.append(pltpu.make_async_copy(src, dst, sems.at[len(copies)]))
+
+    for half in range(2):
+        rows = pl.ds(half * half_len, half_len)
+        for dst, core in ((mine, near), (theirs, 1 - near)):
             for which, src in enumerate((q_ref, g_ref)):
                 for head in range(pairs):
                     row = ((half * 2 + which) * pairs + head) * half_len
-                    dst[pl.ds(row, half_len), :] = src[
-                        pl.ds(half * half_len, half_len), pl.ds((first + head) * size, size)
-                    ]
-
-    for core in range(2):
-
-        @pl.when(near == core)
-        def _():
-            put(mine, core * pairs)
-            put(theirs, (1 - core) * pairs)
-
-    for half in range(2):
-        for which, src in enumerate((k_ref, v_ref)):
-            kv[pl.ds((half * 2 + which) * half_len, half_len), :] = src[
-                pl.ds(half * half_len, half_len), :
-            ]
-
-
-def stats_kernel(sizes, factor, which, shards, place_ref, where_ref, *rest):
+                    lane = pl.multiple_of((core * pairs + head) * size, size)
+                    put(src.at[rows, pl.ds(lane, size)], dst.at[pl.ds(row, half_len), :])
+    for copy in copies:
+        copy.start()
+    for copy in copies:
+        copy.wait()
+
+
+def stats_kernel(sizes, factor, which, shards, where_ref, *rest):
     outer_size, key_blocks, _, width = sizes
+    merged = which[0] > 0
+    if merged:
+        early, rest = rest[0], rest[1:]
     q_refs, kv_refs = rest[: len(which)], rest[len(which) : len(which) + shards]
-    out_ref, qg, kv, bias, t0, d0, t1, d1, state, lists = rest[len(which) + shards :]
+    out_ref, qg, kv, bias, *tiles, state, lists = rest[len(which) + shards :]
     stack_refs(kv_refs, kv)
     stack_refs(q_refs, qg)
     here = [2 * t + half for t in which for half in range(2)]
     first = here[0]
     trips = build_list(
-        (outer_size, key_blocks), here, range(key_blocks), place_ref, where_ref, lists
+        (outer_size, key_blocks), here, range(key_blocks), where_ref, lists
     )
     fill_bias(bias)
     count = len(here)
     state[0] = jnp.full((count, 8, width), NEG, jnp.float32)
     state[1] = jnp.zeros((count, 8, width), jnp.float32)
     state[2] = jnp.zeros((count, 8, width), jnp.float32)
-    slots = ((t0, d0), (t1, d1))
+    slots = [tiles[3 * i : 3 * i + 3] for i in range(4)]
 
     def entry(n):
         query, j0, b0, j1, b1 = entry_of(lists, n, key_blocks)
@@ -151,10 +156,9 @@
 
     def use(n, slot):
         query = entry(n)[0]
-        t_ref, d_ref = slots[slot]
+        t_ref, d_ref, top = slots[slot]
         m, l, r = state[0, query], state[1, query], state[2, query]
-        top = jnp.max(t_ref[...].reshape(-1, 8, width), axis=0)
-        m_new = jnp.maximum(m, jnp.max(top, axis=0, keepdims=True))
+        m_new = jnp.maximum(m, jnp.max(top[...], axis=0, keepdims=True))
         corr = jnp.exp2(m - m_new)
         p = jnp.exp2(t_ref[...].reshape(-1, 8, width) - m_new)
         state[0, query] = m_new
@@ -163,23 +167,25 @@
 
     pair_loop(trips, load, use)
     for i in range(count):
-        out_ref[i, 0:1] = state[0, i, 0:1]
-        out_ref[i, 1:2] = jnp.sum(state[1, i], axis=0, keepdims=True)
-        out_ref[i, 2:3] = jnp.sum(state[2, i], axis=0, keepdims=True)
-        out_ref[i, 3:8] = jnp.zeros((5, width), jnp.float32)
-
-
-def grads_kernel(sizes, scale, steps, last, place_ref, where_ref, *rest):
+        at = pl.ds(first + i if merged else i, 1)
+        out_ref[0, at] = state[0, i, 0:1]
+        out_ref[1, at] = jnp.sum(state[1, i], axis=0, keepdims=True)
+        out_ref[2, at] = jnp.sum(state[2, i], axis=0, keepdims=True)
+    if merged:
+        out_ref[:, pl.ds(0, first)] = early[:, pl.ds(0, first)]
+    else:
+        out_ref[:, pl.ds(count, count)] = jnp.zeros((3, count, width), jnp.float32)
+
+
+def grads_kernel(sizes, scale, steps, last, where_ref, *rest):
     outer_size, key_blocks, size, width = sizes
     pairs = width // size
-    stat_refs = rest[:4] if not last else ()
-    carry_in = rest[:2] if last else ()
-    rest = rest[2:] if last else rest[4:]
+    carry_in, rest = rest[:2], rest[2:]
     q_refs, kv_refs = rest[:4], rest[4 : 4 + 2 * len(steps)]
     rest = rest[4 + 2 * len(steps) :]
     outs, rest = rest[: 2 * len(steps)], rest[2 * len(steps) :]
     tops, rest = rest[: (4 if last else 2)], rest[(4 if last else 2) :]
-    qg, kv, kt, dk, dv, dq, base, bias, t0, d0, t1, d1, lists = rest
+    qg, kv, kt, dk, dv, dq, base, bias, *tiles, lists = rest
     low = 4 * min(steps)
     blocks = [4 * step + i for step in sorted(steps) for i in range(4)]
     stack_refs(kv_refs, kv)
@@ -187,17 +193,17 @@
     if last:
         dq[...] = carry_in[0][...]
         base[...] = carry_in[1][...]
-    trips = build_list((outer_size, key_blocks), range(8), blocks, place_ref, where_ref, lists)
+    trips = build_list((outer_size, key_blocks), range(8), blocks, where_ref, lists)
     fill_bias(bias)
     if not last:
         for query in range(8):
-            a = stat_refs[query // 4][query % 4]
-            b = stat_refs[2 + (1 - query // 4)][query % 4]
-            m = jnp.maximum(a[0:1], b[0:1])
-            ea, eb = jnp.exp2(a[0:1] - m), jnp.exp2(b[0:1] - m)
-            total = a[1:2] * ea + b[1:2] * eb
+            here, there = pl.ds(query, 1), pl.ds(query ^ 4, 1)
+            mine, other = carry_in
+            m = jnp.maximum(mine[0, here], other[0, there])
+            ea, eb = jnp.exp2(mine[0, here] - m), jnp.exp2(other[0, there] - m)
+            total = mine[1, here] * ea + other[1, there] * eb
             base[query, 0:1] = m + jnp.log2(total)
-            base[query, 1:2] = (a[2:3] * ea + b[2:3] * eb) / total
+            base[query, 1:2] = (mine[2, here] * ea + other[2, there] * eb) / total
             base[query, 2:8] = jnp.zeros((6, width), jnp.float32)
         dq[...] = jnp.zeros_like(dq)
     dk[...] = jnp.zeros_like(dk)
@@ -205,7 +211,7 @@
     for block in range(len(blocks)):
         kt[block] = kv[2 * block].T
     factor = scale * LOG2E
-    slots = ((t0, d0), (t1, d1))
+    slots = [tiles[2 * i : 2 * i + 2] for i in range(4)]
 
     def entry(n):
         query, j0, b0, j1, b1 = entry_of(lists, n, key_blocks)
@@ -259,27 +265,32 @@
     scale = 1.0 / math.sqrt(size)
     inner = lax.axis_index("inner")
     outer = lax.axis_index("outer")
-    where = jnp.stack([inner, inner ^ 1, inner ^ 2, inner ^ 3, outer]).astype(jnp.int32)
+    where = jnp.concatenate(
+        [jnp.stack([inner, inner ^ 1, inner ^ 2, inner ^ 3, outer] + [outer] * 3), block_place]
+    )
     smem = pl.BlockSpec(memory_space=pltpu.SMEM)
     vmem = pl.BlockSpec(memory_space=pltpu.VMEM)
     params = pltpu.CompilerParams(vmem_limit_bytes=16 << 20)
     low, full = jnp.bfloat16, jnp.float32
 
     q_shape, kv_shape = (4 * width, size), (4 * block_len, size)
-    mine, theirs, kv = pl.pallas_call(
-        pack_kernel,
+    kv = jnp.stack(
+        [keys.reshape(2, block_len, size), values.reshape(2, block_len, size)], axis=1
+    ).reshape(kv_shape)
+    own2 = from_behind(kv, "outer", 2)
+    mine, theirs = pl.pallas_call(
+        functools.partial(pack_kernel, size),
         name="pack",
-        out_shape=[
-            jax.ShapeDtypeStruct(q_shape, low),
-            jax.ShapeDtypeStruct(q_shape, low),
-            jax.ShapeDtypeStruct(kv_shape, low),
-        ],
-        in_specs=[smem] + [vmem] * 4,
-        out_specs=[vmem] * 3,
+        out_shape=[jax.ShapeDtypeStruct(q_shape, low)] * 2,
+        in_specs=[smem] + [pl.BlockSpec(memory_space=pltpu.HBM)] * 2,
+        out_specs=[vmem] * 2,
+        scratch_shapes=[pltpu.SemaphoreType.DMA((8 * pairs,))],
         compiler_params=params,
-    )(where, queries, out_grad, keys, values)
+    )(where, queries, out_grad)
     asked = [mine, swap(theirs, "inner", 1), swap(mine, "inner", 2), swap(theirs, "inner", 3)]
-    own = [kv] + [from_behind(kv, "outer", step) for step in range(1, STEPS)]
+    own1 = swap(jnp.where(outer % 2 == 1, own2, kv), "outer", 1)
+    own3 = from_behind(own2, "outer", 1)
+    own = [kv, own1, own2, own3]
     near = [swap(block, "inner", 1) for block in own]
     q_parts = [part.reshape(4, width, size) for part in asked]
     shards = [block.reshape(4, block_len, size) for two in zip(own, near) for block in two]
@@ -289,35 +300,31 @@
     tile = pltpu.VMEM((2 * block_len, width), full)
     bias_table = pltpu.VMEM((3, block_len, block_len), full)
 
-    def stats_call(which):
+    def stats_call(which, *early):
         count = 2 * len(which)
         return pl.pallas_call(
             functools.partial(stats_kernel, sizes, scale * LOG2E, which, len(shards)),
             name="stats",
-            out_shape=jax.ShapeDtypeStruct((count, 8, width), full),
-            in_specs=[smem, smem] + [vmem] * (len(which) + len(shards)),
+            out_shape=jax.ShapeDtypeStruct((3, 8, width), full),
+            in_specs=[smem] + [vmem] * (len(early) + len(which) + len(shards)),
             out_specs=vmem,
             scratch_shapes=[
                 pltpu.VMEM((2 * count, width, size), low),
                 pltpu.VMEM((2 * key_blocks, block_len, size), low),
                 bias_table,
-                tile,
-                tile,
-                tile,
-                tile,
+                *[tile, tile, pltpu.VMEM((8, width), full)] * 4,
                 pltpu.VMEM((3, count, 8, width), full),
-                pltpu.SMEM((count * (key_blocks + 1) + 8,), jnp.int32),
+                pltpu.SMEM((count * key_blocks + 16,), jnp.int32),
             ],
             compiler_params=params,
             cost_estimate=pl.CostEstimate(
                 flops=flops // 2, bytes_accessed=1 << 20, transcendentals=0
             ),
-        )(block_place, where, *[q_parts[t] for t in which], *shards)
-
-    stats = []
-    for which in ((0, 1), (2, 3)):
-        stats.append(stats_call(which))
-    others = [swap(stat, "inner", 2) for stat in stats]
+        )(where, *early, *[q_parts[t] for t in which], *shards)
+
+    early = stats_call((0, 1))
+    stats = stats_call((2, 3), early)
+    others = swap(stats, "inner", 2)
     shard_f32 = jax.ShapeDtypeStruct(kv_shape, full)
     shard_low = jax.ShapeDtypeStruct(kv_shape, low)
 
@@ -335,7 +342,7 @@
             functools.partial(grads_kernel, sizes, scale, steps, last),
             name="grads",
             out_shape=[shard_f32, shard_low] * n + tops,
-            in_specs=[smem, smem] + [vmem] * (len(extra) + 4 + 2 * n),
+            in_specs=[smem] + [vmem] * (len(extra) + 4 + 2 * n),
             out_specs=[vmem] * (2 * n + len(tops)),
             scratch_shapes=[
                 pltpu.VMEM((16, width, size), low),
@@ -346,22 +353,19 @@
                 pltpu.VMEM((8, size, width), full),
                 pltpu.VMEM((8, 8, width), full),
                 bias_table,
-                tile,
-                tile,
-                tile,
-                tile,
-                pltpu.SMEM((8 * (4 * n + 1) + 8,), jnp.int32),
+                *[tile] * 8,
+                pltpu.SMEM((8 * 4 * n + 16,), jnp.int32),
             ],
             compiler_params=params,
             cost_estimate=pl.CostEstimate(
                 flops=flops * 3 * n // STEPS, bytes_accessed=1 << 21, transcendentals=0
             ),
-        )(block_place, where, *extra, *q_parts, *used)
+        )(where, *extra, *q_parts, *used)
 
     far_steps = tuple(range(STEPS // 2, STEPS))
     near_steps = tuple(range(STEPS // 2))
     parts = {}
-    got = grads_call(far_steps, False, *stats, *others)
+    got = grads_call(far_steps, False, stats, others)
     for i, step in enumerate(far_steps):
         parts[step] = got[2 * i : 2 * i + 2]
     got = grads_call(near_steps, True, *got[2 * len(far_steps) :])

time: 73.8 us -> 61.2 us (0.83)
  the two profiles are of different devices: /device:TPU:0 before, /device:TPU:15 now
where the time goes in v2:
time: 61.2 us; the launch traced here: 61.1 us
  Pallas kernels  19.7 us (32%)
  waiting for transfers between devices  19.7 us (32%)
  starting transfers between devices  16.5 us (27%)
  local copies, waits for them, and re-layouts  2.35 us (4%)
  other arithmetic  1.95 us (3%)
  between operations  0.81 us (1%)
    pallas_call x2, Pallas kernels, grads_call(): pl.pallas_call(functools.partial(grads_kernel, sizes, scale, steps, last)...  11.9 us
    ppermute x16, waiting for transfers between devices, swap(): lax.ppermute(block, axis, [(i, i ^ bit) for i in range(lax.axis_size(axis...  11.1 us
    ppermute x16, starting transfers between devices, swap(): lax.ppermute(block, axis, [(i, i ^ bit) for i in range(lax.axis_size(axis...  10.7 us
    ppermute x5, waiting for transfers between devices, from_behind(): return lax.ppermute(block, axis, route)  8.66 us
    pallas_call x2, Pallas kernels, stats_call(): pl.pallas_call(functools.partial(stats_kernel, sizes, scale * LOG2E, whic...  6.98 us
    ppermute x5, starting transfers between devices, from_behind(): return lax.ppermute(block, axis, route)  5.82 us
    unnamed x6, local copies, waits for them, and re-layouts  1.6 us
  transfers between devices with their start and end apart: 21, of which 7 were waited for; matrix products, arithmetic and copies ran while one was open for 2% of the time, Pallas kernels for 17%

profile of v2, /device:TPU:15, one launch (start us, length us, event | category | flops | bytes accessed | tf_op | source)
XLA Modules:
  0.0 61.1 jit_solution(15104486081072871799)
XLA Ops:
  0.6 0.9 %pad_maximum_fusion.1 = bf16[2,2,128,128]{3,2,1,0:T(8,128)(2,1)S(1)} fusion(bf16[2,1,128,128]{3,2,1,0:T(8,128)(2,1)} %bitcast.67, bf16[2,1,128,128]{3,2,1,0:T(8,128)(2,1)} %bitcast.68), kind=kLoop, calls=%fused_computation.9 | loop fusion | flops 65536 | bytes 262144 | tf_op jit(solution)/shard_map/stack | solution.py:277
  1.6 1.3 %collective-permute-start.2 = (bf16[512,128]{1,0:T(8,128)(2,1)S(1)}, bf16[512,128]{1,0:T(8,128)(2,1)S(1)}, u32[]{:S(2)}, u32[]{:S(2)}) collective-permute-start(bf16[512,128]{1,0:T(8,128)(2,1)S(1)} %bitcast.28), channel_id=1, source_target_pairs={{6,0},{7,1},{0,2},{1,3},{2,4},{3,5},{4,6},{5,7},{14,8},{15,9},{8,1... | collective-permute-start | bytes 393224 | tf_op jit(solution)/shard_map/ppermute | solution.py:25
  2.9 1.0 %collective-permute-start.1 = (bf16[512,128]{1,0:T(8,128)(2,1)S(1)}, bf16[512,128]{1,0:T(8,128)(2,1)S(1)}, u32[]{:S(2)}, u32[]{:S(2)}) collective-permute-start(bf16[512,128]{1,0:T(8,128)(2,1)S(1)} %bitcast.29), channel_id=1, source_target_pairs={{0,8},{8,0},{16,24},{24,16},{1,9},{9,1},{17,25},{25,17},{2,10},{10... | collective-permute-start | bytes 393224 | tf_op jit(solution)/shard_map/ppermute | solution.py:29
  3.9 0.7 %copy-done.2 = s32[64]{0:T(128)S(1)} copy-done((s32[64]{0:T(128)S(1)}, s32[64]{0:T(128)}, u32[]{:S(2)}) %copy-start.2) | copy-done | bytes 280
  4.5 0.1 concatenate.7.where_ref
  4.6 0.0 copy-start.1
  4.6 0.9 %copy-done.1 = bf16[256,512]{1,0:T(8,128)(2,1)S(1)} copy-done((bf16[256,512]{1,0:T(8,128)(2,1)S(1)}, bf16[256,512]{1,0:T(8,128)(2,1)}, u32[]{:S(2)}) %copy-start.1) | copy-done | bytes 262168
  5.6 0.8 %pack.1 = (bf16[1024,128]{1,0:T(8,128)(2,1)S(1)}, bf16[1024,128]{1,0:T(8,128)(2,1)S(1)}) custom-call(s32[72]{0:T(128)S(1)} %concatenate.7.where_ref, bf16[256,512]{1,0:T(8,128)(2,1)S(1)} %copy-done, bf16[256,512]{1,0:T(8,128)(2,1)S(1)} %copy-done.1), custom_call_target="tpu_custom_call" | custom-call | tf_op jit(solution)/shard_map/pack/pallas_call | solution.py:281
  6.4 0.1 collective-permute-start
  6.5 0.0 collective-permute-done.2
  6.5 0.3 collective-permute-start.3
  6.8 2.3 %collective-permute-start.6 = (bf16[512,128]{1,0:T(8,128)(2,1)S(1)}, bf16[512,128]{1,0:T(8,128)(2,1)S(1)}, u32[]{:S(2)}, u32[]{:S(2)}) collective-permute-start(bf16[512,128]{1,0:T(8,128)(2,1)S(1)} %collective-permute-done.2), channel_id=1, source_target_pairs={{7,0},{0,1},{1,2},{2,3},{3,4},{4,5},{5,6},{6,7},{15,8},{8,9},{9,10... | collective-permute-start | bytes 393224 | tf_op jit(solution)/shard_map/ppermute | solution.py:25
  9.1 0.3 collective-permute-start.8
  9.3 0.0 collective-permute-done.1
  9.3 3.0 %collective-permute-start.9 = (bf16[1024,128]{1,0:T(8,128)(2,1)S(1)}, bf16[1024,128]{1,0:T(8,128)(2,1)S(1)}, u32[]{:S(2)}, u32[]{:S(2)}) collective-permute-start(bf16[1024,128]{1,0:T(8,128)(2,1)S(1)} %get-tuple-element.20), channel_id=1, source_target_pairs={{0,24},{8,16},{16,8},{24,0},{1,25},{9,17},{17,9},{25,1},{2,26},{10... | collective-permute-start | bytes 786440 | tf_op jit(solution)/shard_map/ppermute | solution.py:29
  12.3 0.0 collective-permute-done.3
  12.3 1.6 %collective-permute-start.5 = (bf16[512,128]{1,0:T(8,128)(2,1)S(1)}, bf16[512,128]{1,0:T(8,128)(2,1)S(1)}, u32[]{:S(2)}, u32[]{:S(2)}) collective-permute-start(bf16[512,128]{1,0:T(8,128)(2,1)S(1)} %collective-permute-done.2), channel_id=1, source_target_pairs={{0,8},{8,0},{16,24},{24,16},{1,9},{9,1},{17,25},{25,17},{2,10},{10... | collective-permute-start | bytes 393224 | tf_op jit(solution)/shard_map/ppermute | solution.py:29
  13.9 0.0 collective-permute-start.4
  13.9 1.4 %collective-permute-start.7 = (bf16[512,128]{1,0:T(8,128)(2,1)S(1)}, bf16[512,128]{1,0:T(8,128)(2,1)S(1)}, u32[]{:S(2)}, u32[]{:S(2)}) collective-permute-start(bf16[512,128]{1,0:T(8,128)(2,1)S(1)} %collective-permute-done.6), channel_id=1, source_target_pairs={{0,8},{8,0},{16,24},{24,16},{1,9},{9,1},{17,25},{25,17},{2,10},{10... | collective-permute-start | bytes 393224 | tf_op jit(solution)/shard_map/ppermute | solution.py:29
  15.3 0.0 collective-permute-done.5
  15.3 0.0 collective-permute-done.4
  15.3 1.0 %collective-permute-done.7 = bf16[512,128]{1,0:T(8,128)(2,1)S(1)} collective-permute-done((bf16[512,128]{1,0:T(8,128)(2,1)S(1)}, bf16[512,128]{1,0:T(8,128)(2,1)S(1)}, u32[]{:S(2)}, u32[]{:S(2)}) %collective-permute-start.7) | collective-permute-done | bytes 131104 | tf_op jit(solution)/shard_map/ppermute | solution.py:29
  16.3 3.0 %stats.2.rest_0_ = f32[3,8,256]{2,1,0:T(8,128)S(1)} custom-call(s32[72]{0:T(128)S(1)} %concatenate.7.where_ref, bf16[4,256,128]{2,1,0:T(8,128)(2,1)S(1)} %bitcast.36, bf16[4,256,128]{2,1,0:T(8,128)(2,1)S(1)} %bitcast.39, bf16[4,128,128]{2,1,0:T(8,128)(2,1)S(1)} %bitcast.30, bf16[4,128,128]{2,1,0:T(8,128)(2,1)S(1)} %bitcast.48, ...), custom_call_target="tpu_custom_call" | custom-call | flops 1073741824 | bytes 1048576 | tf_op jit(solution)/shard_map/stats/pallas_call | solution.py:305
  19.3 0.0 collective-permute-done.8
  19.3 3.4 %collective-permute-done.9 = bf16[1024,128]{1,0:T(8,128)(2,1)S(1)} collective-permute-done((bf16[1024,128]{1,0:T(8,128)(2,1)S(1)}, bf16[1024,128]{1,0:T(8,128)(2,1)S(1)}, u32[]{:S(2)}, u32[]{:S(2)}) %collective-permute-start.9) | collective-permute-done | bytes 262176 | tf_op jit(solution)/shard_map/ppermute | solution.py:29
  22.7 4.0 %stats.3.rest_0_ = f32[3,8,256]{2,1,0:T(8,128)S(1)} custom-call(s32[72]{0:T(128)S(1)} %concatenate.7.where_ref, f32[3,8,256]{2,1,0:T(8,128)S(1)} %stats.2.rest_0_, bf16[4,256,128]{2,1,0:T(8,128)(2,1)S(1)} %bitcast.42, bf16[4,256,128]{2,1,0:T(8,128)(2,1)S(1)} %bitcast.45, bf16[4,128,128]{2,1,0:T(8,128)(2,1)S(1)} %bitcast.31, ...), custom_call_target="tpu_custom_call" | custom-call | flops 1073741824 | bytes 1048576 | tf_op jit(solution)/shard_map/stats/pallas_call | solution.py:305
  26.7 0.1 collective-permute-start.10
  26.8 2.7 %collective-permute-done.10.rest_1_ = f32[3,8,256]{2,1,0:T(8,128)S(1)} collective-permute-done((f32[3,8,256]{2,1,0:T(8,128)S(1)}, f32[3,8,256]{2,1,0:T(8,128)S(1)}, u32[]{:S(2)}, u32[]{:S(2)}) %collective-permute-start.10) | collective-permute-done | bytes 24608 | tf_op jit(solution)/shard_map/ppermute | solution.py:29
  29.5 5.5 %grads.2 = (f32[512,128]{1,0:T(8,128)S(1)}, bf16[512,128]{1,0:T(8,128)(2,1)S(1)}, f32[512,128]{1,0:T(8,128)S(1)}, bf16[512,128]{1,0:T(8,128)(2,1)S(1)}, f32[8,12...) custom-call(s32[72]{0:T(128)S(1)} %concatenate.7.where_ref, f32[3,8,256]{2,1,0:T(8,128)S(1)} %stats.3.rest_0_, ...), custom_call_target="tpu_custom_call" | custom-call | flops 3221225472 | bytes 2097152 | tf_op jit(solution)/shard_map/grads/pallas_call | solution.py:341
  34.9 0.1 collective-permute-start.14
  35.0 0.5 collective-permute-start.16
  35.5 6.4 %grads.3 = (f32[512,128]{1,0:T(8,128)S(1)}, bf16[512,128]{1,0:T(8,128)(2,1)S(1)}, f32[512,128]{1,0:T(8,128)S(1)}, bf16[512,128]{1,0:T(8,128)(2,1)S(1)}, f32[256,...) custom-call(s32[72]{0:T(128)S(1)} %concatenate.7.where_ref, ...), custom_call_target="tpu_custom_call" | custom-call | flops 3221225472 | bytes 2097152 | tf_op jit(solution)/shard_map/grads/pallas_call | solution.py:341
  42.0 0.2 collective-permute-start.18
  42.1 0.4 collective-permute-start.20
  42.5 0.0 collective-permute-start.11
  42.5 0.1 collective-permute-start.12
  42.7 1.8 %collective-permute-start.13 = (bf16[256,256]{1,0:T(8,128)(2,1)S(1)}, bf16[256,256]{1,0:T(8,128)(2,1)S(1)}, u32[]{:S(2)}, u32[]{:S(2)}) collective-permute-start(bf16[256,256]{1,0:T(8,128)(2,1)S(1)} %get-tuple-element.26), channel_id=1, source_target_pairs={{0,24},{8,16},{16,8},{24,0},{1,25},{9,17},{17,9},{25,1},{2,26},{10... | collective-permute-start | bytes 393224 | tf_op jit(solution)/shard_map/ppermute | solution.py:29
  44.6 0.1 collective-permute-start.15
  44.7 2.8 %collective-permute-done.11 = bf16[256,256]{1,0:T(8,128)(2,1)S(1)} collective-permute-done((bf16[256,256]{1,0:T(8,128)(2,1)S(1)}, bf16[256,256]{1,0:T(8,128)(2,1)S(1)}, u32[]{:S(2)}, u32[]{:S(2)}) %collective-permute-start.11) | collective-permute-done | bytes 131104 | tf_op jit(solution)/shard_map/ppermute | solution.py:29
  47.5 1.2 %collective-permute-start.17 = (bf16[512,128]{1,0:T(8,128)(2,1)S(1)}, bf16[512,128]{1,0:T(8,128)(2,1)S(1)}, u32[]{:S(2)}, u32[]{:S(2)}) collective-permute-start(bf16[512,128]{1,0:T(8,128)(2,1)S(1)} %add_convert_fusion.2), channel_id=1, source_target_pairs={{2,0},{3,1},{4,2},{5,3},{6,4},{7,5},{0,6},{1,7},{10,8},{11,9},{12,... | collective-permute-start | bytes 393224 | tf_op jit(solution)/shard_map/ppermute | solution.py:25
  48.7 1.0 %collective-permute-start.19 = (bf16[512,128]{1,0:T(8,128)(2,1)S(1)}, bf16[512,128]{1,0:T(8,128)(2,1)S(1)}, u32[]{:S(2)}, u32[]{:S(2)}) collective-permute-start(bf16[512,128]{1,0:T(8,128)(2,1)S(1)} %add_convert_fusion.1), channel_id=1, source_target_pairs={{1,0},{2,1},{3,2},{4,3},{5,4},{6,5},{7,6},{0,7},{9,8},{10,9},{11,1... | collective-permute-start | bytes 393224 | tf_op jit(solution)/shard_map/ppermute | solution.py:25
  49.7 1.2 %collective-permute-done.13 = bf16[256,256]{1,0:T(8,128)(2,1)S(1)} collective-permute-done((bf16[256,256]{1,0:T(8,128)(2,1)S(1)}, bf16[256,256]{1,0:T(8,128)(2,1)S(1)}, u32[]{:S(2)}, u32[]{:S(2)}) %collective-permute-start.13) | collective-permute-done | bytes 131104 | tf_op jit(solution)/shard_map/ppermute | solution.py:29
  50.9 0.1 select_convert_fusion.1
  50.9 0.7 %pad_maximum_fusion = bf16[256,512]{1,0:T(8,128)(2,1)} fusion(bf16[256,256]{1,0:T(8,128)(2,1)S(1)} %get-tuple-element.36, bf16[256,256]{1,0:T(8,128)(2,1)S(1)} %get-tuple-element.35), kind=kLoop, calls=%fused_computation | loop fusion | flops 524288 | bytes 524288 | tf_op jit(solution)/shard_map/concatenate | solution.py:384
  51.7 0.1 collective-permute-done.17
  51.8 8.5 %collective-permute-done.19 = bf16[512,128]{1,0:T(8,128)(2,1)S(1)} collective-permute-done((bf16[512,128]{1,0:T(8,128)(2,1)S(1)}, bf16[512,128]{1,0:T(8,128)(2,1)S(1)}, u32[]{:S(2)}, u32[]{:S(2)}) %collective-permute-start.19) | collective-permute-done | bytes 131104 | tf_op jit(solution)/shard_map/ppermute | solution.py:25
  60.3 0.1 add_convert_fusion
  60.4 0.7 %fusion = (bf16[2,1,128,128]{3,2,1,0:T(8,128)(2,1)}, bf16[2,1,128,128]{3,2,1,0:T(8,128)(2,1)}) fusion(bf16[2,2,128,128]{3,2,1,0:T(8,128)(2,1)S(1)} %bitcast.66), kind=kLoop, calls=%fused_computation.11 | loop fusion | bytes 262144 | tf_op jit(solution)/shard_map/slice | solution.py:391
  (15 shorter events, 0.2 us)
Async XLA Ops:
  0.6 4.0 %copy-start = (bf16[256,512]{1,0:T(8,128)(2,1)S(1)}, bf16[256,512]{1,0:T(8,128)(2,1)}, u32[]{:S(2)}) copy-start(bf16[256,512]{1,0:T(8,128)(2,1)} %q_ref.1) | copy-start | bytes 786436
  1.6 4.9 %collective-permute-start.2 = (bf16[512,128]{1,0:T(8,128)(2,1)S(1)}, bf16[512,128]{1,0:T(8,128)(2,1)S(1)}, u32[]{:S(2)}, u32[]{:S(2)}) collective-permute-start(bf16[512,128]{1,0:T(8,128)(2,1)S(1)} %bitcast.28), channel_id=1, source_target_pairs={{6,0},{7,1},{0,2},{1,3},{2,4},{3,5},{4,6},{5,7},{14,8},{15,9},{8,1... | collective-permute-start | bytes 393224 | tf_op jit(solution)/shard_map/ppermute | solution.py:25
  2.9 6.4 %collective-permute-start.1 = (bf16[512,128]{1,0:T(8,128)(2,1)S(1)}, bf16[512,128]{1,0:T(8,128)(2,1)S(1)}, u32[]{:S(2)}, u32[]{:S(2)}) collective-permute-start(bf16[512,128]{1,0:T(8,128)(2,1)S(1)} %bitcast.29), channel_id=1, source_target_pairs={{0,8},{8,0},{16,24},{24,16},{1,9},{9,1},{17,25},{25,17},{2,10},{10... | collective-permute-start | bytes 393224 | tf_op jit(solution)/shard_map/ppermute | solution.py:29
  3.9 0.7 %copy-start.2 = (s32[64]{0:T(128)S(1)}, s32[64]{0:T(128)}, u32[]{:S(2)}) copy-start(s32[64]{0:T(128)} %param.9) | copy-start | bytes 772
  4.6 1.0 %copy-start.1 = (bf16[256,512]{1,0:T(8,128)(2,1)S(1)}, bf16[256,512]{1,0:T(8,128)(2,1)}, u32[]{:S(2)}) copy-start(bf16[256,512]{1,0:T(8,128)(2,1)} %g_ref.1) | copy-start | bytes 786436
  6.4 7.5 %collective-permute-start = (bf16[1024,128]{1,0:T(8,128)(2,1)S(1)}, bf16[1024,128]{1,0:T(8,128)(2,1)S(1)}, u32[]{:S(2)}, u32[]{:S(2)}) collective-permute-start(bf16[1024,128]{1,0:T(8,128)(2,1)S(1)} %get-tuple-element.20), channel_id=1, source_target_pairs={{0,8},{8,0},{16,24},{24,16},{1,9},{9,1},{17,25},{25,17},{2,10},{10... | collective-permute-start | bytes 786440 | tf_op jit(solution)/shard_map/ppermute | solution.py:29
  6.5 5.8 %collective-permute-start.3 = (bf16[512,128]{1,0:T(8,128)(2,1)S(1)}, bf16[512,128]{1,0:T(8,128)(2,1)S(1)}, u32[]{:S(2)}, u32[]{:S(2)}) collective-permute-start(bf16[512,128]{1,0:T(8,128)(2,1)S(1)} %broadcast_select_fusion), channel_id=1, source_target_pairs={{0,1},{1,0},{2,3},{3,2},{4,5},{5,4},{6,7},{7,6},{8,9},{9,8},{10,11... | collective-permute-start | bytes 393224 | tf_op jit(solution)/shard_map/ppermute | solution.py:29
  6.8 7.1 %collective-permute-start.6 = (bf16[512,128]{1,0:T(8,128)(2,1)S(1)}, bf16[512,128]{1,0:T(8,128)(2,1)S(1)}, u32[]{:S(2)}, u32[]{:S(2)}) collective-permute-start(bf16[512,128]{1,0:T(8,128)(2,1)S(1)} %collective-permute-done.2), channel_id=1, source_target_pairs={{7,0},{0,1},{1,2},{2,3},{3,4},{4,5},{5,6},{6,7},{15,8},{8,9},{9,10... | collective-permute-start | bytes 393224 | tf_op jit(solution)/shard_map/ppermute | solution.py:25
  9.1 10.2 %collective-permute-start.8 = (bf16[1024,128]{1,0:T(8,128)(2,1)S(1)}, bf16[1024,128]{1,0:T(8,128)(2,1)S(1)}, u32[]{:S(2)}, u32[]{:S(2)}) collective-permute-start(bf16[1024,128]{1,0:T(8,128)(2,1)S(1)} %get-tuple-element.19), channel_id=1, source_target_pairs={{0,16},{8,24},{16,0},{24,8},{1,17},{9,25},{17,1},{25,9},{2,18},{10... | collective-permute-start | bytes 786440 | tf_op jit(solution)/shard_map/ppermute | solution.py:29
  9.3 13.4 %collective-permute-start.9 = (bf16[1024,128]{1,0:T(8,128)(2,1)S(1)}, bf16[1024,128]{1,0:T(8,128)(2,1)S(1)}, u32[]{:S(2)}, u32[]{:S(2)}) collective-permute-start(bf16[1024,128]{1,0:T(8,128)(2,1)S(1)} %get-tuple-element.20), channel_id=1, source_target_pairs={{0,24},{8,16},{16,8},{24,0},{1,25},{9,17},{17,9},{25,1},{2,26},{10... | collective-permute-start | bytes 786440 | tf_op jit(solution)/shard_map/ppermute | solution.py:29
  12.3 3.0 %collective-permute-start.5 = (bf16[512,128]{1,0:T(8,128)(2,1)S(1)}, bf16[512,128]{1,0:T(8,128)(2,1)S(1)}, u32[]{:S(2)}, u32[]{:S(2)}) collective-permute-start(bf16[512,128]{1,0:T(8,128)(2,1)S(1)} %collective-permute-done.2), channel_id=1, source_target_pairs={{0,8},{8,0},{16,24},{24,16},{1,9},{9,1},{17,25},{25,17},{2,10},{10... | collective-permute-start | bytes 393224 | tf_op jit(solution)/shard_map/ppermute | solution.py:29
  13.9 1.4 %collective-permute-start.4 = (bf16[512,128]{1,0:T(8,128)(2,1)S(1)}, bf16[512,128]{1,0:T(8,128)(2,1)S(1)}, u32[]{:S(2)}, u32[]{:S(2)}) collective-permute-start(bf16[512,128]{1,0:T(8,128)(2,1)S(1)} %collective-permute-done.3), channel_id=1, source_target_pairs={{0,8},{8,0},{16,24},{24,16},{1,9},{9,1},{17,25},{25,17},{2,10},{10... | collective-permute-start | bytes 393224 | tf_op jit(solution)/shard_map/ppermute | solution.py:29
  13.9 2.4 %collective-permute-start.7 = (bf16[512,128]{1,0:T(8,128)(2,1)S(1)}, bf16[512,128]{1,0:T(8,128)(2,1)S(1)}, u32[]{:S(2)}, u32[]{:S(2)}) collective-permute-start(bf16[512,128]{1,0:T(8,128)(2,1)S(1)} %collective-permute-done.6), channel_id=1, source_target_pairs={{0,8},{8,0},{16,24},{24,16},{1,9},{9,1},{17,25},{25,17},{2,10},{10... | collective-permute-start | bytes 393224 | tf_op jit(solution)/shard_map/ppermute | solution.py:29
  26.7 2.7 %collective-permute-start.10 = (f32[3,8,256]{2,1,0:T(8,128)S(1)}, f32[3,8,256]{2,1,0:T(8,128)S(1)}, u32[]{:S(2)}, u32[]{:S(2)}) collective-permute-start(f32[3,8,256]{2,1,0:T(8,128)S(1)} %stats.3.rest_0_), channel_id=1, source_target_pairs={{0,16},{8,24},{16,0},{24,8},{1,17},{9,25},{17,1},{25,9},{2,18},{10... | collective-permute-start | bytes 73736 | tf_op jit(solution)/shard_map/ppermute | solution.py:29
  34.9 7.6 %collective-permute-start.14 = (bf16[512,128]{1,0:T(8,128)(2,1)S(1)}, bf16[512,128]{1,0:T(8,128)(2,1)S(1)}, u32[]{:S(2)}, u32[]{:S(2)}) collective-permute-start(bf16[512,128]{1,0:T(8,128)(2,1)S(1)} %get-tuple-element.28), channel_id=1, source_target_pairs={{0,8},{8,0},{16,24},{24,16},{1,9},{9,1},{17,25},{25,17},{2,10},{10... | collective-permute-start | bytes 393224 | tf_op jit(solution)/shard_map/ppermute | solution.py:29
  35.0 7.7 %collective-permute-start.16 = (bf16[512,128]{1,0:T(8,128)(2,1)S(1)}, bf16[512,128]{1,0:T(8,128)(2,1)S(1)}, u32[]{:S(2)}, u32[]{:S(2)}) collective-permute-start(bf16[512,128]{1,0:T(8,128)(2,1)S(1)} %get-tuple-element.30), channel_id=1, source_target_pairs={{0,8},{8,0},{16,24},{24,16},{1,9},{9,1},{17,25},{25,17},{2,10},{10... | collective-permute-start | bytes 393224 | tf_op jit(solution)/shard_map/ppermute | solution.py:29
  42.0 2.6 %collective-permute-start.18 = (bf16[512,128]{1,0:T(8,128)(2,1)S(1)}, bf16[512,128]{1,0:T(8,128)(2,1)S(1)}, u32[]{:S(2)}, u32[]{:S(2)}) collective-permute-start(bf16[512,128]{1,0:T(8,128)(2,1)S(1)} %get-tuple-element.32), channel_id=1, source_target_pairs={{0,8},{8,0},{16,24},{24,16},{1,9},{9,1},{17,25},{25,17},{2,10},{10... | collective-permute-start | bytes 393224 | tf_op jit(solution)/shard_map/ppermute | solution.py:29
  42.1 9.5 %collective-permute-start.20 = (bf16[512,128]{1,0:T(8,128)(2,1)S(1)}, bf16[512,128]{1,0:T(8,128)(2,1)S(1)}, u32[]{:S(2)}, u32[]{:S(2)}) collective-permute-start(bf16[512,128]{1,0:T(8,128)(2,1)S(1)} %get-tuple-element.34), channel_id=1, source_target_pairs={{0,8},{8,0},{16,24},{24,16},{1,9},{9,1},{17,25},{25,17},{2,10},{10... | collective-permute-start | bytes 393224 | tf_op jit(solution)/shard_map/ppermute | solution.py:29
  42.5 5.0 %collective-permute-start.11 = (bf16[256,256]{1,0:T(8,128)(2,1)S(1)}, bf16[256,256]{1,0:T(8,128)(2,1)S(1)}, u32[]{:S(2)}, u32[]{:S(2)}) collective-permute-start(bf16[256,256]{1,0:T(8,128)(2,1)S(1)} %get-tuple-element.24), channel_id=1, source_target_pairs={{0,16},{8,24},{16,0},{24,8},{1,17},{9,25},{17,1},{25,9},{2,18},{10... | collective-permute-start | bytes 393224 | tf_op jit(solution)/shard_map/ppermute | solution.py:29
  42.5 6.1 %collective-permute-start.12 = (bf16[256,256]{1,0:T(8,128)(2,1)S(1)}, bf16[256,256]{1,0:T(8,128)(2,1)S(1)}, u32[]{:S(2)}, u32[]{:S(2)}) collective-permute-start(bf16[256,256]{1,0:T(8,128)(2,1)S(1)} %get-tuple-element.25), channel_id=1, source_target_pairs={{0,8},{8,0},{16,24},{24,16},{1,9},{9,1},{17,25},{25,17},{2,10},{10... | collective-permute-start | bytes 393224 | tf_op jit(solution)/shard_map/ppermute | solution.py:29
  42.7 8.2 %collective-permute-start.13 = (bf16[256,256]{1,0:T(8,128)(2,1)S(1)}, bf16[256,256]{1,0:T(8,128)(2,1)S(1)}, u32[]{:S(2)}, u32[]{:S(2)}) collective-permute-start(bf16[256,256]{1,0:T(8,128)(2,1)S(1)} %get-tuple-element.26), channel_id=1, source_target_pairs={{0,24},{8,16},{16,8},{24,0},{1,25},{9,17},{17,9},{25,1},{2,26},{10... | collective-permute-start | bytes 393224 | tf_op jit(solution)/shard_map/ppermute | solution.py:29
  44.6 7.1 %collective-permute-start.15 = (bf16[512,128]{1,0:T(8,128)(2,1)S(1)}, bf16[512,128]{1,0:T(8,128)(2,1)S(1)}, u32[]{:S(2)}, u32[]{:S(2)}) collective-permute-start(bf16[512,128]{1,0:T(8,128)(2,1)S(1)} %add_convert_fusion.3), channel_id=1, source_target_pairs={{3,0},{4,1},{5,2},{6,3},{7,4},{0,5},{1,6},{2,7},{11,8},{12,9},{13,... | collective-permute-start | bytes 393224 | tf_op jit(solution)/shard_map/ppermute | solution.py:25
  47.5 4.3 %collective-permute-start.17 = (bf16[512,128]{1,0:T(8,128)(2,1)S(1)}, bf16[512,128]{1,0:T(8,128)(2,1)S(1)}, u32[]{:S(2)}, u32[]{:S(2)}) collective-permute-start(bf16[512,128]{1,0:T(8,128)(2,1)S(1)} %add_convert_fusion.2), channel_id=1, source_target_pairs={{2,0},{3,1},{4,2},{5,3},{6,4},{7,5},{0,6},{1,7},{10,8},{11,9},{12,... | collective-permute-start | bytes 393224 | tf_op jit(solution)/shard_map/ppermute | solution.py:25
  48.7 11.6 %collective-permute-start.19 = (bf16[512,128]{1,0:T(8,128)(2,1)S(1)}, bf16[512,128]{1,0:T(8,128)(2,1)S(1)}, u32[]{:S(2)}, u32[]{:S(2)}) collective-permute-start(bf16[512,128]{1,0:T(8,128)(2,1)S(1)} %add_convert_fusion.1), channel_id=1, source_target_pairs={{1,0},{2,1},{3,2},{4,3},{5,4},{6,5},{7,6},{0,7},{9,8},{10,9},{11,1... | collective-permute-start | bytes 393224 | tf_op jit(solution)/shard_map/ppermute | solution.py:25

commit v3 on v2

--- a/solution.py
+++ b/solution.py
@@ -38,16 +38,17 @@
     bias_ref[2] = jnp.full((size, size), NEG, jnp.float32)
 
 
-def build_list(sizes, queries, blocks, where_ref, list_ref):
+def build_list(sizes, plan, where_ref, list_ref):
     outer_size, key_blocks = sizes
     outer = where_ref[4]
     key_place = {}
-    for block in blocks:
+    for block in sorted({block for _, blocks in plan for block in blocks}):
         step, core, half = block // 4, (block // 2) % 2, block % 2
         source = lax.rem(outer - step + outer_size, outer_size)
         key_place[block] = where_ref[8 + (where_ref[core] * outer_size + source) * 2 + half]
     position = jnp.int32(0)
-    for query in queries:
+    pad = (plan[0][0] * key_blocks + plan[0][1][0]) * 4 + 2
+    for query, blocks in plan:
         query_place = where_ref[8 + (where_ref[query // 2] * outer_size + outer) * 2 + query % 2]
         for block in blocks:
             kind = jnp.where(key_place[block] == query_place, 1, 0)
@@ -56,8 +57,12 @@
         list_ref[position] = (query * key_blocks + blocks[0]) * 4 + 2
         position = position + lax.rem(position, 2)
     for extra in range(10):
-        list_ref[position + extra] = (queries[0] * key_blocks + blocks[0]) * 4 + 2
+        list_ref[position + extra] = pad
     return (position + 6) // 8
+
+
+def blocks_of(steps):
+    return [4 * step + i for step in steps for i in range(4)]
 
 
 def entry_of(list_ref, index, key_blocks):
@@ -103,53 +108,40 @@
         use(4 * i + 3, 3)
 
 
-def pack_kernel(size, where_ref, q_ref, g_ref, mine, theirs, sems):
-    half_len = q_ref.shape[0] // 2
-    pairs = q_ref.shape[1] // size // 2
-    near = lax.rem(where_ref[0], 2)
-    copies = []
-
-    def put(src, dst):
-        copies.append(pltpu.make_async_copy(src, dst, sems.at[len(copies)]))
-
-    for half in range(2):
-        rows = pl.ds(half * half_len, half_len)
-        for dst, core in ((mine, near), (theirs, 1 - near)):
-            for which, src in enumerate((q_ref, g_ref)):
-                for head in range(pairs):
-                    row = ((half * 2 + which) * pairs + head) * half_len
-                    lane = pl.multiple_of((core * pairs + head) * size, size)
-                    put(src.at[rows, pl.ds(lane, size)], dst.at[pl.ds(row, half_len), :])
-    for copy in copies:
-        copy.start()
-    for copy in copies:
-        copy.wait()
-
-
-def stats_kernel(sizes, factor, which, shards, where_ref, *rest):
+def stats_kernel(sizes, factor, steps, merged, where_ref, *rest):
     outer_size, key_blocks, _, width = sizes
-    merged = which[0] > 0
     if merged:
         early, rest = rest[0], rest[1:]
-    q_refs, kv_refs = rest[: len(which)], rest[len(which) : len(which) + shards]
-    out_ref, qg, kv, bias, *tiles, state, lists = rest[len(which) + shards :]
+    count = 8 if merged else 4
+    held = list(range(STEPS)) if merged else list(steps)
+    q_refs, kv_refs = rest[: count // 2], rest[count // 2 : count // 2 + 2 * len(held)]
+    out_ref, qg, kv, bias, *tiles, state, lists = rest[count // 2 + 2 * len(held) :]
     stack_refs(kv_refs, kv)
     stack_refs(q_refs, qg)
-    here = [2 * t + half for t in which for half in range(2)]
-    first = here[0]
-    trips = build_list(
-        (outer_size, key_blocks), here, range(key_blocks), where_ref, lists
-    )
+    plan = [
+        (query, blocks_of(held if query >= 4 else steps))
+        for query in (list(range(4, 8)) if merged else []) + list(range(4))
+    ]
+    trips = build_list((outer_size, key_blocks), plan, where_ref, lists)
     fill_bias(bias)
-    count = len(here)
     state[0] = jnp.full((count, 8, width), NEG, jnp.float32)
     state[1] = jnp.zeros((count, 8, width), jnp.float32)
     state[2] = jnp.zeros((count, 8, width), jnp.float32)
+    if merged:
+        for i in range(4):
+            at = pl.ds(i, 1)
+            state[0, i] = jnp.broadcast_to(early[0, at], (8, width))
+            state[1, i, 0:1] = early[1, at]
+            state[2, i, 0:1] = early[2, at]
+    gap = held[1] - held[0]
     slots = [tiles[3 * i : 3 * i + 3] for i in range(4)]
+
+    def slot_of(block):
+        return block if gap == 1 else (block // 4 // gap) * 4 + block % 4
 
     def entry(n):
         query, j0, b0, j1, b1 = entry_of(lists, n, key_blocks)
-        return query - first, j0, b0, j1, b1
+        return query, slot_of(j0), b0, slot_of(j1), b1
 
     def load(n, slot):
         score_tiles(entry(n), factor, qg, kv, bias, *slots[slot])
@@ -167,13 +159,11 @@
 
     pair_loop(trips, load, use)
     for i in range(count):
-        at = pl.ds(first + i if merged else i, 1)
+        at = pl.ds(i, 1)
         out_ref[0, at] = state[0, i, 0:1]
         out_ref[1, at] = jnp.sum(state[1, i], axis=0, keepdims=True)
         out_ref[2, at] = jnp.sum(state[2, i], axis=0, keepdims=True)
-    if merged:
-        out_ref[:, pl.ds(0, first)] = early[:, pl.ds(0, first)]
-    else:
+    if not merged:
         out_ref[:, pl.ds(count, count)] = jnp.zeros((3, count, width), jnp.float32)
 
 
@@ -183,17 +173,18 @@
     carry_in, rest = rest[:2], rest[2:]
     q_refs, kv_refs = rest[:4], rest[4 : 4 + 2 * len(steps)]
     rest = rest[4 + 2 * len(steps) :]
-    outs, rest = rest[: 2 * len(steps)], rest[2 * len(steps) :]
-    tops, rest = rest[: (4 if last else 2)], rest[(4 if last else 2) :]
+    outs, sent, rest = rest[: len(steps)], rest[len(steps)], rest[len(steps) + 1 :]
+    tops, rest = rest[: (3 if last else 2)], rest[(3 if last else 2) :]
     qg, kv, kt, dk, dv, dq, base, bias, *tiles, lists = rest
     low = 4 * min(steps)
-    blocks = [4 * step + i for step in sorted(steps) for i in range(4)]
+    blocks = blocks_of(steps)
     stack_refs(kv_refs, kv)
     stack_refs(q_refs, qg)
     if last:
         dq[...] = carry_in[0][...]
         base[...] = carry_in[1][...]
-    trips = build_list((outer_size, key_blocks), range(8), blocks, where_ref, lists)
+    plan = [(query, blocks) for query in range(8)]
+    trips = build_list((outer_size, key_blocks), plan, where_ref, lists)
     fill_bias(bias)
     if not last:
         for query in range(8):
@@ -239,15 +230,17 @@
     for i in range(len(steps)):
         for half in range(2):
             for core in range(2):
-                dst = outs[2 * i + core]
+                dst, row = (sent, 4 * i * size) if core else (outs[i], 0)
+                row += 2 * half * size
                 block = i * 4 + core * 2 + half
-                dst[pl.ds(2 * half * size, size), :] = (dk[block] * scale).astype(dst.dtype)
-                dst[pl.ds((2 * half + 1) * size, size), :] = dv[block].astype(dst.dtype)
+                dst[pl.ds(row, size), :] = (dk[block] * scale).astype(dst.dtype)
+                dst[pl.ds(row + size, size), :] = dv[block].astype(dst.dtype)
     if last:
         for query in range(8):
-            dst = tops[query // 2]
+            t, half = query // 2, query % 2
+            dst, row = (sent, 4 * len(steps) * size) if t == 1 else (tops[max(t - 1, 0)], 0)
             for head in range(pairs):
-                dst[pl.ds((query % 2) * size, size), pl.ds(head * size, size)] = (
+                dst[pl.ds(row + (head * 2 + half) * size, size), :] = (
                     dq[query, :, pl.ds(head * size, size)].T * scale
                 ).astype(dst.dtype)
     else:
@@ -278,15 +271,17 @@
         [keys.reshape(2, block_len, size), values.reshape(2, block_len, size)], axis=1
     ).reshape(kv_shape)
     own2 = from_behind(kv, "outer", 2)
-    mine, theirs = pl.pallas_call(
-        functools.partial(pack_kernel, size),
-        name="pack",
-        out_shape=[jax.ShapeDtypeStruct(q_shape, low)] * 2,
-        in_specs=[smem] + [pl.BlockSpec(memory_space=pltpu.HBM)] * 2,
-        out_specs=[vmem] * 2,
-        scratch_shapes=[pltpu.SemaphoreType.DMA((8 * pairs,))],
-        compiler_params=params,
-    )(where, queries, out_grad)
+    near_core = inner % 2
+
+    def heads_of(array, core):
+        split = array.reshape(2, block_len, 2, pairs, size)
+        return lax.dynamic_index_in_dim(split, core, 2, False).transpose(0, 2, 1, 3)
+
+    def packed(core):
+        both = [heads_of(queries, core), heads_of(out_grad, core)]
+        return jnp.stack(both, axis=1).reshape(q_shape)
+
+    mine, theirs = packed(near_core), packed(1 - near_core)
     asked = [mine, swap(theirs, "inner", 1), swap(mine, "inner", 2), swap(theirs, "inner", 3)]
     own1 = swap(jnp.where(outer % 2 == 1, own2, kv), "outer", 1)
     own3 = from_behind(own2, "outer", 1)
@@ -300,17 +295,20 @@
     tile = pltpu.VMEM((2 * block_len, width), full)
     bias_table = pltpu.VMEM((3, block_len, block_len), full)
 
-    def stats_call(which, *early):
-        count = 2 * len(which)
+    def stats_call(steps, *early):
+        merged = len(early) > 0
+        count = 8 if merged else 4
+        held = range(STEPS) if merged else steps
+        used = [part for step in held for part in shards[2 * step : 2 * step + 2]]
         return pl.pallas_call(
-            functools.partial(stats_kernel, sizes, scale * LOG2E, which, len(shards)),
+            functools.partial(stats_kernel, sizes, scale * LOG2E, steps, merged),
             name="stats",
             out_shape=jax.ShapeDtypeStruct((3, 8, width), full),
-            in_specs=[smem] + [vmem] * (len(early) + len(which) + len(shards)),
+            in_specs=[smem] + [vmem] * (len(early) + count // 2 + len(used)),
             out_specs=vmem,
             scratch_shapes=[
                 pltpu.VMEM((2 * count, width, size), low),
-                pltpu.VMEM((2 * key_blocks, block_len, size), low),
+                pltpu.VMEM((4 * len(used), block_len, size), low),
                 bias_table,
                 *[tile, tile, pltpu.VMEM((8, width), full)] * 4,
                 pltpu.VMEM((3, count, 8, width), full),
@@ -318,20 +316,22 @@
             ],
             compiler_params=params,
             cost_estimate=pl.CostEstimate(
-                flops=flops // 2, bytes_accessed=1 << 20, transcendentals=0
+                flops=flops * 3 // 4 if merged else flops // 4, bytes_accessed=1 << 20, transcendentals=0
             ),
-        )(where, *early, *[q_parts[t] for t in which], *shards)
-
-    early = stats_call((0, 1))
-    stats = stats_call((2, 3), early)
+        )(where, *early, *q_parts[: count // 2], *used)
+
+    early = stats_call((0, 2))
+    stats = stats_call((1, 3), early)
     others = swap(stats, "inner", 2)
     shard_f32 = jax.ShapeDtypeStruct(kv_shape, full)
-    shard_low = jax.ShapeDtypeStruct(kv_shape, low)
+    rows = kv_shape[0]
 
     def grads_call(steps, last, *extra):
         n = len(steps)
         if last:
-            tops = [jax.ShapeDtypeStruct((row_count, width), full if t == 0 else low) for t in range(4)]
+            tops = [
+                jax.ShapeDtypeStruct((pairs * row_count, size), kind) for kind in (full, low, low)
+            ]
         else:
             tops = [
                 jax.ShapeDtypeStruct((8, size, width), full),
@@ -341,9 +341,11 @@
         return pl.pallas_call(
             functools.partial(grads_kernel, sizes, scale, steps, last),
             name="grads",
-            out_shape=[shard_f32, shard_low] * n + tops,
+            out_shape=[shard_f32] * n
+            + [jax.ShapeDtypeStruct((n * rows + (pairs * row_count if last else 0), size), low)]
+            + tops,
             in_specs=[smem] + [vmem] * (len(extra) + 4 + 2 * n),
-            out_specs=[vmem] * (2 * n + len(tops)),
+            out_specs=[vmem] * (n + 1 + len(tops)),
             scratch_shapes=[
                 pltpu.VMEM((16, width, size), low),
                 pltpu.VMEM((8 * n, block_len, size), low),
@@ -364,26 +366,29 @@
 
     far_steps = tuple(range(STEPS // 2, STEPS))
     near_steps = tuple(range(STEPS // 2))
-    parts = {}
-    got = grads_call(far_steps, False, stats, others)
-    for i, step in enumerate(far_steps):
-        parts[step] = got[2 * i : 2 * i + 2]
-    got = grads_call(near_steps, True, *got[2 * len(far_steps) :])
-    for i, step in enumerate(near_steps):
-        parts[step] = got[2 * i : 2 * i + 2]
-    tops = got[2 * len(near_steps) :]
+    *far_own, sent, dq_carry, base = grads_call(far_steps, False, stats, others)
+    far_got = swap(sent, "inner", 1)
+    *near_own, sent, dq0, dq2, dq3 = grads_call(near_steps, True, dq_carry, base)
+    near_got = swap(sent, "inner", 1)
     back = []
-    for step in reversed(range(STEPS)):
-        whole = parts[step][0] + swap(parts[step][1], "inner", 1).astype(full)
-        if step > 0:
-            whole = from_behind(whole.astype(low), "outer", -step)
-        back.append(whole.astype(full))
-    heads_mine = tops[0] + swap(tops[2], "inner", 2).astype(full)
-    heads_other = swap(tops[1], "inner", 1).astype(full) + swap(tops[3], "inner", 3).astype(full)
-    first = inner % 2 == 0
+    for steps, parts, got in ((far_steps, far_own, far_got), (near_steps, near_own, near_got)):
+        for i, step in enumerate(steps):
+            whole = parts[i] + got[i * rows : (i + 1) * rows].astype(full)
+            if step > 0:
+                whole = from_behind(whole.astype(low), "outer", -step)
+            back.append(whole.astype(full))
+    heads_mine = dq0 + swap(dq2, "inner", 2).astype(full)
+    heads_other = near_got[len(near_steps) * rows :].astype(full) + swap(dq3, "inner", 3).astype(full)
+    first = near_core == 0
     dq = jnp.concatenate(
-        [jnp.where(first, heads_mine, heads_other), jnp.where(first, heads_other, heads_mine)], axis=1
-    )
+        [
+            part.reshape(pairs, row_count, size)[head]
+            for part in (jnp.where(first, heads_mine, heads_other), jnp.where(first, heads_other, heads_mine))
+            for head in range(pairs)
+        ],
+        axis=1,
+    )
+    back.reverse()
     total = sum(back[1:], back[0]).astype(low).reshape(2, 2, block_len, size)
     return (
         dq.astype(low),

time: 61.2 us -> 62.8 us (1.026)
  starting transfers between devices: 16.5 us -> 20.2 us
  waiting for transfers between devices: 19.7 us -> 16.9 us
    ppermute x16 -> x13, waiting for transfers between devices: 11.1 us -> 4.4 us  [swap(): lax.ppermute(block, axis, [(i, i ^ bit) for i in range(lax.axis_size(axis...]
    ppermute x5, waiting for transfers between devices: 8.66 us -> 12.5 us  [from_behind(): return lax.ppermute(block, axis, route)]
    ppermute x5, starting transfers between devices: 5.82 us -> 9.47 us  [from_behind(): return lax.ppermute(block, axis, route)]
    ppermute x16 -> x13, starting transfers between devices: 10.7 us -> 10.7 us  [swap(): lax.ppermute(block, axis, [(i, i ^ bit) for i in range(lax.axis_size(axis...]
    pallas_call x3 -> x2, Pallas kernels: 7.8 us -> 7.79 us  [stats_call(): pl.pallas_call(functools.partial(stats_kernel, sizes, scale * LOG2E, step...]
  transfers between devices with their start and end apart: 21 -> 18, of which waited for: 7 -> 8; matrix products, arithmetic and copies ran while one was open for 2% -> 1% of each run, Pallas kernels for 17% -> 15%
where the time goes in v3:
time: 62.8 us; the launch traced here: 62.6 us
  starting transfers between devices  20.2 us (32%)
  Pallas kernels  19.7 us (31%)
  waiting for transfers between devices  16.9 us (27%)
  local copies, waits for them, and re-layouts  2.92 us (5%)
  other arithmetic  1.99 us (3%)
  between operations  0.84 us (1%)
    ppermute x5, waiting for transfers between devices, from_behind(): return lax.ppermute(block, axis, route)  12.5 us
    pallas_call x2, Pallas kernels, grads_call(): pl.pallas_call(functools.partial(grads_kernel, sizes, scale, steps, last)...  11.9 us
    ppermute x13, starting transfers between devices, swap(): lax.ppermute(block, axis, [(i, i ^ bit) for i in range(lax.axis_size(axis...  10.7 us
    ppermute x5, starting transfers between devices, from_behind(): return lax.ppermute(block, axis, route)  9.47 us
    pallas_call x2, Pallas kernels, stats_call(): pl.pallas_call(functools.partial(stats_kernel, sizes, scale * LOG2E, step...  7.79 us
    ppermute x13, waiting for transfers between devices, swap(): lax.ppermute(block, axis, [(i, i ^ bit) for i in range(lax.axis_size(axis...  4.4 us
    unnamed x6, local copies, waits for them, and re-layouts  1.54 us
  transfers between devices with their start and end apart: 18, of which 8 were waited for; matrix products, arithmetic and copies ran while one was open for 1% of the time, Pallas kernels for 15%

profile of v3, /device:TPU:15, one launch (start us, length us, event | category | flops | bytes accessed | tf_op | source)
XLA Modules:
  0.0 62.6 jit_solution(13840005170612387202)
XLA Ops:
  0.6 0.9 %pad_maximum_fusion.3 = bf16[2,2,128,128]{3,2,1,0:T(8,128)(2,1)S(1)} fusion(bf16[2,1,128,128]{3,2,1,0:T(8,128)(2,1)} %bitcast.102, bf16[2,1,128,128]{3,2,1,0:T(8,128)(2,1)} %bitcast.103), kind=kLoop, calls=%fused_computation.11 | loop fusion | flops 65536 | bytes 262144 | tf_op jit(solution)/shard_map/stack | solution.py:270
  1.6 1.3 %collective-permute-start.2 = (bf16[512,128]{1,0:T(8,128)(2,1)S(1)}, bf16[512,128]{1,0:T(8,128)(2,1)S(1)}, u32[]{:S(2)}, u32[]{:S(2)}) collective-permute-start(bf16[512,128]{1,0:T(8,128)(2,1)S(1)} %bitcast.58), channel_id=1, source_target_pairs={{6,0},{7,1},{0,2},{1,3},{2,4},{3,5},{4,6},{5,7},{14,8},{15,9},{8,1... | collective-permute-start | bytes 393224 | tf_op jit(solution)/shard_map/ppermute | solution.py:25
  2.9 1.0 %collective-permute-start.1 = (bf16[512,128]{1,0:T(8,128)(2,1)S(1)}, bf16[512,128]{1,0:T(8,128)(2,1)S(1)}, u32[]{:S(2)}, u32[]{:S(2)}) collective-permute-start(bf16[512,128]{1,0:T(8,128)(2,1)S(1)} %bitcast.59), channel_id=1, source_target_pairs={{0,8},{8,0},{16,24},{24,16},{1,9},{9,1},{17,25},{25,17},{2,10},{10... | collective-permute-start | bytes 393224 | tf_op jit(solution)/shard_map/ppermute | solution.py:29
  3.9 0.1 reshape.68
  4.0 0.9 %copy-done.1 = bf16[256,512]{1,0:T(8,128)(2,1)S(1)} copy-done((bf16[256,512]{1,0:T(8,128)(2,1)S(1)}, bf16[256,512]{1,0:T(8,128)(2,1)}, u32[]{:S(2)}) %copy-start.1) | copy-done | bytes 262168
  4.8 0.1 reshape.69
  4.9 0.4 constant_dynamic-slice_fusion
  5.3 0.7 %collective-permute-done.2 = bf16[512,128]{1,0:T(8,128)(2,1)S(1)} collective-permute-done((bf16[512,128]{1,0:T(8,128)(2,1)S(1)}, bf16[512,128]{1,0:T(8,128)(2,1)S(1)}, u32[]{:S(2)}, u32[]{:S(2)}) %collective-permute-start.2) | collective-permute-done | bytes 131104 | tf_op jit(solution)/shard_map/ppermute | solution.py:25
  6.0 0.3 collective-permute-start.6
  6.4 2.0 %collective-permute-start.5 = (bf16[1024,128]{1,0:T(8,128)(2,1)S(1)}, bf16[1024,128]{1,0:T(8,128)(2,1)S(1)}, u32[]{:S(2)}, u32[]{:S(2)}) collective-permute-start(bf16[1024,128]{1,0:T(8,128)(2,1)S(1)} %bitcast.100), channel_id=1, source_target_pairs={{0,24},{8,16},{16,8},{24,0},{1,25},{9,17},{17,9},{25,1},{2,26},{10... | collective-permute-start | bytes 786440 | tf_op jit(solution)/shard_map/ppermute | solution.py:29
  8.4 0.0 collective-permute-start
  8.5 1.3 %collective-permute-start.4 = (bf16[1024,128]{1,0:T(8,128)(2,1)S(1)}, bf16[1024,128]{1,0:T(8,128)(2,1)S(1)}, u32[]{:S(2)}, u32[]{:S(2)}) collective-permute-start(bf16[1024,128]{1,0:T(8,128)(2,1)S(1)} %bitcast.63), channel_id=1, source_target_pairs={{0,16},{8,24},{16,0},{24,8},{1,17},{9,25},{17,1},{25,9},{2,18},{10... | collective-permute-start | bytes 786440 | tf_op jit(solution)/shard_map/ppermute | solution.py:29
  9.8 0.0 collective-permute-done.1
  9.8 2.3 %collective-permute-start.8 = (bf16[512,128]{1,0:T(8,128)(2,1)S(1)}, bf16[512,128]{1,0:T(8,128)(2,1)S(1)}, u32[]{:S(2)}, u32[]{:S(2)}) collective-permute-start(bf16[512,128]{1,0:T(8,128)(2,1)S(1)} %collective-permute-done.2), channel_id=1, source_target_pairs={{7,0},{0,1},{1,2},{2,3},{3,4},{4,5},{5,6},{6,7},{15,8},{8,9},{9,10... | collective-permute-start | bytes 393224 | tf_op jit(solution)/shard_map/ppermute | solution.py:25
  12.1 0.0 collective-permute-done.6
  12.1 1.1 %collective-permute-start.3 = (bf16[512,128]{1,0:T(8,128)(2,1)S(1)}, bf16[512,128]{1,0:T(8,128)(2,1)S(1)}, u32[]{:S(2)}, u32[]{:S(2)}) collective-permute-start(bf16[512,128]{1,0:T(8,128)(2,1)S(1)} %collective-permute-done.2), channel_id=1, source_target_pairs={{0,8},{8,0},{16,24},{24,16},{1,9},{9,1},{17,25},{25,17},{2,10},{10... | collective-permute-start | bytes 393224 | tf_op jit(solution)/shard_map/ppermute | solution.py:29
  13.1 0.9 %collective-permute-done.8 = bf16[512,128]{1,0:T(8,128)(2,1)S(1)} collective-permute-done((bf16[512,128]{1,0:T(8,128)(2,1)S(1)}, bf16[512,128]{1,0:T(8,128)(2,1)S(1)}, u32[]{:S(2)}, u32[]{:S(2)}) %collective-permute-start.8) | collective-permute-done | bytes 131104 | tf_op jit(solution)/shard_map/ppermute | solution.py:25
  14.1 1.7 %collective-permute-start.7 = (bf16[512,128]{1,0:T(8,128)(2,1)S(1)}, bf16[512,128]{1,0:T(8,128)(2,1)S(1)}, u32[]{:S(2)}, u32[]{:S(2)}) collective-permute-start(bf16[512,128]{1,0:T(8,128)(2,1)S(1)} %collective-permute-done.6), channel_id=1, source_target_pairs={{0,8},{8,0},{16,24},{24,16},{1,9},{9,1},{17,25},{25,17},{2,10},{10... | collective-permute-start | bytes 393224 | tf_op jit(solution)/shard_map/ppermute | solution.py:29
  15.8 0.0 collective-permute-done.3
  15.8 0.0 collective-permute-start.9
  15.8 0.7 %copy-done.2 = s32[64]{0:T(128)S(1)} copy-done((s32[64]{0:T(128)S(1)}, s32[64]{0:T(128)}, u32[]{:S(2)}) %copy-start.2) | copy-done | bytes 280
  16.4 0.1 concatenate.7.where_ref
  16.5 0.0 collective-permute-done
  16.5 2.8 %stats.2.rest_0_ = f32[3,8,256]{2,1,0:T(8,128)S(1)} custom-call(s32[72]{0:T(128)S(1)} %concatenate.7.where_ref, bf16[4,256,128]{2,1,0:T(8,128)(2,1)S(1)} %bitcast.64, bf16[4,256,128]{2,1,0:T(8,128)(2,1)S(1)} %bitcast.74, bf16[4,128,128]{2,1,0:T(8,128)(2,1)S(1)} %bitcast.60, bf16[4,128,128]{2,1,0:T(8,128)(2,1)S(1)} %bitcast.81, ...), custom_call_target="tpu_custom_call" | custom-call | flops 536870912 | bytes 1048576 | tf_op jit(solution)/shard_map/stats/pallas_call | solution.py:303
  19.3 0.0 collective-permute-done.5
  19.3 1.6 %collective-permute-done.4 = bf16[1024,128]{1,0:T(8,128)(2,1)S(1)} collective-permute-done((bf16[1024,128]{1,0:T(8,128)(2,1)S(1)}, bf16[1024,128]{1,0:T(8,128)(2,1)S(1)}, u32[]{:S(2)}, u32[]{:S(2)}) %collective-permute-start.4) | collective-permute-done | bytes 262176 | tf_op jit(solution)/shard_map/ppermute | solution.py:29
  20.9 0.0 collective-permute-done.9
  20.9 5.0 %stats.3.rest_0_ = f32[3,8,256]{2,1,0:T(8,128)S(1)} custom-call(s32[72]{0:T(128)S(1)} %concatenate.7.where_ref, f32[3,8,256]{2,1,0:T(8,128)S(1)} %stats.2.rest_0_, bf16[4,256,128]{2,1,0:T(8,128)(2,1)S(1)} %bitcast.65, bf16[4,256,128]{2,1,0:T(8,128)(2,1)S(1)} %bitcast.75, bf16[4,256,128]{2,1,0:T(8,128)(2,1)S(1)} %bitcast.78, ...), custom_call_target="tpu_custom_call" | custom-call | flops 1610612736 | bytes 1048576 | tf_op jit(solution)/shard_map/stats/pallas_call | solution.py:303
  25.9 0.5 collective-permute-start.10
  26.5 2.5 %collective-permute-done.10.rest_1_ = f32[3,8,256]{2,1,0:T(8,128)S(1)} collective-permute-done((f32[3,8,256]{2,1,0:T(8,128)S(1)}, f32[3,8,256]{2,1,0:T(8,128)S(1)}, u32[]{:S(2)}, u32[]{:S(2)}) %collective-permute-start.10) | collective-permute-done | bytes 24608 | tf_op jit(solution)/shard_map/ppermute | solution.py:29
  29.0 5.5 %grads.2 = (f32[512,128]{1,0:T(8,128)S(1)}, f32[512,128]{1,0:T(8,128)S(1)}, bf16[1024,128]{1,0:T(8,128)(2,1)S(1)}, f32[8,128,256]{2,1,0:T(8,128)S(1)}, f32[8,8,256]{2,1,0:T(8,128)S(1)}) custom-call(s32[72]{0:T(128)S(1)} %concatenate.7.where_ref, f32[3,8,256]{2,1,0:T(8,128)S(1)} %stats.3.rest_0_, f32[3,8,256]{2,1,0:T(8,128)S(1)} %collective-permute-done.10.rest_1_, ...), custom_call_target="tpu_custom_call" | custom-call | flops 3221225472 | bytes 2097152 | tf_op jit(solution)/shard_map/grads/pallas_call | solution.py:341
  34.5 0.7 %collective-permute-start.15 = (bf16[1024,128]{1,0:T(8,128)(2,1)S(1)}, bf16[1024,128]{1,0:T(8,128)(2,1)S(1)}, u32[]{:S(2)}, u32[]{:S(2)}) collective-permute-start(bf16[1024,128]{1,0:T(8,128)(2,1)S(1)} %get-tuple-element.23), channel_id=1, source_target_pairs={{0,8},{8,0},{16,24},{24,16},{1,9},{9,1},{17,25},{25,17},{2,10},{10... | collective-permute-start | bytes 786440 | tf_op jit(solution)/shard_map/ppermute | solution.py:29
  35.2 6.4 %grads.3 = (f32[512,128]{1,0:T(8,128)S(1)}, f32[512,128]{1,0:T(8,128)S(1)}, bf16[1536,128]{1,0:T(8,128)(2,1)S(1)}, f32[512,128]{1,0:T(8,128)S(1)}, bf16[512,128]...) custom-call(s32[72]{0:T(128)S(1)} %concatenate.7.where_ref, f32[8,128,256]{2,1,0:T(8,128)S(1)} %get-tuple-element.14.rest_0_, ...), custom_call_target="tpu_custom_call" | custom-call | flops 3221225472 | bytes 2097152 | tf_op jit(solution)/shard_map/grads/pallas_call | solution.py:341
  41.6 0.1 collective-permute-start.12
  41.7 0.1 collective-permute-start.11
  41.8 2.0 %collective-permute-start.13 = (bf16[512,128]{1,0:T(8,128)(2,1)S(1)}, bf16[512,128]{1,0:T(8,128)(2,1)S(1)}, u32[]{:S(2)}, u32[]{:S(2)}) collective-permute-start(bf16[512,128]{1,0:T(8,128)(2,1)S(1)} %get-tuple-element.19), channel_id=1, source_target_pairs={{0,24},{8,16},{16,8},{24,0},{1,25},{9,17},{17,9},{25,1},{2,26},{10... | collective-permute-start | bytes 393224 | tf_op jit(solution)/shard_map/ppermute | solution.py:29
  43.8 0.1 add_convert_fusion.2
  43.9 2.7 %collective-permute-start.16 = (bf16[512,128]{1,0:T(8,128)(2,1)S(1)}, bf16[512,128]{1,0:T(8,128)(2,1)S(1)}, u32[]{:S(2)}, u32[]{:S(2)}) collective-permute-start(bf16[512,128]{1,0:T(8,128)(2,1)S(1)} %get-tuple-element.28), channel_id=1, source_target_pairs={{3,0},{4,1},{5,2},{6,3},{7,4},{0,5},{1,6},{2,7},{11,8},{12,9},{13,... | collective-permute-start | bytes 393224 | tf_op jit(solution)/shard_map/ppermute | solution.py:25
  46.6 3.1 %collective-permute-start.17 = (bf16[512,128]{1,0:T(8,128)(2,1)S(1)}, bf16[512,128]{1,0:T(8,128)(2,1)S(1)}, u32[]{:S(2)}, u32[]{:S(2)}) collective-permute-start(bf16[512,128]{1,0:T(8,128)(2,1)S(1)} %get-tuple-element.29), channel_id=1, source_target_pairs={{2,0},{3,1},{4,2},{5,3},{6,4},{7,5},{0,6},{1,7},{10,8},{11,9},{12,... | collective-permute-start | bytes 393224 | tf_op jit(solution)/shard_map/ppermute | solution.py:25
  49.7 0.1 collective-permute-start.14
  49.8 0.0 collective-permute-done.11
  49.8 0.3 collective-permute-done.13
  50.1 2.5 %collective-permute-done.16 = bf16[512,128]{1,0:T(8,128)(2,1)S(1)} collective-permute-done((bf16[512,128]{1,0:T(8,128)(2,1)S(1)}, bf16[512,128]{1,0:T(8,128)(2,1)S(1)}, u32[]{:S(2)}, u32[]{:S(2)}) %collective-permute-start.16) | collective-permute-done | bytes 131104 | tf_op jit(solution)/shard_map/ppermute | solution.py:25
  52.6 1.7 %collective-permute-done.17 = bf16[512,128]{1,0:T(8,128)(2,1)S(1)} collective-permute-done((bf16[512,128]{1,0:T(8,128)(2,1)S(1)}, bf16[512,128]{1,0:T(8,128)(2,1)S(1)}, u32[]{:S(2)}, u32[]{:S(2)}) %collective-permute-start.17) | collective-permute-done | bytes 131104 | tf_op jit(solution)/shard_map/ppermute | solution.py:25
  54.2 6.7 %collective-permute-done.14 = bf16[512,128]{1,0:T(8,128)(2,1)S(1)} collective-permute-done((bf16[512,128]{1,0:T(8,128)(2,1)S(1)}, bf16[512,128]{1,0:T(8,128)(2,1)S(1)}, u32[]{:S(2)}, u32[]{:S(2)}) %collective-permute-start.14) | collective-permute-done | bytes 131104 | tf_op jit(solution)/shard_map/ppermute | solution.py:25
  61.0 0.2 select_convert_fusion.1
  61.2 0.7 %fusion = (bf16[2,1,128,128]{3,2,1,0:T(8,128)(2,1)}, bf16[2,1,128,128]{3,2,1,0:T(8,128)(2,1)}) fusion(bf16[2,2,128,128]{3,2,1,0:T(8,128)(2,1)S(1)} %bitcast.99), kind=kLoop, calls=%fused_computation.21 | loop fusion | bytes 262144 | tf_op jit(solution)/shard_map/slice | solution.py:396
  61.9 0.7 %pad_maximum_fusion.2 = bf16[256,512]{1,0:T(8,128)(2,1)} fusion(bf16[256,128]{1,0:T(8,128)(2,1)S(1)} %get-tuple-element.39, bf16[256,128]{1,0:T(8,128)(2,1)S(1)} %get-tuple-element.38, bf16[256,128]{1,0:T(8,128)(2,1)S(1)} %get-tuple-element.37, bf16[256,128]{1,0:T(8,128)(2,1)S(1)} %get-tuple-element.36), kind=kLoop, calls=%fused_computation.2 | loop fusion | flops 1048576 | bytes 524288 | tf_op jit(solution)/shard_map/concatenate | solution.py:383
  (19 shorter events, 0.3 us)
Async XLA Ops:
  0.6 3.3 %copy-start = (bf16[256,512]{1,0:T(8,128)(2,1)S(1)}, bf16[256,512]{1,0:T(8,128)(2,1)}, u32[]{:S(2)}) copy-start(bf16[256,512]{1,0:T(8,128)(2,1)} %param.5) | copy-start | bytes 786436
  1.6 4.4 %collective-permute-start.2 = (bf16[512,128]{1,0:T(8,128)(2,1)S(1)}, bf16[512,128]{1,0:T(8,128)(2,1)S(1)}, u32[]{:S(2)}, u32[]{:S(2)}) collective-permute-start(bf16[512,128]{1,0:T(8,128)(2,1)S(1)} %bitcast.58), channel_id=1, source_target_pairs={{6,0},{7,1},{0,2},{1,3},{2,4},{3,5},{4,6},{5,7},{14,8},{15,9},{8,1... | collective-permute-start | bytes 393224 | tf_op jit(solution)/shard_map/ppermute | solution.py:25
  2.9 6.9 %collective-permute-start.1 = (bf16[512,128]{1,0:T(8,128)(2,1)S(1)}, bf16[512,128]{1,0:T(8,128)(2,1)S(1)}, u32[]{:S(2)}, u32[]{:S(2)}) collective-permute-start(bf16[512,128]{1,0:T(8,128)(2,1)S(1)} %bitcast.59), channel_id=1, source_target_pairs={{0,8},{8,0},{16,24},{24,16},{1,9},{9,1},{17,25},{25,17},{2,10},{10... | collective-permute-start | bytes 393224 | tf_op jit(solution)/shard_map/ppermute | solution.py:29
  3.9 1.0 %copy-start.1 = (bf16[256,512]{1,0:T(8,128)(2,1)S(1)}, bf16[256,512]{1,0:T(8,128)(2,1)}, u32[]{:S(2)}) copy-start(bf16[256,512]{1,0:T(8,128)(2,1)} %param.8) | copy-start | bytes 786436
  6.0 6.0 %collective-permute-start.6 = (bf16[512,128]{1,0:T(8,128)(2,1)S(1)}, bf16[512,128]{1,0:T(8,128)(2,1)S(1)}, u32[]{:S(2)}, u32[]{:S(2)}) collective-permute-start(bf16[512,128]{1,0:T(8,128)(2,1)S(1)} %broadcast_select_fusion), channel_id=1, source_target_pairs={{0,1},{1,0},{2,3},{3,2},{4,5},{5,4},{6,7},{7,6},{8,9},{9,8},{10,11... | collective-permute-start | bytes 393224 | tf_op jit(solution)/shard_map/ppermute | solution.py:29
  6.4 12.9 %collective-permute-start.5 = (bf16[1024,128]{1,0:T(8,128)(2,1)S(1)}, bf16[1024,128]{1,0:T(8,128)(2,1)S(1)}, u32[]{:S(2)}, u32[]{:S(2)}) collective-permute-start(bf16[1024,128]{1,0:T(8,128)(2,1)S(1)} %bitcast.100), channel_id=1, source_target_pairs={{0,24},{8,16},{16,8},{24,0},{1,25},{9,17},{17,9},{25,1},{2,26},{10... | collective-permute-start | bytes 786440 | tf_op jit(solution)/shard_map/ppermute | solution.py:29
  8.4 8.1 %collective-permute-start = (bf16[1024,128]{1,0:T(8,128)(2,1)S(1)}, bf16[1024,128]{1,0:T(8,128)(2,1)S(1)}, u32[]{:S(2)}, u32[]{:S(2)}) collective-permute-start(bf16[1024,128]{1,0:T(8,128)(2,1)S(1)} %bitcast.101), channel_id=1, source_target_pairs={{0,8},{8,0},{16,24},{24,16},{1,9},{9,1},{17,25},{25,17},{2,10},{10... | collective-permute-start | bytes 786440 | tf_op jit(solution)/shard_map/ppermute | solution.py:29
  8.5 12.4 %collective-permute-start.4 = (bf16[1024,128]{1,0:T(8,128)(2,1)S(1)}, bf16[1024,128]{1,0:T(8,128)(2,1)S(1)}, u32[]{:S(2)}, u32[]{:S(2)}) collective-permute-start(bf16[1024,128]{1,0:T(8,128)(2,1)S(1)} %bitcast.63), channel_id=1, source_target_pairs={{0,16},{8,24},{16,0},{24,8},{1,17},{9,25},{17,1},{25,9},{2,18},{10... | collective-permute-start | bytes 786440 | tf_op jit(solution)/shard_map/ppermute | solution.py:29
  9.8 4.3 %collective-permute-start.8 = (bf16[512,128]{1,0:T(8,128)(2,1)S(1)}, bf16[512,128]{1,0:T(8,128)(2,1)S(1)}, u32[]{:S(2)}, u32[]{:S(2)}) collective-permute-start(bf16[512,128]{1,0:T(8,128)(2,1)S(1)} %collective-permute-done.2), channel_id=1, source_target_pairs={{7,0},{0,1},{1,2},{2,3},{3,4},{4,5},{5,6},{6,7},{15,8},{8,9},{9,10... | collective-permute-start | bytes 393224 | tf_op jit(solution)/shard_map/ppermute | solution.py:25
  12.1 3.7 %collective-permute-start.3 = (bf16[512,128]{1,0:T(8,128)(2,1)S(1)}, bf16[512,128]{1,0:T(8,128)(2,1)S(1)}, u32[]{:S(2)}, u32[]{:S(2)}) collective-permute-start(bf16[512,128]{1,0:T(8,128)(2,1)S(1)} %collective-permute-done.2), channel_id=1, source_target_pairs={{0,8},{8,0},{16,24},{24,16},{1,9},{9,1},{17,25},{25,17},{2,10},{10... | collective-permute-start | bytes 393224 | tf_op jit(solution)/shard_map/ppermute | solution.py:29
  14.1 6.8 %collective-permute-start.7 = (bf16[512,128]{1,0:T(8,128)(2,1)S(1)}, bf16[512,128]{1,0:T(8,128)(2,1)S(1)}, u32[]{:S(2)}, u32[]{:S(2)}) collective-permute-start(bf16[512,128]{1,0:T(8,128)(2,1)S(1)} %collective-permute-done.6), channel_id=1, source_target_pairs={{0,8},{8,0},{16,24},{24,16},{1,9},{9,1},{17,25},{25,17},{2,10},{10... | collective-permute-start | bytes 393224 | tf_op jit(solution)/shard_map/ppermute | solution.py:29
  15.8 5.1 %collective-permute-start.9 = (bf16[512,128]{1,0:T(8,128)(2,1)S(1)}, bf16[512,128]{1,0:T(8,128)(2,1)S(1)}, u32[]{:S(2)}, u32[]{:S(2)}) collective-permute-start(bf16[512,128]{1,0:T(8,128)(2,1)S(1)} %collective-permute-done.8), channel_id=1, source_target_pairs={{0,8},{8,0},{16,24},{24,16},{1,9},{9,1},{17,25},{25,17},{2,10},{10... | collective-permute-start | bytes 393224 | tf_op jit(solution)/shard_map/ppermute | solution.py:29
  15.8 0.7 %copy-start.2 = (s32[64]{0:T(128)S(1)}, s32[64]{0:T(128)}, u32[]{:S(2)}) copy-start(s32[64]{0:T(128)} %param.9) | copy-start | bytes 772
  25.9 3.1 %collective-permute-start.10 = (f32[3,8,256]{2,1,0:T(8,128)S(1)}, f32[3,8,256]{2,1,0:T(8,128)S(1)}, u32[]{:S(2)}, u32[]{:S(2)}) collective-permute-start(f32[3,8,256]{2,1,0:T(8,128)S(1)} %stats.3.rest_0_), channel_id=1, source_target_pairs={{0,16},{8,24},{16,0},{24,8},{1,17},{9,25},{17,1},{25,9},{2,18},{10... | collective-permute-start | bytes 73736 | tf_op jit(solution)/shard_map/ppermute | solution.py:29
  34.5 9.4 %collective-permute-start.15 = (bf16[1024,128]{1,0:T(8,128)(2,1)S(1)}, bf16[1024,128]{1,0:T(8,128)(2,1)S(1)}, u32[]{:S(2)}, u32[]{:S(2)}) collective-permute-start(bf16[1024,128]{1,0:T(8,128)(2,1)S(1)} %get-tuple-element.23), channel_id=1, source_target_pairs={{0,8},{8,0},{16,24},{24,16},{1,9},{9,1},{17,25},{25,17},{2,10},{10... | collective-permute-start | bytes 786440 | tf_op jit(solution)/shard_map/ppermute | solution.py:29
  41.6 8.1 %collective-permute-start.12 = (bf16[1536,128]{1,0:T(8,128)(2,1)S(1)}, bf16[1536,128]{1,0:T(8,128)(2,1)S(1)}, u32[]{:S(2)}, u32[]{:S(2)}) collective-permute-start(bf16[1536,128]{1,0:T(8,128)(2,1)S(1)} %get-tuple-element.18), channel_id=1, source_target_pairs={{0,8},{8,0},{16,24},{24,16},{1,9},{9,1},{17,25},{25,17},{2,10},{10... | collective-permute-start | bytes 1179656 | tf_op jit(solution)/shard_map/ppermute | solution.py:29
  41.7 8.1 %collective-permute-start.11 = (bf16[512,128]{1,0:T(8,128)(2,1)S(1)}, bf16[512,128]{1,0:T(8,128)(2,1)S(1)}, u32[]{:S(2)}, u32[]{:S(2)}) collective-permute-start(bf16[512,128]{1,0:T(8,128)(2,1)S(1)} %get-tuple-element.17), channel_id=1, source_target_pairs={{0,16},{8,24},{16,0},{24,8},{1,17},{9,25},{17,1},{25,9},{2,18},{10... | collective-permute-start | bytes 393224 | tf_op jit(solution)/shard_map/ppermute | solution.py:29
  41.8 8.3 %collective-permute-start.13 = (bf16[512,128]{1,0:T(8,128)(2,1)S(1)}, bf16[512,128]{1,0:T(8,128)(2,1)S(1)}, u32[]{:S(2)}, u32[]{:S(2)}) collective-permute-start(bf16[512,128]{1,0:T(8,128)(2,1)S(1)} %get-tuple-element.19), channel_id=1, source_target_pairs={{0,24},{8,16},{16,8},{24,0},{1,25},{9,17},{17,9},{25,1},{2,26},{10... | collective-permute-start | bytes 393224 | tf_op jit(solution)/shard_map/ppermute | solution.py:29
  43.9 8.7 %collective-permute-start.16 = (bf16[512,128]{1,0:T(8,128)(2,1)S(1)}, bf16[512,128]{1,0:T(8,128)(2,1)S(1)}, u32[]{:S(2)}, u32[]{:S(2)}) collective-permute-start(bf16[512,128]{1,0:T(8,128)(2,1)S(1)} %get-tuple-element.28), channel_id=1, source_target_pairs={{3,0},{4,1},{5,2},{6,3},{7,4},{0,5},{1,6},{2,7},{11,8},{12,9},{13,... | collective-permute-start | bytes 393224 | tf_op jit(solution)/shard_map/ppermute | solution.py:25
  46.6 7.7 %collective-permute-start.17 = (bf16[512,128]{1,0:T(8,128)(2,1)S(1)}, bf16[512,128]{1,0:T(8,128)(2,1)S(1)}, u32[]{:S(2)}, u32[]{:S(2)}) collective-permute-start(bf16[512,128]{1,0:T(8,128)(2,1)S(1)} %get-tuple-element.29), channel_id=1, source_target_pairs={{2,0},{3,1},{4,2},{5,3},{6,4},{7,5},{0,6},{1,7},{10,8},{11,9},{12,... | collective-permute-start | bytes 393224 | tf_op jit(solution)/shard_map/ppermute | solution.py:25
  49.7 11.3 %collective-permute-start.14 = (bf16[512,128]{1,0:T(8,128)(2,1)S(1)}, bf16[512,128]{1,0:T(8,128)(2,1)S(1)}, u32[]{:S(2)}, u32[]{:S(2)}) collective-permute-start(bf16[512,128]{1,0:T(8,128)(2,1)S(1)} %add_convert_fusion.3), channel_id=1, source_target_pairs={{1,0},{2,1},{3,2},{4,3},{5,4},{6,5},{7,6},{0,7},{9,8},{10,9},{11,1... | collective-permute-start | bytes 393224 | tf_op jit(solution)/shard_map/ppermute | solution.py:25

commit v4 on v3

--- a/solution.py
+++ b/solution.py
@@ -58,7 +58,23 @@
         position = position + lax.rem(position, 2)
     for extra in range(10):
         list_ref[position + extra] = pad
-    return (position + 6) // 8
+    trips = (position + 6) // 8
+    list_ref[list_ref.shape[0] - 1] = trips
+    return trips
+
+
+def list_size(plan):
+    return sum(len(blocks) for _, blocks in plan) + 16
+
+
+def stats_plan(steps, merged):
+    held = range(STEPS) if merged else steps
+    order = (list(range(4, 8)) if merged else []) + list(range(4))
+    return [(query, blocks_of(held if query >= 4 else steps)) for query in order]
+
+
+def grads_plan(steps):
+    return [(query, blocks_of(steps)) for query in range(8)]
 
 
 def blocks_of(steps):
@@ -71,7 +87,7 @@
     return at0 // key_blocks, at0 % key_blocks, e0 % 4, at1 % key_blocks, e1 % 4
 
 
-def score_tiles(entry, factor, qg, kv, bias, t_ref, dp_ref, top_ref=None):
+def score_tiles(entry, factor, qg, kv, bias):
     query, j0, b0, j1, b1 = entry
     k2 = jnp.concatenate([kv[2 * j0], kv[2 * j1]], axis=0)
     v2 = jnp.concatenate([kv[2 * j0 + 1], kv[2 * j1 + 1]], axis=0)
@@ -80,10 +96,7 @@
         [jnp.concatenate([low, low], axis=1), jnp.concatenate([high, high], axis=1)], axis=0
     )
     t = dot_nt(k2, qg[2 * query]) * factor + b2
-    t_ref[...] = t
-    if top_ref is not None:
-        top_ref[...] = jnp.max(t.reshape(-1, 8, t.shape[1]), axis=0)
-    dp_ref[...] = dot_nt(v2, qg[2 * query + 1])
+    return t, dot_nt(v2, qg[2 * query + 1])
 
 
 def stack_refs(refs, dst):
@@ -108,21 +121,25 @@
         use(4 * i + 3, 3)
 
 
-def stats_kernel(sizes, factor, steps, merged, where_ref, *rest):
+def stats_kernel(sizes, factor, steps, merged, later, where_ref, *rest):
     outer_size, key_blocks, _, width = sizes
     if merged:
         early, rest = rest[0], rest[1:]
     count = 8 if merged else 4
     held = list(range(STEPS)) if merged else list(steps)
     q_refs, kv_refs = rest[: count // 2], rest[count // 2 : count // 2 + 2 * len(held)]
-    out_ref, qg, kv, bias, *tiles, state, lists = rest[count // 2 + 2 * len(held) :]
+    rest = rest[count // 2 + 2 * len(held) :]
+    out_ref, later_refs, rest = rest[0], rest[1 : 1 + len(later)], rest[1 + len(later) :]
+    qg, kv, bias, *tiles, state, lists = rest
     stack_refs(kv_refs, kv)
     stack_refs(q_refs, qg)
-    plan = [
-        (query, blocks_of(held if query >= 4 else steps))
-        for query in (list(range(4, 8)) if merged else []) + list(range(4))
-    ]
-    trips = build_list((outer_size, key_blocks), plan, where_ref, lists)
+    if merged:
+        lists = where_ref
+        trips = lists[lists.shape[0] - 1]
+    else:
+        trips = build_list((outer_size, key_blocks), stats_plan(steps, merged), where_ref, lists)
+    for plan, list_ref in zip(later, later_refs):
+        build_list((outer_size, key_blocks), plan, where_ref, list_ref)
     fill_bias(bias)
     state[0] = jnp.full((count, 8, width), NEG, jnp.float32)
     state[1] = jnp.zeros((count, 8, width), jnp.float32)
@@ -144,7 +161,11 @@
         return query, slot_of(j0), b0, slot_of(j1), b1
 
     def load(n, slot):
-        score_tiles(entry(n), factor, qg, kv, bias, *slots[slot])
+        t_ref, d_ref, top = slots[slot]
+        t, dp = score_tiles(entry(n), factor, qg, kv, bias)
+        t_ref[...] = t
+        top[...] = jnp.max(t.reshape(-1, 8, width), axis=0)
+        d_ref[...] = dp
 
     def use(n, slot):
         query = entry(n)[0]
@@ -167,15 +188,15 @@
         out_ref[:, pl.ds(count, count)] = jnp.zeros((3, count, width), jnp.float32)
 
 
-def grads_kernel(sizes, scale, steps, last, where_ref, *rest):
-    outer_size, key_blocks, size, width = sizes
+def grads_kernel(sizes, scale, steps, last, lists, *rest):
+    _, key_blocks, size, width = sizes
     pairs = width // size
     carry_in, rest = rest[:2], rest[2:]
     q_refs, kv_refs = rest[:4], rest[4 : 4 + 2 * len(steps)]
     rest = rest[4 + 2 * len(steps) :]
     outs, sent, rest = rest[: len(steps)], rest[len(steps)], rest[len(steps) + 1 :]
     tops, rest = rest[: (3 if last else 2)], rest[(3 if last else 2) :]
-    qg, kv, kt, dk, dv, dq, base, bias, *tiles, lists = rest
+    qg, kv, kt, dk, dv, dq, base, bias, *tiles = rest
     low = 4 * min(steps)
     blocks = blocks_of(steps)
     stack_refs(kv_refs, kv)
@@ -183,8 +204,7 @@
     if last:
         dq[...] = carry_in[0][...]
         base[...] = carry_in[1][...]
-    plan = [(query, blocks) for query in range(8)]
-    trips = build_list((outer_size, key_blocks), plan, where_ref, lists)
+    trips = lists[lists.shape[0] - 1]
     fill_bias(bias)
     if not last:
         for query in range(8):
@@ -209,14 +229,16 @@
         return query, j0 - low, b0, j1 - low, b1
 
     def load(n, slot):
-        score_tiles(entry(n), factor, qg, kv, bias, *slots[slot])
+        at = entry(n)
+        p_ref, s_ref = slots[slot]
+        t, dp = score_tiles(at, factor, qg, kv, bias)
+        p = jnp.exp2(t - base[at[0], 0:1])
+        p_ref[...] = p.astype(jnp.bfloat16)
+        s_ref[...] = (p * (dp - base[at[0], 1:2])).astype(jnp.bfloat16)
 
     def use(n, slot):
         query, j0, _, j1, _ = entry(n)
-        t_ref, d_ref = slots[slot]
-        p = jnp.exp2(t_ref[...] - base[query, 0:1])
-        ds = (p * (d_ref[...] - base[query, 1:2])).astype(jnp.bfloat16)
-        p = p.astype(jnp.bfloat16)
+        p, ds = slots[slot][0][...], slots[slot][1][...]
         dv_part = jnp.dot(p, qg[2 * query + 1], preferred_element_type=jnp.float32)
         dk_part = jnp.dot(ds, qg[2 * query], preferred_element_type=jnp.float32)
         kt2 = jnp.concatenate([kt[j0], kt[j1]], axis=1)
@@ -291,21 +313,24 @@
     shards = [block.reshape(4, block_len, size) for two in zip(own, near) for block in two]
 
     sizes = (outer_size, key_blocks, size, width)
+    far_steps = tuple(range(STEPS // 2, STEPS))
+    near_steps = tuple(range(STEPS // 2))
     flops = 2 * 2 * width * 8 * key_blocks * block_len * size
     tile = pltpu.VMEM((2 * block_len, width), full)
     bias_table = pltpu.VMEM((3, block_len, block_len), full)
 
-    def stats_call(steps, *early):
+    def stats_call(table, steps, later, *early):
         merged = len(early) > 0
         count = 8 if merged else 4
         held = range(STEPS) if merged else steps
         used = [part for step in held for part in shards[2 * step : 2 * step + 2]]
         return pl.pallas_call(
-            functools.partial(stats_kernel, sizes, scale * LOG2E, steps, merged),
+            functools.partial(stats_kernel, sizes, scale * LOG2E, steps, merged, later),
             name="stats",
-            out_shape=jax.ShapeDtypeStruct((3, 8, width), full),
+            out_shape=[jax.ShapeDtypeStruct((3, 8, width), full)]
+            + [jax.ShapeDtypeStruct((list_size(plan),), jnp.int32) for plan in later],
             in_specs=[smem] + [vmem] * (len(early) + count // 2 + len(used)),
-            out_specs=vmem,
+            out_specs=[vmem] + [smem] * len(later),
             scratch_shapes=[
                 pltpu.VMEM((2 * count, width, size), low),
                 pltpu.VMEM((4 * len(used), block_len, size), low),
@@ -318,15 +343,17 @@
             cost_estimate=pl.CostEstimate(
                 flops=flops * 3 // 4 if merged else flops // 4, bytes_accessed=1 << 20, transcendentals=0
             ),
-        )(where, *early, *q_parts[: count // 2], *used)
-
-    early = stats_call((0, 2))
-    stats = stats_call((1, 3), early)
+        )(table, *early, *q_parts[: count // 2], *used)
+
+    early, rest_list, far_list, near_list = stats_call(
+        where, (0, 2), (stats_plan((1, 3), True), grads_plan(far_steps), grads_plan(near_steps))
+    )
+    (stats,) = stats_call(rest_list, (1, 3), (), early)
     others = swap(stats, "inner", 2)
     shard_f32 = jax.ShapeDtypeStruct(kv_shape, full)
     rows = kv_shape[0]
 
-    def grads_call(steps, last, *extra):
+    def grads_call(table, steps, last, *extra):
         n = len(steps)
         if last:
             tops = [
@@ -355,20 +382,17 @@
                 pltpu.VMEM((8, size, width), full),
                 pltpu.VMEM((8, 8, width), full),
                 bias_table,
-                *[tile] * 8,
-                pltpu.SMEM((8 * 4 * n + 16,), jnp.int32),
+                *[pltpu.VMEM((2 * block_len, width), low)] * 8,
             ],
             compiler_params=params,
             cost_estimate=pl.CostEstimate(
                 flops=flops * 3 * n // STEPS, bytes_accessed=1 << 21, transcendentals=0
             ),
-        )(where, *extra, *q_parts, *used)
-
-    far_steps = tuple(range(STEPS // 2, STEPS))
-    near_steps = tuple(range(STEPS // 2))
-    *far_own, sent, dq_carry, base = grads_call(far_steps, False, stats, others)
+        )(table, *extra, *q_parts, *used)
+
+    *far_own, sent, dq_carry, base = grads_call(far_list, far_steps, False, stats, others)
     far_got = swap(sent, "inner", 1)
-    *near_own, sent, dq0, dq2, dq3 = grads_call(near_steps, True, dq_carry, base)
+    *near_own, sent, dq0, dq2, dq3 = grads_call(near_list, near_steps, True, dq_carry, base)
     near_got = swap(sent, "inner", 1)
     back = []
     for steps, parts, got in ((far_steps, far_own, far_got), (near_steps, near_own, near_got)):

time: 62.8 us -> 62.4 us (level)
  waiting for transfers between devices: 16.9 us -> 14.5 us
  starting transfers between devices: 20.2 us -> 21.8 us
    ppermute x13, waiting for transfers between devices: 4.4 us -> 2.48 us  [swap(): lax.ppermute(block, axis, [(i, i ^ bit) for i in range(lax.axis_size(axis...]
    pallas_call x2, Pallas kernels: 7.79 us -> 8.88 us  [stats_call(): pl.pallas_call(functools.partial(stats_kernel, sizes, scale * LOG2E, step...]
    ppermute x5, starting transfers between devices: 9.47 us -> 10.3 us  [from_behind(): return lax.ppermute(block, axis, route)]
    ppermute x13, starting transfers between devices: 10.7 us -> 11.5 us  [swap(): lax.ppermute(block, axis, [(i, i ^ bit) for i in range(lax.axis_size(axis...]
  transfers between devices with their start and end apart: 18 -> 18, of which waited for: 8 -> 7; matrix products, arithmetic and copies ran while one was open for 1% -> 1% of each run, Pallas kernels for 15% -> 16%
where the time goes in v4:
time: 62.4 us; the launch traced here: 62.2 us
  starting transfers between devices  21.8 us (35%)
  Pallas kernels  20.2 us (32%)
  waiting for transfers between devices  14.5 us (23%)
  local copies, waits for them, and re-layouts  2.92 us (5%)
  other arithmetic  1.98 us (3%)
  between operations  0.85 us (1%)
    ppermute x5, waiting for transfers between devices, from_behind(): return lax.ppermute(block, axis, route)  12 us
    ppermute x13, starting transfers between devices, swap(): lax.ppermute(block, axis, [(i, i ^ bit) for i in range(lax.axis_size(axis...  11.5 us
    pallas_call x2, Pallas kernels, grads_call(): pl.pallas_call(functools.partial(grads_kernel, sizes, scale, steps, last)...  11.3 us
    ppermute x5, starting transfers between devices, from_behind(): return lax.ppermute(block, axis, route)  10.3 us
    pallas_call x2, Pallas kernels, stats_call(): pl.pallas_call(functools.partial(stats_kernel, sizes, scale * LOG2E, step...  8.88 us
    ppermute x13, waiting for transfers between devices, swap(): lax.ppermute(block, axis, [(i, i ^ bit) for i in range(lax.axis_size(axis...  2.48 us
    unnamed x6, local copies, waits for them, and re-layouts  1.54 us
  transfers between devices with their start and end apart: 18, of which 7 were waited for; matrix products, arithmetic and copies ran while one was open for 1% of the time, Pallas kernels for 16%

profile of v4, /device:TPU:15, one launch (start us, length us, event | category | flops | bytes accessed | tf_op | source)
XLA Modules:
  0.0 62.2 jit_solution(18382854897632919072)
XLA Ops:
  0.6 0.9 %pad_maximum_fusion.3 = bf16[2,2,128,128]{3,2,1,0:T(8,128)(2,1)S(1)} fusion(bf16[2,1,128,128]{3,2,1,0:T(8,128)(2,1)} %bitcast.102, bf16[2,1,128,128]{3,2,1,0:T(8,128)(2,1)} %bitcast.103), kind=kLoop, calls=%fused_computation.11 | loop fusion | flops 65536 | bytes 262144 | tf_op jit(solution)/shard_map/stack | solution.py:292
  1.6 1.3 %collective-permute-start.2 = (bf16[512,128]{1,0:T(8,128)(2,1)S(1)}, bf16[512,128]{1,0:T(8,128)(2,1)S(1)}, u32[]{:S(2)}, u32[]{:S(2)}) collective-permute-start(bf16[512,128]{1,0:T(8,128)(2,1)S(1)} %bitcast.58), channel_id=1, source_target_pairs={{6,0},{7,1},{0,2},{1,3},{2,4},{3,5},{4,6},{5,7},{14,8},{15,9},{8,1... | collective-permute-start | bytes 393224 | tf_op jit(solution)/shard_map/ppermute | solution.py:25
  2.9 1.0 %collective-permute-start.1 = (bf16[512,128]{1,0:T(8,128)(2,1)S(1)}, bf16[512,128]{1,0:T(8,128)(2,1)S(1)}, u32[]{:S(2)}, u32[]{:S(2)}) collective-permute-start(bf16[512,128]{1,0:T(8,128)(2,1)S(1)} %bitcast.59), channel_id=1, source_target_pairs={{0,8},{8,0},{16,24},{24,16},{1,9},{9,1},{17,25},{25,17},{2,10},{10... | collective-permute-start | bytes 393224 | tf_op jit(solution)/shard_map/ppermute | solution.py:29
  3.9 0.1 reshape.68
  4.0 0.9 %copy-done.1 = bf16[256,512]{1,0:T(8,128)(2,1)S(1)} copy-done((bf16[256,512]{1,0:T(8,128)(2,1)S(1)}, bf16[256,512]{1,0:T(8,128)(2,1)}, u32[]{:S(2)}) %copy-start.1) | copy-done | bytes 262168
  4.8 0.1 reshape.69
  4.9 0.4 constant_dynamic-slice_fusion
  5.3 0.7 %collective-permute-done.2 = bf16[512,128]{1,0:T(8,128)(2,1)S(1)} collective-permute-done((bf16[512,128]{1,0:T(8,128)(2,1)S(1)}, bf16[512,128]{1,0:T(8,128)(2,1)S(1)}, u32[]{:S(2)}, u32[]{:S(2)}) %collective-permute-start.2) | collective-permute-done | bytes 131104 | tf_op jit(solution)/shard_map/ppermute | solution.py:25
  6.0 0.3 collective-permute-start.6
  6.4 2.0 %collective-permute-start.5 = (bf16[1024,128]{1,0:T(8,128)(2,1)S(1)}, bf16[1024,128]{1,0:T(8,128)(2,1)S(1)}, u32[]{:S(2)}, u32[]{:S(2)}) collective-permute-start(bf16[1024,128]{1,0:T(8,128)(2,1)S(1)} %bitcast.100), channel_id=1, source_target_pairs={{0,24},{8,16},{16,8},{24,0},{1,25},{9,17},{17,9},{25,1},{2,26},{10... | collective-permute-start | bytes 786440 | tf_op jit(solution)/shard_map/ppermute | solution.py:29
  8.4 0.0 collective-permute-start
  8.5 1.3 %collective-permute-start.4 = (bf16[1024,128]{1,0:T(8,128)(2,1)S(1)}, bf16[1024,128]{1,0:T(8,128)(2,1)S(1)}, u32[]{:S(2)}, u32[]{:S(2)}) collective-permute-start(bf16[1024,128]{1,0:T(8,128)(2,1)S(1)} %bitcast.63), channel_id=1, source_target_pairs={{0,16},{8,24},{16,0},{24,8},{1,17},{9,25},{17,1},{25,9},{2,18},{10... | collective-permute-start | bytes 786440 | tf_op jit(solution)/shard_map/ppermute | solution.py:29
  9.8 0.0 collective-permute-done.1
  9.8 2.3 %collective-permute-start.8 = (bf16[512,128]{1,0:T(8,128)(2,1)S(1)}, bf16[512,128]{1,0:T(8,128)(2,1)S(1)}, u32[]{:S(2)}, u32[]{:S(2)}) collective-permute-start(bf16[512,128]{1,0:T(8,128)(2,1)S(1)} %collective-permute-done.2), channel_id=1, source_target_pairs={{7,0},{0,1},{1,2},{2,3},{3,4},{4,5},{5,6},{6,7},{15,8},{8,9},{9,10... | collective-permute-start | bytes 393224 | tf_op jit(solution)/shard_map/ppermute | solution.py:25
  12.1 0.0 collective-permute-done.6
  12.1 1.1 %collective-permute-start.3 = (bf16[512,128]{1,0:T(8,128)(2,1)S(1)}, bf16[512,128]{1,0:T(8,128)(2,1)S(1)}, u32[]{:S(2)}, u32[]{:S(2)}) collective-permute-start(bf16[512,128]{1,0:T(8,128)(2,1)S(1)} %collective-permute-done.2), channel_id=1, source_target_pairs={{0,8},{8,0},{16,24},{24,16},{1,9},{9,1},{17,25},{25,17},{2,10},{10... | collective-permute-start | bytes 393224 | tf_op jit(solution)/shard_map/ppermute | solution.py:29
  13.1 0.9 %collective-permute-done.8 = bf16[512,128]{1,0:T(8,128)(2,1)S(1)} collective-permute-done((bf16[512,128]{1,0:T(8,128)(2,1)S(1)}, bf16[512,128]{1,0:T(8,128)(2,1)S(1)}, u32[]{:S(2)}, u32[]{:S(2)}) %collective-permute-start.8) | collective-permute-done | bytes 131104 | tf_op jit(solution)/shard_map/ppermute | solution.py:25
  14.1 1.7 %collective-permute-start.7 = (bf16[512,128]{1,0:T(8,128)(2,1)S(1)}, bf16[512,128]{1,0:T(8,128)(2,1)S(1)}, u32[]{:S(2)}, u32[]{:S(2)}) collective-permute-start(bf16[512,128]{1,0:T(8,128)(2,1)S(1)} %collective-permute-done.6), channel_id=1, source_target_pairs={{0,8},{8,0},{16,24},{24,16},{1,9},{9,1},{17,25},{25,17},{2,10},{10... | collective-permute-start | bytes 393224 | tf_op jit(solution)/shard_map/ppermute | solution.py:29
  15.8 0.0 collective-permute-done.3
  15.8 0.0 collective-permute-start.9
  15.8 0.7 %copy-done.2 = s32[64]{0:T(128)S(1)} copy-done((s32[64]{0:T(128)S(1)}, s32[64]{0:T(128)}, u32[]{:S(2)}) %copy-start.2) | copy-done | bytes 280
  16.4 0.1 concatenate.7.where_ref
  16.5 0.0 collective-permute-done
  16.5 4.1 %stats.2 = (f32[3,8,256]{2,1,0:T(8,128)S(1)}, s32[112]{0:T(128)S(1)}, s32[80]{0:T(128)S(1)}, s32[80]{0:T(128)S(1)}) custom-call(s32[72]{0:T(128)S(1)} %concatenate.7.where_ref, bf16[4,256,128]{2,1,0:T(8,128)(2,1)S(1)} %bitcast.64, bf16[4,256,128]{2,1,0:T(8,128)(2,1)S(1)} %bitcast.74, bf16[4,128,128]{2,1,0:T(8,128)(2,1)S(1)} %bitcast.60, ...), custom_call_target="tpu_custom_call" | custom-call | flops 536870912 | bytes 1048576 | tf_op jit(solution)/shard_map/stats/pallas_call | solution.py:327
  20.6 0.0 collective-permute-done.5
  20.6 0.2 collective-permute-done.4
  20.9 0.0 collective-permute-done.9
  20.9 4.8 %stats.3.rest_0_ = f32[3,8,256]{2,1,0:T(8,128)S(1)} custom-call(s32[112]{0:T(128)S(1)} %get-tuple-element.20.where_ref, f32[3,8,256]{2,1,0:T(8,128)S(1)} %get-tuple-element.21.rest_0_, bf16[4,256,128]{2,1,0:T(8,128)(2,1)S(1)} %bitcast.65, bf16[4,256,128]{2,1,0:T(8,128)(2,1)S(1)} %bitcast.75, bf16[4,256,128]{2,1,0:T(8,128)(2,1)S(1)} %bitcast.78, ...), custom_call_target="tpu_custom_call" | custom-call | flops 1610612736 | bytes 1048576 | tf_op jit(solution)/shard_map/stats/pallas_call | solution.py:327
  25.7 0.5 collective-permute-start.10
  26.2 2.2 %collective-permute-done.10.rest_1_ = f32[3,8,256]{2,1,0:T(8,128)S(1)} collective-permute-done((f32[3,8,256]{2,1,0:T(8,128)S(1)}, f32[3,8,256]{2,1,0:T(8,128)S(1)}, u32[]{:S(2)}, u32[]{:S(2)}) %collective-permute-start.10) | collective-permute-done | bytes 24608 | tf_op jit(solution)/shard_map/ppermute | solution.py:29
  28.4 5.2 %grads.2 = (f32[512,128]{1,0:T(8,128)S(1)}, f32[512,128]{1,0:T(8,128)S(1)}, bf16[1024,128]{1,0:T(8,128)(2,1)S(1)}, f32[8,128,256]{2,1,0:T(8,128)S(1)}, f32[8,8,256]{2,1,0:T(8,128)S(1)}) custom-call(s32[80]{0:T(128)S(1)} %get-tuple-element.19.lists, f32[3,8,256]{2,1,0:T(8,128)S(1)} %stats.3.rest_0_, f32[3,8,256]{2,1,0:T(8,128)S(1)} %collective-permute-done.10.rest_1_, ...), custom_call_target="tpu_custom_call" | custom-call | flops 3221225472 | bytes 2097152 | tf_op jit(solution)/shard_map/grads/pallas_call | solution.py:368
  33.6 1.5 %collective-permute-start.15 = (bf16[1024,128]{1,0:T(8,128)(2,1)S(1)}, bf16[1024,128]{1,0:T(8,128)(2,1)S(1)}, u32[]{:S(2)}, u32[]{:S(2)}) collective-permute-start(bf16[1024,128]{1,0:T(8,128)(2,1)S(1)} %get-tuple-element.31), channel_id=1, source_target_pairs={{0,8},{8,0},{16,24},{24,16},{1,9},{9,1},{17,25},{25,17},{2,10},{10... | collective-permute-start | bytes 786440 | tf_op jit(solution)/shard_map/ppermute | solution.py:29
  35.1 6.1 %grads.3 = (f32[512,128]{1,0:T(8,128)S(1)}, f32[512,128]{1,0:T(8,128)S(1)}, bf16[1536,128]{1,0:T(8,128)(2,1)S(1)}, f32[512,128]{1,0:T(8,128)S(1)}, bf16[512,128]...) custom-call(s32[80]{0:T(128)S(1)} %get-tuple-element.18.lists, f32[8,128,256]{2,1,0:T(8,128)S(1)} %get-tuple-element.22.rest_0_, ...), custom_call_target="tpu_custom_call" | custom-call | flops 3221225472 | bytes 2097152 | tf_op jit(solution)/shard_map/grads/pallas_call | solution.py:368
  41.2 0.1 collective-permute-start.12
  41.3 0.1 collective-permute-start.11
  41.4 2.0 %collective-permute-start.13 = (bf16[512,128]{1,0:T(8,128)(2,1)S(1)}, bf16[512,128]{1,0:T(8,128)(2,1)S(1)}, u32[]{:S(2)}, u32[]{:S(2)}) collective-permute-start(bf16[512,128]{1,0:T(8,128)(2,1)S(1)} %get-tuple-element.27), channel_id=1, source_target_pairs={{0,24},{8,16},{16,8},{24,0},{1,25},{9,17},{17,9},{25,1},{2,26},{10... | collective-permute-start | bytes 393224 | tf_op jit(solution)/shard_map/ppermute | solution.py:29
  43.4 0.1 add_convert_fusion.2
  43.5 3.6 %collective-permute-start.16 = (bf16[512,128]{1,0:T(8,128)(2,1)S(1)}, bf16[512,128]{1,0:T(8,128)(2,1)S(1)}, u32[]{:S(2)}, u32[]{:S(2)}) collective-permute-start(bf16[512,128]{1,0:T(8,128)(2,1)S(1)} %get-tuple-element.36), channel_id=1, source_target_pairs={{3,0},{4,1},{5,2},{6,3},{7,4},{0,5},{1,6},{2,7},{11,8},{12,9},{13,... | collective-permute-start | bytes 393224 | tf_op jit(solution)/shard_map/ppermute | solution.py:25
  47.1 3.0 %collective-permute-start.17 = (bf16[512,128]{1,0:T(8,128)(2,1)S(1)}, bf16[512,128]{1,0:T(8,128)(2,1)S(1)}, u32[]{:S(2)}, u32[]{:S(2)}) collective-permute-start(bf16[512,128]{1,0:T(8,128)(2,1)S(1)} %get-tuple-element.37), channel_id=1, source_target_pairs={{2,0},{3,1},{4,2},{5,3},{6,4},{7,5},{0,6},{1,7},{10,8},{11,9},{12,... | collective-permute-start | bytes 393224 | tf_op jit(solution)/shard_map/ppermute | solution.py:25
  50.1 0.1 collective-permute-start.14
  50.2 0.0 collective-permute-done.11
  50.2 0.0 collective-permute-done.13
  50.2 2.7 %collective-permute-done.16 = bf16[512,128]{1,0:T(8,128)(2,1)S(1)} collective-permute-done((bf16[512,128]{1,0:T(8,128)(2,1)S(1)}, bf16[512,128]{1,0:T(8,128)(2,1)S(1)}, u32[]{:S(2)}, u32[]{:S(2)}) %collective-permute-start.16) | collective-permute-done | bytes 131104 | tf_op jit(solution)/shard_map/ppermute | solution.py:25
  53.0 1.1 %collective-permute-done.17 = bf16[512,128]{1,0:T(8,128)(2,1)S(1)} collective-permute-done((bf16[512,128]{1,0:T(8,128)(2,1)S(1)}, bf16[512,128]{1,0:T(8,128)(2,1)S(1)}, u32[]{:S(2)}, u32[]{:S(2)}) %collective-permute-start.17) | collective-permute-done | bytes 131104 | tf_op jit(solution)/shard_map/ppermute | solution.py:25
  54.1 6.6 %collective-permute-done.14 = bf16[512,128]{1,0:T(8,128)(2,1)S(1)} collective-permute-done((bf16[512,128]{1,0:T(8,128)(2,1)S(1)}, bf16[512,128]{1,0:T(8,128)(2,1)S(1)}, u32[]{:S(2)}, u32[]{:S(2)}) %collective-permute-start.14) | collective-permute-done | bytes 131104 | tf_op jit(solution)/shard_map/ppermute | solution.py:25
  60.6 0.2 select_convert_fusion.1
  60.8 0.7 %fusion = (bf16[2,1,128,128]{3,2,1,0:T(8,128)(2,1)}, bf16[2,1,128,128]{3,2,1,0:T(8,128)(2,1)}) fusion(bf16[2,2,128,128]{3,2,1,0:T(8,128)(2,1)S(1)} %bitcast.99), kind=kLoop, calls=%fused_computation.21 | loop fusion | bytes 262144 | tf_op jit(solution)/shard_map/slice | solution.py:420
  61.5 0.7 %pad_maximum_fusion.2 = bf16[256,512]{1,0:T(8,128)(2,1)} fusion(bf16[256,128]{1,0:T(8,128)(2,1)S(1)} %get-tuple-element.47, bf16[256,128]{1,0:T(8,128)(2,1)S(1)} %get-tuple-element.46, bf16[256,128]{1,0:T(8,128)(2,1)S(1)} %get-tuple-element.45, bf16[256,128]{1,0:T(8,128)(2,1)S(1)} %get-tuple-element.44), kind=kLoop, calls=%fused_computation.2 | loop fusion | flops 1048576 | bytes 524288 | tf_op jit(solution)/shard_map/concatenate | solution.py:407
  (19 shorter events, 0.3 us)
Async XLA Ops:
  0.6 3.3 %copy-start = (bf16[256,512]{1,0:T(8,128)(2,1)S(1)}, bf16[256,512]{1,0:T(8,128)(2,1)}, u32[]{:S(2)}) copy-start(bf16[256,512]{1,0:T(8,128)(2,1)} %param.5) | copy-start | bytes 786436
  1.6 4.4 %collective-permute-start.2 = (bf16[512,128]{1,0:T(8,128)(2,1)S(1)}, bf16[512,128]{1,0:T(8,128)(2,1)S(1)}, u32[]{:S(2)}, u32[]{:S(2)}) collective-permute-start(bf16[512,128]{1,0:T(8,128)(2,1)S(1)} %bitcast.58), channel_id=1, source_target_pairs={{6,0},{7,1},{0,2},{1,3},{2,4},{3,5},{4,6},{5,7},{14,8},{15,9},{8,1... | collective-permute-start | bytes 393224 | tf_op jit(solution)/shard_map/ppermute | solution.py:25
  2.9 6.9 %collective-permute-start.1 = (bf16[512,128]{1,0:T(8,128)(2,1)S(1)}, bf16[512,128]{1,0:T(8,128)(2,1)S(1)}, u32[]{:S(2)}, u32[]{:S(2)}) collective-permute-start(bf16[512,128]{1,0:T(8,128)(2,1)S(1)} %bitcast.59), channel_id=1, source_target_pairs={{0,8},{8,0},{16,24},{24,16},{1,9},{9,1},{17,25},{25,17},{2,10},{10... | collective-permute-start | bytes 393224 | tf_op jit(solution)/shard_map/ppermute | solution.py:29
  3.9 1.0 %copy-start.1 = (bf16[256,512]{1,0:T(8,128)(2,1)S(1)}, bf16[256,512]{1,0:T(8,128)(2,1)}, u32[]{:S(2)}) copy-start(bf16[256,512]{1,0:T(8,128)(2,1)} %param.8) | copy-start | bytes 786436
  6.0 6.0 %collective-permute-start.6 = (bf16[512,128]{1,0:T(8,128)(2,1)S(1)}, bf16[512,128]{1,0:T(8,128)(2,1)S(1)}, u32[]{:S(2)}, u32[]{:S(2)}) collective-permute-start(bf16[512,128]{1,0:T(8,128)(2,1)S(1)} %broadcast_select_fusion), channel_id=1, source_target_pairs={{0,1},{1,0},{2,3},{3,2},{4,5},{5,4},{6,7},{7,6},{8,9},{9,8},{10,11... | collective-permute-start | bytes 393224 | tf_op jit(solution)/shard_map/ppermute | solution.py:29
  6.4 14.2 %collective-permute-start.5 = (bf16[1024,128]{1,0:T(8,128)(2,1)S(1)}, bf16[1024,128]{1,0:T(8,128)(2,1)S(1)}, u32[]{:S(2)}, u32[]{:S(2)}) collective-permute-start(bf16[1024,128]{1,0:T(8,128)(2,1)S(1)} %bitcast.100), channel_id=1, source_target_pairs={{0,24},{8,16},{16,8},{24,0},{1,25},{9,17},{17,9},{25,1},{2,26},{10... | collective-permute-start | bytes 786440 | tf_op jit(solution)/shard_map/ppermute | solution.py:29
  8.4 8.1 %collective-permute-start = (bf16[1024,128]{1,0:T(8,128)(2,1)S(1)}, bf16[1024,128]{1,0:T(8,128)(2,1)S(1)}, u32[]{:S(2)}, u32[]{:S(2)}) collective-permute-start(bf16[1024,128]{1,0:T(8,128)(2,1)S(1)} %bitcast.101), channel_id=1, source_target_pairs={{0,8},{8,0},{16,24},{24,16},{1,9},{9,1},{17,25},{25,17},{2,10},{10... | collective-permute-start | bytes 786440 | tf_op jit(solution)/shard_map/ppermute | solution.py:29
  8.5 12.4 %collective-permute-start.4 = (bf16[1024,128]{1,0:T(8,128)(2,1)S(1)}, bf16[1024,128]{1,0:T(8,128)(2,1)S(1)}, u32[]{:S(2)}, u32[]{:S(2)}) collective-permute-start(bf16[1024,128]{1,0:T(8,128)(2,1)S(1)} %bitcast.63), channel_id=1, source_target_pairs={{0,16},{8,24},{16,0},{24,8},{1,17},{9,25},{17,1},{25,9},{2,18},{10... | collective-permute-start | bytes 786440 | tf_op jit(solution)/shard_map/ppermute | solution.py:29
  9.8 4.3 %collective-permute-start.8 = (bf16[512,128]{1,0:T(8,128)(2,1)S(1)}, bf16[512,128]{1,0:T(8,128)(2,1)S(1)}, u32[]{:S(2)}, u32[]{:S(2)}) collective-permute-start(bf16[512,128]{1,0:T(8,128)(2,1)S(1)} %collective-permute-done.2), channel_id=1, source_target_pairs={{7,0},{0,1},{1,2},{2,3},{3,4},{4,5},{5,6},{6,7},{15,8},{8,9},{9,10... | collective-permute-start | bytes 393224 | tf_op jit(solution)/shard_map/ppermute | solution.py:25
  12.1 3.7 %collective-permute-start.3 = (bf16[512,128]{1,0:T(8,128)(2,1)S(1)}, bf16[512,128]{1,0:T(8,128)(2,1)S(1)}, u32[]{:S(2)}, u32[]{:S(2)}) collective-permute-start(bf16[512,128]{1,0:T(8,128)(2,1)S(1)} %collective-permute-done.2), channel_id=1, source_target_pairs={{0,8},{8,0},{16,24},{24,16},{1,9},{9,1},{17,25},{25,17},{2,10},{10... | collective-permute-start | bytes 393224 | tf_op jit(solution)/shard_map/ppermute | solution.py:29
  14.1 6.8 %collective-permute-start.7 = (bf16[512,128]{1,0:T(8,128)(2,1)S(1)}, bf16[512,128]{1,0:T(8,128)(2,1)S(1)}, u32[]{:S(2)}, u32[]{:S(2)}) collective-permute-start(bf16[512,128]{1,0:T(8,128)(2,1)S(1)} %collective-permute-done.6), channel_id=1, source_target_pairs={{0,8},{8,0},{16,24},{24,16},{1,9},{9,1},{17,25},{25,17},{2,10},{10... | collective-permute-start | bytes 393224 | tf_op jit(solution)/shard_map/ppermute | solution.py:29
  15.8 5.1 %collective-permute-start.9 = (bf16[512,128]{1,0:T(8,128)(2,1)S(1)}, bf16[512,128]{1,0:T(8,128)(2,1)S(1)}, u32[]{:S(2)}, u32[]{:S(2)}) collective-permute-start(bf16[512,128]{1,0:T(8,128)(2,1)S(1)} %collective-permute-done.8), channel_id=1, source_target_pairs={{0,8},{8,0},{16,24},{24,16},{1,9},{9,1},{17,25},{25,17},{2,10},{10... | collective-permute-start | bytes 393224 | tf_op jit(solution)/shard_map/ppermute | solution.py:29
  15.8 0.7 %copy-start.2 = (s32[64]{0:T(128)S(1)}, s32[64]{0:T(128)}, u32[]{:S(2)}) copy-start(s32[64]{0:T(128)} %param.9) | copy-start | bytes 772
  25.7 2.7 %collective-permute-start.10 = (f32[3,8,256]{2,1,0:T(8,128)S(1)}, f32[3,8,256]{2,1,0:T(8,128)S(1)}, u32[]{:S(2)}, u32[]{:S(2)}) collective-permute-start(f32[3,8,256]{2,1,0:T(8,128)S(1)} %stats.3.rest_0_), channel_id=1, source_target_pairs={{0,16},{8,24},{16,0},{24,8},{1,17},{9,25},{17,1},{25,9},{2,18},{10... | collective-permute-start | bytes 73736 | tf_op jit(solution)/shard_map/ppermute | solution.py:29
  33.6 9.8 %collective-permute-start.15 = (bf16[1024,128]{1,0:T(8,128)(2,1)S(1)}, bf16[1024,128]{1,0:T(8,128)(2,1)S(1)}, u32[]{:S(2)}, u32[]{:S(2)}) collective-permute-start(bf16[1024,128]{1,0:T(8,128)(2,1)S(1)} %get-tuple-element.31), channel_id=1, source_target_pairs={{0,8},{8,0},{16,24},{24,16},{1,9},{9,1},{17,25},{25,17},{2,10},{10... | collective-permute-start | bytes 786440 | tf_op jit(solution)/shard_map/ppermute | solution.py:29
  41.2 8.9 %collective-permute-start.12 = (bf16[1536,128]{1,0:T(8,128)(2,1)S(1)}, bf16[1536,128]{1,0:T(8,128)(2,1)S(1)}, u32[]{:S(2)}, u32[]{:S(2)}) collective-permute-start(bf16[1536,128]{1,0:T(8,128)(2,1)S(1)} %get-tuple-element.26), channel_id=1, source_target_pairs={{0,8},{8,0},{16,24},{24,16},{1,9},{9,1},{17,25},{25,17},{2,10},{10... | collective-permute-start | bytes 1179656 | tf_op jit(solution)/shard_map/ppermute | solution.py:29
  41.3 8.9 %collective-permute-start.11 = (bf16[512,128]{1,0:T(8,128)(2,1)S(1)}, bf16[512,128]{1,0:T(8,128)(2,1)S(1)}, u32[]{:S(2)}, u32[]{:S(2)}) collective-permute-start(bf16[512,128]{1,0:T(8,128)(2,1)S(1)} %get-tuple-element.25), channel_id=1, source_target_pairs={{0,16},{8,24},{16,0},{24,8},{1,17},{9,25},{17,1},{25,9},{2,18},{10... | collective-permute-start | bytes 393224 | tf_op jit(solution)/shard_map/ppermute | solution.py:29
  41.4 8.9 %collective-permute-start.13 = (bf16[512,128]{1,0:T(8,128)(2,1)S(1)}, bf16[512,128]{1,0:T(8,128)(2,1)S(1)}, u32[]{:S(2)}, u32[]{:S(2)}) collective-permute-start(bf16[512,128]{1,0:T(8,128)(2,1)S(1)} %get-tuple-element.27), channel_id=1, source_target_pairs={{0,24},{8,16},{16,8},{24,0},{1,25},{9,17},{17,9},{25,1},{2,26},{10... | collective-permute-start | bytes 393224 | tf_op jit(solution)/shard_map/ppermute | solution.py:29
  43.5 9.5 %collective-permute-start.16 = (bf16[512,128]{1,0:T(8,128)(2,1)S(1)}, bf16[512,128]{1,0:T(8,128)(2,1)S(1)}, u32[]{:S(2)}, u32[]{:S(2)}) collective-permute-start(bf16[512,128]{1,0:T(8,128)(2,1)S(1)} %get-tuple-element.36), channel_id=1, source_target_pairs={{3,0},{4,1},{5,2},{6,3},{7,4},{0,5},{1,6},{2,7},{11,8},{12,9},{13,... | collective-permute-start | bytes 393224 | tf_op jit(solution)/shard_map/ppermute | solution.py:25
  47.1 7.0 %collective-permute-start.17 = (bf16[512,128]{1,0:T(8,128)(2,1)S(1)}, bf16[512,128]{1,0:T(8,128)(2,1)S(1)}, u32[]{:S(2)}, u32[]{:S(2)}) collective-permute-start(bf16[512,128]{1,0:T(8,128)(2,1)S(1)} %get-tuple-element.37), channel_id=1, source_target_pairs={{2,0},{3,1},{4,2},{5,3},{6,4},{7,5},{0,6},{1,7},{10,8},{11,9},{12,... | collective-permute-start | bytes 393224 | tf_op jit(solution)/shard_map/ppermute | solution.py:25
  50.1 10.5 %collective-permute-start.14 = (bf16[512,128]{1,0:T(8,128)(2,1)S(1)}, bf16[512,128]{1,0:T(8,128)(2,1)S(1)}, u32[]{:S(2)}, u32[]{:S(2)}) collective-permute-start(bf16[512,128]{1,0:T(8,128)(2,1)S(1)} %add_convert_fusion.3), channel_id=1, source_target_pairs={{1,0},{2,1},{3,2},{4,3},{5,4},{6,5},{7,6},{0,7},{9,8},{10,9},{11,1... | collective-permute-start | bytes 393224 | tf_op jit(solution)/shard_map/ppermute | solution.py:25

commit v5 on v4

--- a/solution.py
+++ b/solution.py
@@ -165,7 +165,7 @@
         t, dp = score_tiles(entry(n), factor, qg, kv, bias)
         t_ref[...] = t
         top[...] = jnp.max(t.reshape(-1, 8, width), axis=0)
-        d_ref[...] = dp
+        d_ref[...] = dp.astype(jnp.bfloat16)
 
     def use(n, slot):
         query = entry(n)[0]
@@ -176,7 +176,7 @@
         p = jnp.exp2(t_ref[...].reshape(-1, 8, width) - m_new)
         state[0, query] = m_new
         state[1, query] = l * corr + jnp.sum(p, axis=0)
-        state[2, query] = r * corr + jnp.sum(p * d_ref[...].reshape(-1, 8, width), axis=0)
+        state[2, query] = r * corr + jnp.sum(p * d_ref[...].astype(jnp.float32).reshape(-1, 8, width), axis=0)
 
     pair_loop(trips, load, use)
     for i in range(count):
@@ -335,7 +335,7 @@
                 pltpu.VMEM((2 * count, width, size), low),
                 pltpu.VMEM((4 * len(used), block_len, size), low),
                 bias_table,
-                *[tile, tile, pltpu.VMEM((8, width), full)] * 4,
+                *[tile, pltpu.VMEM((2 * block_len, width), low), pltpu.VMEM((8, width), full)] * 4,
                 pltpu.VMEM((3, count, 8, width), full),
                 pltpu.SMEM((count * key_blocks + 16,), jnp.int32),
             ],

time: 62.4 us -> 62.8 us (level)
  no operation moved by 1% of the time
where the time goes in v5:
time: 62.8 us; the launch traced here: 62.6 us
  starting transfers between devices  21.9 us (35%)
  Pallas kernels  20.5 us (33%)
  waiting for transfers between devices  14.5 us (23%)
  local copies, waits for them, and re-layouts  2.92 us (5%)
  other arithmetic  1.98 us (3%)
  between operations  0.85 us (1%)
    ppermute x5, waiting for transfers between devices, from_behind(): return lax.ppermute(block, axis, route)  12 us
    ppermute x13, starting transfers between devices, swap(): lax.ppermute(block, axis, [(i, i ^ bit) for i in range(lax.axis_size(axis...  11.5 us
    pallas_call x2, Pallas kernels, grads_call(): pl.pallas_call(functools.partial(grads_kernel, sizes, scale, steps, last)...  11.3 us
    ppermute x5, starting transfers between devices, from_behind(): return lax.ppermute(block, axis, route)  10.3 us
    pallas_call x2, Pallas kernels, stats_call(): pl.pallas_call(functools.partial(stats_kernel, sizes, scale * LOG2E, step...  9.22 us
    ppermute x13, waiting for transfers between devices, swap(): lax.ppermute(block, axis, [(i, i ^ bit) for i in range(lax.axis_size(axis...  2.49 us
    unnamed x6, local copies, waits for them, and re-layouts  1.54 us
  transfers between devices with their start and end apart: 18, of which 7 were waited for; matrix products, arithmetic and copies ran while one was open for 1% of the time, Pallas kernels for 16%

profile of v5, /device:TPU:15, one launch (start us, length us, event | category | flops | bytes accessed | tf_op | source)
XLA Modules:
  0.0 62.6 jit_solution(5532232804499649200)
XLA Ops:
  0.6 0.9 %pad_maximum_fusion.3 = bf16[2,2,128,128]{3,2,1,0:T(8,128)(2,1)S(1)} fusion(bf16[2,1,128,128]{3,2,1,0:T(8,128)(2,1)} %bitcast.102, bf16[2,1,128,128]{3,2,1,0:T(8,128)(2,1)} %bitcast.103), kind=kLoop, calls=%fused_computation.11 | loop fusion | flops 65536 | bytes 262144 | tf_op jit(solution)/shard_map/stack | solution.py:292
  1.6 1.3 %collective-permute-start.2 = (bf16[512,128]{1,0:T(8,128)(2,1)S(1)}, bf16[512,128]{1,0:T(8,128)(2,1)S(1)}, u32[]{:S(2)}, u32[]{:S(2)}) collective-permute-start(bf16[512,128]{1,0:T(8,128)(2,1)S(1)} %bitcast.58), channel_id=1, source_target_pairs={{6,0},{7,1},{0,2},{1,3},{2,4},{3,5},{4,6},{5,7},{14,8},{15,9},{8,1... | collective-permute-start | bytes 393224 | tf_op jit(solution)/shard_map/ppermute | solution.py:25
  2.9 1.0 %collective-permute-start.1 = (bf16[512,128]{1,0:T(8,128)(2,1)S(1)}, bf16[512,128]{1,0:T(8,128)(2,1)S(1)}, u32[]{:S(2)}, u32[]{:S(2)}) collective-permute-start(bf16[512,128]{1,0:T(8,128)(2,1)S(1)} %bitcast.59), channel_id=1, source_target_pairs={{0,8},{8,0},{16,24},{24,16},{1,9},{9,1},{17,25},{25,17},{2,10},{10... | collective-permute-start | bytes 393224 | tf_op jit(solution)/shard_map/ppermute | solution.py:29
  3.9 0.1 reshape.68
  4.0 0.9 %copy-done.1 = bf16[256,512]{1,0:T(8,128)(2,1)S(1)} copy-done((bf16[256,512]{1,0:T(8,128)(2,1)S(1)}, bf16[256,512]{1,0:T(8,128)(2,1)}, u32[]{:S(2)}) %copy-start.1) | copy-done | bytes 262168
  4.8 0.1 reshape.69
  4.9 0.4 constant_dynamic-slice_fusion
  5.3 0.7 %collective-permute-done.2 = bf16[512,128]{1,0:T(8,128)(2,1)S(1)} collective-permute-done((bf16[512,128]{1,0:T(8,128)(2,1)S(1)}, bf16[512,128]{1,0:T(8,128)(2,1)S(1)}, u32[]{:S(2)}, u32[]{:S(2)}) %collective-permute-start.2) | collective-permute-done | bytes 131104 | tf_op jit(solution)/shard_map/ppermute | solution.py:25
  6.0 0.3 collective-permute-start.6
  6.4 2.0 %collective-permute-start.5 = (bf16[1024,128]{1,0:T(8,128)(2,1)S(1)}, bf16[1024,128]{1,0:T(8,128)(2,1)S(1)}, u32[]{:S(2)}, u32[]{:S(2)}) collective-permute-start(bf16[1024,128]{1,0:T(8,128)(2,1)S(1)} %bitcast.100), channel_id=1, source_target_pairs={{0,24},{8,16},{16,8},{24,0},{1,25},{9,17},{17,9},{25,1},{2,26},{10... | collective-permute-start | bytes 786440 | tf_op jit(solution)/shard_map/ppermute | solution.py:29
  8.4 0.0 collective-permute-start
  8.5 1.3 %collective-permute-start.4 = (bf16[1024,128]{1,0:T(8,128)(2,1)S(1)}, bf16[1024,128]{1,0:T(8,128)(2,1)S(1)}, u32[]{:S(2)}, u32[]{:S(2)}) collective-permute-start(bf16[1024,128]{1,0:T(8,128)(2,1)S(1)} %bitcast.63), channel_id=1, source_target_pairs={{0,16},{8,24},{16,0},{24,8},{1,17},{9,25},{17,1},{25,9},{2,18},{10... | collective-permute-start | bytes 786440 | tf_op jit(solution)/shard_map/ppermute | solution.py:29
  9.8 0.0 collective-permute-done.1
  9.8 2.3 %collective-permute-start.8 = (bf16[512,128]{1,0:T(8,128)(2,1)S(1)}, bf16[512,128]{1,0:T(8,128)(2,1)S(1)}, u32[]{:S(2)}, u32[]{:S(2)}) collective-permute-start(bf16[512,128]{1,0:T(8,128)(2,1)S(1)} %collective-permute-done.2), channel_id=1, source_target_pairs={{7,0},{0,1},{1,2},{2,3},{3,4},{4,5},{5,6},{6,7},{15,8},{8,9},{9,10... | collective-permute-start | bytes 393224 | tf_op jit(solution)/shard_map/ppermute | solution.py:25
  12.1 0.0 collective-permute-done.6
  12.1 1.1 %collective-permute-start.3 = (bf16[512,128]{1,0:T(8,128)(2,1)S(1)}, bf16[512,128]{1,0:T(8,128)(2,1)S(1)}, u32[]{:S(2)}, u32[]{:S(2)}) collective-permute-start(bf16[512,128]{1,0:T(8,128)(2,1)S(1)} %collective-permute-done.2), channel_id=1, source_target_pairs={{0,8},{8,0},{16,24},{24,16},{1,9},{9,1},{17,25},{25,17},{2,10},{10... | collective-permute-start | bytes 393224 | tf_op jit(solution)/shard_map/ppermute | solution.py:29
  13.1 0.9 %collective-permute-done.8 = bf16[512,128]{1,0:T(8,128)(2,1)S(1)} collective-permute-done((bf16[512,128]{1,0:T(8,128)(2,1)S(1)}, bf16[512,128]{1,0:T(8,128)(2,1)S(1)}, u32[]{:S(2)}, u32[]{:S(2)}) %collective-permute-start.8) | collective-permute-done | bytes 131104 | tf_op jit(solution)/shard_map/ppermute | solution.py:25
  14.1 1.7 %collective-permute-start.7 = (bf16[512,128]{1,0:T(8,128)(2,1)S(1)}, bf16[512,128]{1,0:T(8,128)(2,1)S(1)}, u32[]{:S(2)}, u32[]{:S(2)}) collective-permute-start(bf16[512,128]{1,0:T(8,128)(2,1)S(1)} %collective-permute-done.6), channel_id=1, source_target_pairs={{0,8},{8,0},{16,24},{24,16},{1,9},{9,1},{17,25},{25,17},{2,10},{10... | collective-permute-start | bytes 393224 | tf_op jit(solution)/shard_map/ppermute | solution.py:29
  15.8 0.0 collective-permute-done.3
  15.8 0.0 collective-permute-start.9
  15.8 0.7 %copy-done.2 = s32[64]{0:T(128)S(1)} copy-done((s32[64]{0:T(128)S(1)}, s32[64]{0:T(128)}, u32[]{:S(2)}) %copy-start.2) | copy-done | bytes 280
  16.4 0.1 concatenate.7.where_ref
  16.5 0.0 collective-permute-done
  16.5 4.2 %stats.2 = (f32[3,8,256]{2,1,0:T(8,128)S(1)}, s32[112]{0:T(128)S(1)}, s32[80]{0:T(128)S(1)}, s32[80]{0:T(128)S(1)}) custom-call(s32[72]{0:T(128)S(1)} %concatenate.7.where_ref, bf16[4,256,128]{2,1,0:T(8,128)(2,1)S(1)} %bitcast.64, bf16[4,256,128]{2,1,0:T(8,128)(2,1)S(1)} %bitcast.74, bf16[4,128,128]{2,1,0:T(8,128)(2,1)S(1)} %bitcast.60, ...), custom_call_target="tpu_custom_call" | custom-call | flops 536870912 | bytes 1048576 | tf_op jit(solution)/shard_map/stats/pallas_call | solution.py:327
  20.7 0.0 collective-permute-done.5
  20.7 0.2 collective-permute-done.4
  20.9 0.0 collective-permute-done.9
  20.9 5.0 %stats.3.rest_0_ = f32[3,8,256]{2,1,0:T(8,128)S(1)} custom-call(s32[112]{0:T(128)S(1)} %get-tuple-element.20.where_ref, f32[3,8,256]{2,1,0:T(8,128)S(1)} %get-tuple-element.21.rest_0_, bf16[4,256,128]{2,1,0:T(8,128)(2,1)S(1)} %bitcast.65, bf16[4,256,128]{2,1,0:T(8,128)(2,1)S(1)} %bitcast.75, bf16[4,256,128]{2,1,0:T(8,128)(2,1)S(1)} %bitcast.78, ...), custom_call_target="tpu_custom_call" | custom-call | flops 1610612736 | bytes 1048576 | tf_op jit(solution)/shard_map/stats/pallas_call | solution.py:327
  25.9 0.5 collective-permute-start.10
  26.4 2.3 %collective-permute-done.10.rest_1_ = f32[3,8,256]{2,1,0:T(8,128)S(1)} collective-permute-done((f32[3,8,256]{2,1,0:T(8,128)S(1)}, f32[3,8,256]{2,1,0:T(8,128)S(1)}, u32[]{:S(2)}, u32[]{:S(2)}) %collective-permute-start.10) | collective-permute-done | bytes 24608 | tf_op jit(solution)/shard_map/ppermute | solution.py:29
  28.7 5.2 %grads.2 = (f32[512,128]{1,0:T(8,128)S(1)}, f32[512,128]{1,0:T(8,128)S(1)}, bf16[1024,128]{1,0:T(8,128)(2,1)S(1)}, f32[8,128,256]{2,1,0:T(8,128)S(1)}, f32[8,8,256]{2,1,0:T(8,128)S(1)}) custom-call(s32[80]{0:T(128)S(1)} %get-tuple-element.19.lists, f32[3,8,256]{2,1,0:T(8,128)S(1)} %stats.3.rest_0_, f32[3,8,256]{2,1,0:T(8,128)S(1)} %collective-permute-done.10.rest_1_, ...), custom_call_target="tpu_custom_call" | custom-call | flops 3221225472 | bytes 2097152 | tf_op jit(solution)/shard_map/grads/pallas_call | solution.py:368
  33.9 1.6 %collective-permute-start.15 = (bf16[1024,128]{1,0:T(8,128)(2,1)S(1)}, bf16[1024,128]{1,0:T(8,128)(2,1)S(1)}, u32[]{:S(2)}, u32[]{:S(2)}) collective-permute-start(bf16[1024,128]{1,0:T(8,128)(2,1)S(1)} %get-tuple-element.31), channel_id=1, source_target_pairs={{0,8},{8,0},{16,24},{24,16},{1,9},{9,1},{17,25},{25,17},{2,10},{10... | collective-permute-start | bytes 786440 | tf_op jit(solution)/shard_map/ppermute | solution.py:29
  35.4 6.1 %grads.3 = (f32[512,128]{1,0:T(8,128)S(1)}, f32[512,128]{1,0:T(8,128)S(1)}, bf16[1536,128]{1,0:T(8,128)(2,1)S(1)}, f32[512,128]{1,0:T(8,128)S(1)}, bf16[512,128]...) custom-call(s32[80]{0:T(128)S(1)} %get-tuple-element.18.lists, f32[8,128,256]{2,1,0:T(8,128)S(1)} %get-tuple-element.22.rest_0_, ...), custom_call_target="tpu_custom_call" | custom-call | flops 3221225472 | bytes 2097152 | tf_op jit(solution)/shard_map/grads/pallas_call | solution.py:368
  41.5 0.1 collective-permute-start.12
  41.6 0.1 collective-permute-start.11
  41.7 2.0 %collective-permute-start.13 = (bf16[512,128]{1,0:T(8,128)(2,1)S(1)}, bf16[512,128]{1,0:T(8,128)(2,1)S(1)}, u32[]{:S(2)}, u32[]{:S(2)}) collective-permute-start(bf16[512,128]{1,0:T(8,128)(2,1)S(1)} %get-tuple-element.27), channel_id=1, source_target_pairs={{0,24},{8,16},{16,8},{24,0},{1,25},{9,17},{17,9},{25,1},{2,26},{10... | collective-permute-start | bytes 393224 | tf_op jit(solution)/shard_map/ppermute | solution.py:29
  43.7 0.0 collective-permute-done.15
  43.7 0.1 add_convert_fusion.2
  43.8 3.6 %collective-permute-start.16 = (bf16[512,128]{1,0:T(8,128)(2,1)S(1)}, bf16[512,128]{1,0:T(8,128)(2,1)S(1)}, u32[]{:S(2)}, u32[]{:S(2)}) collective-permute-start(bf16[512,128]{1,0:T(8,128)(2,1)S(1)} %get-tuple-element.36), channel_id=1, source_target_pairs={{3,0},{4,1},{5,2},{6,3},{7,4},{0,5},{1,6},{2,7},{11,8},{12,9},{13,... | collective-permute-start | bytes 393224 | tf_op jit(solution)/shard_map/ppermute | solution.py:25
  47.4 3.1 %collective-permute-start.17 = (bf16[512,128]{1,0:T(8,128)(2,1)S(1)}, bf16[512,128]{1,0:T(8,128)(2,1)S(1)}, u32[]{:S(2)}, u32[]{:S(2)}) collective-permute-start(bf16[512,128]{1,0:T(8,128)(2,1)S(1)} %get-tuple-element.37), channel_id=1, source_target_pairs={{2,0},{3,1},{4,2},{5,3},{6,4},{7,5},{0,6},{1,7},{10,8},{11,9},{12,... | collective-permute-start | bytes 393224 | tf_op jit(solution)/shard_map/ppermute | solution.py:25
  50.5 0.1 collective-permute-start.14
  50.6 0.0 collective-permute-done.11
  50.6 2.7 %collective-permute-done.16 = bf16[512,128]{1,0:T(8,128)(2,1)S(1)} collective-permute-done((bf16[512,128]{1,0:T(8,128)(2,1)S(1)}, bf16[512,128]{1,0:T(8,128)(2,1)S(1)}, u32[]{:S(2)}, u32[]{:S(2)}) %collective-permute-start.16) | collective-permute-done | bytes 131104 | tf_op jit(solution)/shard_map/ppermute | solution.py:25
  53.3 1.1 %collective-permute-done.17 = bf16[512,128]{1,0:T(8,128)(2,1)S(1)} collective-permute-done((bf16[512,128]{1,0:T(8,128)(2,1)S(1)}, bf16[512,128]{1,0:T(8,128)(2,1)S(1)}, u32[]{:S(2)}, u32[]{:S(2)}) %collective-permute-start.17) | collective-permute-done | bytes 131104 | tf_op jit(solution)/shard_map/ppermute | solution.py:25
  54.4 6.6 %collective-permute-done.14 = bf16[512,128]{1,0:T(8,128)(2,1)S(1)} collective-permute-done((bf16[512,128]{1,0:T(8,128)(2,1)S(1)}, bf16[512,128]{1,0:T(8,128)(2,1)S(1)}, u32[]{:S(2)}, u32[]{:S(2)}) %collective-permute-start.14) | collective-permute-done | bytes 131104 | tf_op jit(solution)/shard_map/ppermute | solution.py:25
  61.0 0.2 select_convert_fusion.1
  61.2 0.7 %fusion = (bf16[2,1,128,128]{3,2,1,0:T(8,128)(2,1)}, bf16[2,1,128,128]{3,2,1,0:T(8,128)(2,1)}) fusion(bf16[2,2,128,128]{3,2,1,0:T(8,128)(2,1)S(1)} %bitcast.99), kind=kLoop, calls=%fused_computation.21 | loop fusion | bytes 262144 | tf_op jit(solution)/shard_map/slice | solution.py:420
  61.9 0.7 %pad_maximum_fusion.2 = bf16[256,512]{1,0:T(8,128)(2,1)} fusion(bf16[256,128]{1,0:T(8,128)(2,1)S(1)} %get-tuple-element.47, bf16[256,128]{1,0:T(8,128)(2,1)S(1)} %get-tuple-element.46, bf16[256,128]{1,0:T(8,128)(2,1)S(1)} %get-tuple-element.45, bf16[256,128]{1,0:T(8,128)(2,1)S(1)} %get-tuple-element.44), kind=kLoop, calls=%fused_computation.2 | loop fusion | flops 1048576 | bytes 524288 | tf_op jit(solution)/shard_map/concatenate | solution.py:407
  (19 shorter events, 0.3 us)
Async XLA Ops:
  0.6 3.3 %copy-start = (bf16[256,512]{1,0:T(8,128)(2,1)S(1)}, bf16[256,512]{1,0:T(8,128)(2,1)}, u32[]{:S(2)}) copy-start(bf16[256,512]{1,0:T(8,128)(2,1)} %param.5) | copy-start | bytes 786436
  1.6 4.4 %collective-permute-start.2 = (bf16[512,128]{1,0:T(8,128)(2,1)S(1)}, bf16[512,128]{1,0:T(8,128)(2,1)S(1)}, u32[]{:S(2)}, u32[]{:S(2)}) collective-permute-start(bf16[512,128]{1,0:T(8,128)(2,1)S(1)} %bitcast.58), channel_id=1, source_target_pairs={{6,0},{7,1},{0,2},{1,3},{2,4},{3,5},{4,6},{5,7},{14,8},{15,9},{8,1... | collective-permute-start | bytes 393224 | tf_op jit(solution)/shard_map/ppermute | solution.py:25
  2.9 6.9 %collective-permute-start.1 = (bf16[512,128]{1,0:T(8,128)(2,1)S(1)}, bf16[512,128]{1,0:T(8,128)(2,1)S(1)}, u32[]{:S(2)}, u32[]{:S(2)}) collective-permute-start(bf16[512,128]{1,0:T(8,128)(2,1)S(1)} %bitcast.59), channel_id=1, source_target_pairs={{0,8},{8,0},{16,24},{24,16},{1,9},{9,1},{17,25},{25,17},{2,10},{10... | collective-permute-start | bytes 393224 | tf_op jit(solution)/shard_map/ppermute | solution.py:29
  3.9 1.0 %copy-start.1 = (bf16[256,512]{1,0:T(8,128)(2,1)S(1)}, bf16[256,512]{1,0:T(8,128)(2,1)}, u32[]{:S(2)}) copy-start(bf16[256,512]{1,0:T(8,128)(2,1)} %param.8) | copy-start | bytes 786436
  6.0 6.0 %collective-permute-start.6 = (bf16[512,128]{1,0:T(8,128)(2,1)S(1)}, bf16[512,128]{1,0:T(8,128)(2,1)S(1)}, u32[]{:S(2)}, u32[]{:S(2)}) collective-permute-start(bf16[512,128]{1,0:T(8,128)(2,1)S(1)} %broadcast_select_fusion), channel_id=1, source_target_pairs={{0,1},{1,0},{2,3},{3,2},{4,5},{5,4},{6,7},{7,6},{8,9},{9,8},{10,11... | collective-permute-start | bytes 393224 | tf_op jit(solution)/shard_map/ppermute | solution.py:29
  6.4 14.3 %collective-permute-start.5 = (bf16[1024,128]{1,0:T(8,128)(2,1)S(1)}, bf16[1024,128]{1,0:T(8,128)(2,1)S(1)}, u32[]{:S(2)}, u32[]{:S(2)}) collective-permute-start(bf16[1024,128]{1,0:T(8,128)(2,1)S(1)} %bitcast.100), channel_id=1, source_target_pairs={{0,24},{8,16},{16,8},{24,0},{1,25},{9,17},{17,9},{25,1},{2,26},{10... | collective-permute-start | bytes 786440 | tf_op jit(solution)/shard_map/ppermute | solution.py:29
  8.4 8.1 %collective-permute-start = (bf16[1024,128]{1,0:T(8,128)(2,1)S(1)}, bf16[1024,128]{1,0:T(8,128)(2,1)S(1)}, u32[]{:S(2)}, u32[]{:S(2)}) collective-permute-start(bf16[1024,128]{1,0:T(8,128)(2,1)S(1)} %bitcast.101), channel_id=1, source_target_pairs={{0,8},{8,0},{16,24},{24,16},{1,9},{9,1},{17,25},{25,17},{2,10},{10... | collective-permute-start | bytes 786440 | tf_op jit(solution)/shard_map/ppermute | solution.py:29
  8.5 12.4 %collective-permute-start.4 = (bf16[1024,128]{1,0:T(8,128)(2,1)S(1)}, bf16[1024,128]{1,0:T(8,128)(2,1)S(1)}, u32[]{:S(2)}, u32[]{:S(2)}) collective-permute-start(bf16[1024,128]{1,0:T(8,128)(2,1)S(1)} %bitcast.63), channel_id=1, source_target_pairs={{0,16},{8,24},{16,0},{24,8},{1,17},{9,25},{17,1},{25,9},{2,18},{10... | collective-permute-start | bytes 786440 | tf_op jit(solution)/shard_map/ppermute | solution.py:29
  9.8 4.3 %collective-permute-start.8 = (bf16[512,128]{1,0:T(8,128)(2,1)S(1)}, bf16[512,128]{1,0:T(8,128)(2,1)S(1)}, u32[]{:S(2)}, u32[]{:S(2)}) collective-permute-start(bf16[512,128]{1,0:T(8,128)(2,1)S(1)} %collective-permute-done.2), channel_id=1, source_target_pairs={{7,0},{0,1},{1,2},{2,3},{3,4},{4,5},{5,6},{6,7},{15,8},{8,9},{9,10... | collective-permute-start | bytes 393224 | tf_op jit(solution)/shard_map/ppermute | solution.py:25
  12.1 3.7 %collective-permute-start.3 = (bf16[512,128]{1,0:T(8,128)(2,1)S(1)}, bf16[512,128]{1,0:T(8,128)(2,1)S(1)}, u32[]{:S(2)}, u32[]{:S(2)}) collective-permute-start(bf16[512,128]{1,0:T(8,128)(2,1)S(1)} %collective-permute-done.2), channel_id=1, source_target_pairs={{0,8},{8,0},{16,24},{24,16},{1,9},{9,1},{17,25},{25,17},{2,10},{10... | collective-permute-start | bytes 393224 | tf_op jit(solution)/shard_map/ppermute | solution.py:29
  14.1 6.8 %collective-permute-start.7 = (bf16[512,128]{1,0:T(8,128)(2,1)S(1)}, bf16[512,128]{1,0:T(8,128)(2,1)S(1)}, u32[]{:S(2)}, u32[]{:S(2)}) collective-permute-start(bf16[512,128]{1,0:T(8,128)(2,1)S(1)} %collective-permute-done.6), channel_id=1, source_target_pairs={{0,8},{8,0},{16,24},{24,16},{1,9},{9,1},{17,25},{25,17},{2,10},{10... | collective-permute-start | bytes 393224 | tf_op jit(solution)/shard_map/ppermute | solution.py:29
  15.8 5.1 %collective-permute-start.9 = (bf16[512,128]{1,0:T(8,128)(2,1)S(1)}, bf16[512,128]{1,0:T(8,128)(2,1)S(1)}, u32[]{:S(2)}, u32[]{:S(2)}) collective-permute-start(bf16[512,128]{1,0:T(8,128)(2,1)S(1)} %collective-permute-done.8), channel_id=1, source_target_pairs={{0,8},{8,0},{16,24},{24,16},{1,9},{9,1},{17,25},{25,17},{2,10},{10... | collective-permute-start | bytes 393224 | tf_op jit(solution)/shard_map/ppermute | solution.py:29
  15.8 0.7 %copy-start.2 = (s32[64]{0:T(128)S(1)}, s32[64]{0:T(128)}, u32[]{:S(2)}) copy-start(s32[64]{0:T(128)} %param.9) | copy-start | bytes 772
  25.9 2.7 %collective-permute-start.10 = (f32[3,8,256]{2,1,0:T(8,128)S(1)}, f32[3,8,256]{2,1,0:T(8,128)S(1)}, u32[]{:S(2)}, u32[]{:S(2)}) collective-permute-start(f32[3,8,256]{2,1,0:T(8,128)S(1)} %stats.3.rest_0_), channel_id=1, source_target_pairs={{0,16},{8,24},{16,0},{24,8},{1,17},{9,25},{17,1},{25,9},{2,18},{10... | collective-permute-start | bytes 73736 | tf_op jit(solution)/shard_map/ppermute | solution.py:29
  33.9 9.9 %collective-permute-start.15 = (bf16[1024,128]{1,0:T(8,128)(2,1)S(1)}, bf16[1024,128]{1,0:T(8,128)(2,1)S(1)}, u32[]{:S(2)}, u32[]{:S(2)}) collective-permute-start(bf16[1024,128]{1,0:T(8,128)(2,1)S(1)} %get-tuple-element.31), channel_id=1, source_target_pairs={{0,8},{8,0},{16,24},{24,16},{1,9},{9,1},{17,25},{25,17},{2,10},{10... | collective-permute-start | bytes 786440 | tf_op jit(solution)/shard_map/ppermute | solution.py:29
  41.5 8.9 %collective-permute-start.12 = (bf16[1536,128]{1,0:T(8,128)(2,1)S(1)}, bf16[1536,128]{1,0:T(8,128)(2,1)S(1)}, u32[]{:S(2)}, u32[]{:S(2)}) collective-permute-start(bf16[1536,128]{1,0:T(8,128)(2,1)S(1)} %get-tuple-element.26), channel_id=1, source_target_pairs={{0,8},{8,0},{16,24},{24,16},{1,9},{9,1},{17,25},{25,17},{2,10},{10... | collective-permute-start | bytes 1179656 | tf_op jit(solution)/shard_map/ppermute | solution.py:29
  41.6 8.9 %collective-permute-start.11 = (bf16[512,128]{1,0:T(8,128)(2,1)S(1)}, bf16[512,128]{1,0:T(8,128)(2,1)S(1)}, u32[]{:S(2)}, u32[]{:S(2)}) collective-permute-start(bf16[512,128]{1,0:T(8,128)(2,1)S(1)} %get-tuple-element.25), channel_id=1, source_target_pairs={{0,16},{8,24},{16,0},{24,8},{1,17},{9,25},{17,1},{25,9},{2,18},{10... | collective-permute-start | bytes 393224 | tf_op jit(solution)/shard_map/ppermute | solution.py:29
  41.7 8.9 %collective-permute-start.13 = (bf16[512,128]{1,0:T(8,128)(2,1)S(1)}, bf16[512,128]{1,0:T(8,128)(2,1)S(1)}, u32[]{:S(2)}, u32[]{:S(2)}) collective-permute-start(bf16[512,128]{1,0:T(8,128)(2,1)S(1)} %get-tuple-element.27), channel_id=1, source_target_pairs={{0,24},{8,16},{16,8},{24,0},{1,25},{9,17},{17,9},{25,1},{2,26},{10... | collective-permute-start | bytes 393224 | tf_op jit(solution)/shard_map/ppermute | solution.py:29
  43.8 9.5 %collective-permute-start.16 = (bf16[512,128]{1,0:T(8,128)(2,1)S(1)}, bf16[512,128]{1,0:T(8,128)(2,1)S(1)}, u32[]{:S(2)}, u32[]{:S(2)}) collective-permute-start(bf16[512,128]{1,0:T(8,128)(2,1)S(1)} %get-tuple-element.36), channel_id=1, source_target_pairs={{3,0},{4,1},{5,2},{6,3},{7,4},{0,5},{1,6},{2,7},{11,8},{12,9},{13,... | collective-permute-start | bytes 393224 | tf_op jit(solution)/shard_map/ppermute | solution.py:25
  47.4 7.0 %collective-permute-start.17 = (bf16[512,128]{1,0:T(8,128)(2,1)S(1)}, bf16[512,128]{1,0:T(8,128)(2,1)S(1)}, u32[]{:S(2)}, u32[]{:S(2)}) collective-permute-start(bf16[512,128]{1,0:T(8,128)(2,1)S(1)} %get-tuple-element.37), channel_id=1, source_target_pairs={{2,0},{3,1},{4,2},{5,3},{6,4},{7,5},{0,6},{1,7},{10,8},{11,9},{12,... | collective-permute-start | bytes 393224 | tf_op jit(solution)/shard_map/ppermute | solution.py:25
  50.5 10.5 %collective-permute-start.14 = (bf16[512,128]{1,0:T(8,128)(2,1)S(1)}, bf16[512,128]{1,0:T(8,128)(2,1)S(1)}, u32[]{:S(2)}, u32[]{:S(2)}) collective-permute-start(bf16[512,128]{1,0:T(8,128)(2,1)S(1)} %add_convert_fusion.3), channel_id=1, source_target_pairs={{1,0},{2,1},{3,2},{4,3},{5,4},{6,5},{7,6},{0,7},{9,8},{10,9},{11,1... | collective-permute-start | bytes 393224 | tf_op jit(solution)/shard_map/ppermute | solution.py:25
